TPU v7x, 32 devices: a whole 2x2x4 slice. The times are simulated.
32 devices in a mesh: fsdp: 4 (over y, x), context: 4 (over z), tensor: 2 (over core).
Axes of the slice: x: 2, y: 2, z: 4, core: 2. Of those that a mesh axis runs over, the one named last changes fastest.
Arguments:
- tokens: bfloat16 [4, 1024, 2048], P('fsdp', 'context'), may hold values from -6 to 6
- cotangent: bfloat16 [4, 1024, 2048], P('fsdp', 'context'), may hold values from -6 to 6
- norm_gain_attn: bfloat16 [2048], replicated, may hold values from 0.25 to 1.75
- norm_gain_mlp: bfloat16 [2048], replicated, may hold values from 0.25 to 1.75
- head_gains: bfloat16 [2, 128], replicated, may hold values from 0.25 to 1.75
- query_weight: bfloat16 [2048, 2048], P(('fsdp', 'context'), 'tensor'), may hold values from -0.125 to 0.125
- key_matrix: bfloat16 [2048, 1024], P(('fsdp', 'context'), 'tensor'), may hold values from -0.125 to 0.125
- value_matrix: bfloat16 [2048, 1024], P(('fsdp', 'context'), 'tensor'), may hold values from -0.125 to 0.125
- output_weight: bfloat16 [2048, 2048], P(('fsdp', 'context'), 'tensor'), may hold values from -1.5 to 1.5
- gate_weight: bfloat16 [2048, 6144], P(('fsdp', 'context'), 'tensor'), may hold values from -0.125 to 0.125
- up_weight: bfloat16 [2048, 6144], P(('fsdp', 'context'), 'tensor'), may hold values from -0.125 to 0.125
- down_weight: bfloat16 [2048, 6144], P(('fsdp', 'context'), 'tensor'), may hold values from -0.078125 to 0.078125
Outputs:
- out: bfloat16 [4, 1024, 2048], P('fsdp', 'context')
- tokens_grad: float32 [4, 1024, 2048], P('fsdp', 'context')
- attn_gain_grad: float32 [2048], replicated
- mlp_gain_grad: float32 [2048], replicated
- head_gains_grad: float32 [2, 128], replicated
- query_grad: float32 [2048, 2048], P(('fsdp', 'context'), 'tensor')
- key_grad: float32 [2048, 1024], P(('fsdp', 'context'), 'tensor')
- value_grad: float32 [2048, 1024], P(('fsdp', 'context'), 'tensor')
- output_grad: float32 [2048, 2048], P(('fsdp', 'context'), 'tensor')
- gate_grad: float32 [2048, 6144], P(('fsdp', 'context'), 'tensor')
- up_grad: float32 [2048, 6144], P(('fsdp', 'context'), 'tensor')
- down_grad: float32 [2048, 6144], P(('fsdp', 'context'), 'tensor')
All inputs are finite; a program needn't handle non-finite values.
Results may differ from a plain program's by a relative error of at most 0.017.
Values may be sent and summed in bfloat16 or wider, within the bound.
A program may use at most 320 MiB of HBM per device.

v0:
```python
import math

import jax
import jax.numpy as jnp
from jax import lax
from jax.sharding import PartitionSpec as P

HEAD_DIM = 128


EPS = 1e-06
THETA = 1000000.0


def rms_scale(values):
    return lax.rsqrt(jnp.mean(values * values, axis=-1, keepdims=True) + EPS)


def rope_tables(positions, head_size):
    halves = head_size // 2
    inverse = THETA ** (-(jnp.arange(halves, dtype=jnp.float32) * 2.0) / head_size)
    angle = positions[:, None].astype(jnp.float32) * inverse[None, :]
    return (jnp.cos(angle), jnp.sin(angle))


def rotate(values, cosine_table, sine_table):
    halves = values.shape[-1] // 2
    leading = values[..., :halves]
    trailing = values[..., halves:]
    return jnp.concatenate(
        [
            leading * cosine_table - trailing * sine_table,
            trailing * cosine_table + leading * sine_table,
        ],
        axis=-1,
    )


def unrotate(values, cosine_table, sine_table):
    halves = values.shape[-1] // 2
    leading = values[..., :halves]
    trailing = values[..., halves:]
    return jnp.concatenate(
        [
            leading * cosine_table + trailing * sine_table,
            trailing * cosine_table - leading * sine_table,
        ],
        axis=-1,
    )


def norm_back(grad_normed, normed_hat, scale_factor, gain):
    scaled = grad_normed * gain
    return scale_factor * (
        scaled - normed_hat * jnp.mean(normed_hat * scaled, axis=-1, keepdims=True)
    )


def row_product(left, right):
    return lax.dot_general(
        left, right, (((0,), (0,)), ((), ())), preferred_element_type=jnp.float32
    )


def column_product(left, right):
    return lax.dot_general(
        left, right, (((1,), (1,)), ((), ())), preferred_element_type=jnp.float32
    )


def blank(row_total, col_total):
    return jnp.zeros((row_total, col_total), jnp.float32)


def placing(left):

    def place_rows(total, piece, start):
        return column_product(left, piece)

    return place_rows


def adding(left):

    def add_rows(total, piece, start):
        return jnp.dot(left, piece, preferred_element_type=jnp.float32)

    return add_rows


def tensor_total(partial_sum):
    return lax.psum(partial_sum, "tensor")


def owner_rows(term_fn, row_total):
    return lax.psum_scatter(
        term_fn(jnp.int32(0), lax.axis_size(("fsdp", "context")) * row_total),
        ("fsdp", "context"),
        scatter_dimension=0,
        tiled=True,
    )


def shards(
    tokens,
    cotangent,
    norm_gain_attn,
    norm_gain_mlp,
    head_gains,
    query_weight,
    key_matrix,
    value_matrix,
    output_weight,
    gate_weight,
    up_weight,
    down_weight,
):
    seq_count, local_len, model_width = tokens.shape
    row_count = seq_count * local_len
    owned_rows = query_weight.shape[0]
    query_cols = query_weight.shape[1]
    kv_cols = key_matrix.shape[1]
    hidden_cols = gate_weight.shape[1]
    query_heads = query_cols // HEAD_DIM
    kv_heads = kv_cols // HEAD_DIM
    head_group = query_heads // kv_heads
    score_scale = 1.0 / math.sqrt(HEAD_DIM)
    full_len = local_len * lax.axis_size("context")
    query_pos = lax.axis_index("context") * local_len + jnp.arange(local_len, dtype=jnp.int32)
    key_pos = jnp.arange(full_len, dtype=jnp.int32)
    cosine_table, sine_table = rope_tables(query_pos, HEAD_DIM)
    cosine_table = cosine_table[:, None, :]
    sine_table = sine_table[:, None, :]
    visible = key_pos[None, :] <= query_pos[:, None]
    inputs = tokens.reshape(row_count, model_width).astype(jnp.float32)
    grad_out = cotangent.reshape(row_count, model_width)
    gain_attn = norm_gain_attn.astype(jnp.float32)
    gain_mlp = norm_gain_mlp.astype(jnp.float32)
    gain_heads = head_gains.astype(jnp.float32)

    def attn_rows(fold_fn, initial):
        return fold_fn(
            initial,
            (
                lax.all_gather(query_weight, ("fsdp", "context"), axis=0, tiled=True),
                lax.all_gather(key_matrix, ("fsdp", "context"), axis=0, tiled=True),
                lax.all_gather(value_matrix, ("fsdp", "context"), axis=0, tiled=True),
            ),
            jnp.int32(0),
        )

    def attn_out_rows(fold_fn, initial):
        return fold_fn(
            initial,
            lax.all_gather(output_weight, ("fsdp", "context"), axis=0, tiled=True),
            jnp.int32(0),
        )

    def mlp_rows(fold_fn, initial):
        return fold_fn(
            initial,
            (
                lax.all_gather(gate_weight, ("fsdp", "context"), axis=0, tiled=True),
                lax.all_gather(up_weight, ("fsdp", "context"), axis=0, tiled=True),
            ),
            jnp.int32(0),
        )

    def down_rows(fold_fn, initial):
        return fold_fn(
            initial,
            lax.all_gather(down_weight, ("fsdp", "context"), axis=0, tiled=True),
            jnp.int32(0),
        )

    scale_attn = rms_scale(inputs)
    hat_attn = inputs * scale_attn
    normed_attn = (hat_attn * gain_attn).astype(jnp.bfloat16)

    def project_in(totals, pieces, start):
        return (
            jnp.dot(normed_attn, pieces[0], preferred_element_type=jnp.float32),
            jnp.dot(normed_attn, pieces[1], preferred_element_type=jnp.float32),
            jnp.dot(normed_attn, pieces[2], preferred_element_type=jnp.float32),
        )

    query_raw, key_unrotated, value_raw = attn_rows(
        project_in,
        (blank(row_count, query_cols), blank(row_count, kv_cols), blank(row_count, kv_cols)),
    )
    query_split = query_raw.reshape(seq_count, local_len, query_heads, HEAD_DIM)
    query_scale = rms_scale(query_split)
    query_hat = query_split * query_scale
    query_rows = rotate(query_hat * gain_heads[0], cosine_table, sine_table).astype(jnp.bfloat16)
    key_split = key_unrotated.reshape(seq_count, local_len, kv_heads, HEAD_DIM)
    key_scale = rms_scale(key_split)
    key_hat = key_split * key_scale
    keys_local = rotate(key_hat * gain_heads[1], cosine_table, sine_table).astype(jnp.bfloat16)
    values_local = value_raw.astype(jnp.bfloat16)
    keys_all, value_rows_gathered = (
        lax.all_gather(
            keys_local.reshape(seq_count, local_len, kv_cols), "context", axis=1, tiled=True
        ),
        lax.all_gather(
            values_local.reshape(seq_count, local_len, kv_cols), "context", axis=1, tiled=True
        ),
    )
    query_blocks = query_rows.reshape(
        seq_count, local_len, kv_heads, head_group, HEAD_DIM
    ).transpose(2, 0, 1, 3, 4)
    key_blocks = keys_all.reshape(seq_count, full_len, kv_heads, HEAD_DIM).transpose(2, 0, 1, 3)
    value_blocks = value_rows_gathered.reshape(seq_count, full_len, kv_heads, HEAD_DIM).transpose(
        2, 0, 1, 3
    )

    def attend(operands):
        query_block, key_block, value_block = operands
        scores = (
            jnp.einsum("bigd,bjd->bgij", query_block, key_block, preferred_element_type=jnp.float32)
            * score_scale
        )
        weights = jnp.where(visible, jnp.exp(scores), 0.0)
        totals = jnp.sum(weights, axis=-1)
        probs_low = (weights / totals[..., None]).astype(jnp.bfloat16)
        mixed_heads = jnp.einsum(
            "bgij,bjd->bigd", probs_low, value_block, preferred_element_type=jnp.float32
        )
        return (mixed_heads.astype(jnp.bfloat16), jnp.log(totals))

    mixed_all, log_totals = lax.map(attend, (query_blocks, key_blocks, value_blocks))
    attended = mixed_all.transpose(1, 2, 0, 3, 4).reshape(row_count, query_cols)
    attn_part = attn_out_rows(placing(attended), blank(row_count, model_width))
    residual = inputs + tensor_total(attn_part)
    scale_mlp = rms_scale(residual)
    hat_mlp = residual * scale_mlp
    normed_mlp = (hat_mlp * gain_mlp).astype(jnp.bfloat16)

    def project_mlp(totals, pieces, start):
        return (
            jnp.dot(normed_mlp, pieces[0], preferred_element_type=jnp.float32),
            jnp.dot(normed_mlp, pieces[1], preferred_element_type=jnp.float32),
        )

    gate_act, upward = mlp_rows(
        project_mlp, (blank(row_count, hidden_cols), blank(row_count, hidden_cols))
    )
    sig_gate = jax.nn.sigmoid(gate_act)
    activated = gate_act * sig_gate
    hidden = (activated * upward).astype(jnp.bfloat16)
    mlp_part = down_rows(placing(hidden), blank(row_count, model_width))
    result = residual + tensor_total(mlp_part)
    out = result.astype(jnp.bfloat16).reshape(seq_count, local_len, model_width)
    grad_hidden = down_rows(adding(grad_out), blank(row_count, hidden_cols))
    derivative = sig_gate * (1.0 + gate_act * (1.0 - sig_gate))
    grad_gate = (grad_hidden * upward * derivative).astype(jnp.bfloat16)
    grad_up = (grad_hidden * activated).astype(jnp.bfloat16)

    def gate_back(total, pieces, start):
        part_sum = column_product(grad_gate, pieces[0]) + column_product(grad_up, pieces[1])
        return part_sum

    grad_normed_mlp = tensor_total(mlp_rows(gate_back, blank(row_count, model_width)))

    def mlp_terms(start, span_rows):
        return jnp.concatenate(
            [
                row_product(normed_mlp, grad_gate),
                row_product(normed_mlp, grad_up),
                row_product(grad_out, hidden),
            ],
            axis=1,
        )

    mlp_grads = owner_rows(mlp_terms, owned_rows)
    grad_gain_mlp = jnp.sum(grad_normed_mlp * hat_mlp, axis=0)
    grad_residual = grad_out.astype(jnp.float32) + norm_back(
        grad_normed_mlp, hat_mlp, scale_mlp, gain_mlp
    )
    grad_branch = grad_residual.astype(jnp.bfloat16)
    grad_attended = attn_out_rows(adding(grad_branch), blank(row_count, query_cols))
    grad_attended_low = grad_attended.astype(jnp.bfloat16)
    grad_blocks = grad_attended_low.reshape(
        seq_count, local_len, kv_heads, head_group, HEAD_DIM
    ).transpose(2, 0, 1, 3, 4)

    def attend_back(operands):
        query_block, key_block, value_block, grad_block, log_total = operands
        scores = (
            jnp.einsum("bigd,bjd->bgij", query_block, key_block, preferred_element_type=jnp.float32)
            * score_scale
        )
        probs = jnp.where(visible, jnp.exp(scores - log_total[..., None]), 0.0)
        probs_low = probs.astype(jnp.bfloat16)
        grad_probs = jnp.einsum(
            "bigd,bjd->bgij", grad_block, value_block, preferred_element_type=jnp.float32
        )
        delta = jnp.sum(probs * grad_probs, axis=-1, keepdims=True)
        grad_scores = (probs * (grad_probs - delta)).astype(jnp.bfloat16)
        grad_query = (
            jnp.einsum("bgij,bjd->bigd", grad_scores, key_block, preferred_element_type=jnp.float32)
            * score_scale
        )
        grad_key = (
            jnp.einsum(
                "bgij,bigd->bjd", grad_scores, query_block, preferred_element_type=jnp.float32
            )
            * score_scale
        )
        grad_value = jnp.einsum(
            "bgij,bigd->bjd", probs_low, grad_block, preferred_element_type=jnp.float32
        )
        return (grad_query, grad_key, grad_value, delta[..., 0])

    grad_query_all, grad_key_all, grad_value_all, delta_all = lax.map(
        attend_back, (query_blocks, key_blocks, value_blocks, grad_blocks, log_totals)
    )
    grad_key_full = grad_key_all.transpose(1, 2, 0, 3).reshape(seq_count, full_len, kv_cols)
    grad_value_full = grad_value_all.transpose(1, 2, 0, 3).reshape(seq_count, full_len, kv_cols)
    grad_key_own, grad_value_own = (
        lax.psum_scatter(
            grad_key_full.astype(jnp.bfloat16), "context", scatter_dimension=1, tiled=True
        ).astype(jnp.float32),
        lax.psum_scatter(
            grad_value_full.astype(jnp.bfloat16), "context", scatter_dimension=1, tiled=True
        ).astype(jnp.float32),
    )
    grad_query_rot = grad_query_all.transpose(1, 2, 0, 3, 4).reshape(
        seq_count, local_len, query_heads, HEAD_DIM
    )
    grad_query_hat = unrotate(grad_query_rot, cosine_table, sine_table)
    grad_key_hat = unrotate(
        grad_key_own.reshape(seq_count, local_len, kv_heads, HEAD_DIM), cosine_table, sine_table
    )
    grad_gain_query = jnp.sum(grad_query_hat * query_hat, axis=(0, 1, 2))
    grad_gain_key = jnp.sum(grad_key_hat * key_hat, axis=(0, 1, 2))
    grad_query_raw = (
        norm_back(grad_query_hat, query_hat, query_scale, gain_heads[0])
        .reshape(row_count, query_cols)
        .astype(jnp.bfloat16)
    )
    grad_key_raw = (
        norm_back(grad_key_hat, key_hat, key_scale, gain_heads[1])
        .reshape(row_count, kv_cols)
        .astype(jnp.bfloat16)
    )
    grad_value_low = grad_value_own.reshape(row_count, kv_cols).astype(jnp.bfloat16)

    def attn_back(total, pieces, start):
        part_sum = (
            column_product(grad_query_raw, pieces[0])
            + column_product(grad_key_raw, pieces[1])
            + column_product(grad_value_low, pieces[2])
        )
        return part_sum

    grad_normed_part = attn_rows(attn_back, blank(row_count, model_width))
    grad_normed_attn, grad_heads_gain = (
        lax.psum(grad_normed_part.astype(jnp.bfloat16), "tensor").astype(jnp.float32),
        lax.psum(jnp.stack([grad_gain_query, grad_gain_key]).astype(jnp.bfloat16), "tensor").astype(
            jnp.float32
        ),
    )

    def attn_terms(start, span_rows):
        return jnp.concatenate(
            [
                row_product(normed_attn, grad_query_raw),
                row_product(normed_attn, grad_key_raw),
                row_product(normed_attn, grad_value_low),
                row_product(grad_branch, attended),
            ],
            axis=1,
        )

    attn_grads = owner_rows(attn_terms, owned_rows)
    grad_gain_attn = jnp.sum(grad_normed_attn * hat_attn, axis=0)
    grad_tokens = grad_residual + norm_back(grad_normed_attn, hat_attn, scale_attn, gain_attn)
    total_attn, total_mlp, total_heads = lax.psum(
        (grad_gain_attn, grad_gain_mlp, grad_heads_gain), ("fsdp", "context")
    )
    query_grad = attn_grads[:, :query_cols]
    key_grad = attn_grads[:, query_cols : query_cols + kv_cols]
    value_grad = attn_grads[:, query_cols + kv_cols : query_cols + 2 * kv_cols]
    output_grad = attn_grads[:, query_cols + 2 * kv_cols :]
    gate_grad = mlp_grads[:, :hidden_cols]
    up_grad = mlp_grads[:, hidden_cols : 2 * hidden_cols]
    down_grad = mlp_grads[:, 2 * hidden_cols :]
    return (
        out,
        grad_tokens.reshape(seq_count, local_len, model_width),
        total_attn,
        total_mlp,
        total_heads,
        query_grad,
        key_grad,
        value_grad,
        output_grad,
        gate_grad,
        up_grad,
        down_grad,
    )


def solution(mesh):
    return jax.shard_map(
        shards,
        mesh=mesh,
        in_specs=(
            P("fsdp", "context", None),
            P("fsdp", "context", None),
            P(),
            P(),
            P(),
            P(("fsdp", "context"), "tensor"),
            P(("fsdp", "context"), "tensor"),
            P(("fsdp", "context"), "tensor"),
            P(("fsdp", "context"), "tensor"),
            P(("fsdp", "context"), "tensor"),
            P(("fsdp", "context"), "tensor"),
            P(("fsdp", "context"), "tensor"),
        ),
        out_specs=(
            P("fsdp", "context", None),
            P("fsdp", "context", None),
            P(),
            P(),
            P(),
            P(("fsdp", "context"), "tensor"),
            P(("fsdp", "context"), "tensor"),
            P(("fsdp", "context"), "tensor"),
            P(("fsdp", "context"), "tensor"),
            P(("fsdp", "context"), "tensor"),
            P(("fsdp", "context"), "tensor"),
            P(("fsdp", "context"), "tensor"),
        ),
        check_vma=False,
    )
```

profile of v0, /device:TPU:0, one launch (start us, length us, event | category | flops | bytes accessed | tf_op | source)
XLA Modules:
  0.0 2445.1 jit_solution(1971568516917772017)
XLA Ops:
  12.2 61.8 %all-gather.11.cloned.1.call-done = bf16[2048,512]{1,0:T(8,128)(2,1)} async-done(((bf16[128,512]{1,0:T(8,128)(2,1)}), bf16[2048,512]{1,0:T(8,128)(2,1)}) %all-gather.11.cloned.1.call-update) | async-done | bytes 2097168 | tf_op jit(solution)/shard_map/all_gather | solution.py:147
  78.0 58.1 %all-gather.13.cloned.1.call-done = bf16[2048,512]{1,0:T(8,128)(2,1)} async-done(((bf16[128,512]{1,0:T(8,128)(2,1)}), bf16[2048,512]{1,0:T(8,128)(2,1)}) %all-gather.13.cloned.1.call-update) | async-done | bytes 2097168 | tf_op jit(solution)/shard_map/all_gather | solution.py:146
  142.4 22.6 all-gather.27.cloned.1.call-done
  166.6 29.8 %all-gather.15.cloned.1.call-done = bf16[1,1024,512]{1,2,0:T(8,128)(2,1)} async-done(((bf16[1,256,512]{1,2,0:T(8,128)(2,1)}), bf16[1,1024,512]{1,2,0:T(8,128)(2,1)}) %all-gather.15.cloned.1.call-update) | async-done | bytes 1048592 | tf_op jit(solution)/shard_map/all_gather | solution.py:201
  198.0 74.9 %all-gather.17.cloned.1.call-done = bf16[2048,1024]{1,0:T(8,128)(2,1)} async-done(((bf16[128,1024]{1,0:T(8,128)(2,1)}), bf16[2048,1024]{1,0:T(8,128)(2,1)}) %all-gather.17.cloned.1.call-update) | async-done | bytes 4194320 | tf_op jit(solution)/shard_map/all_gather | solution.py:145
  279.8 14.4 while.28
  294.2 55.6 %all-gather.19.cloned.1.call-done = bf16[2048,1024]{1,0:T(8,128)(2,1)} async-done(((bf16[128,1024]{1,0:T(8,128)(2,1)}), bf16[2048,1024]{1,0:T(8,128)(2,1)}) %all-gather.19.cloned.1.call-update) | async-done | bytes 4194320 | tf_op jit(solution)/shard_map/all_gather | solution.py:155
  357.4 17.5 all-reduce.6.cloned.1.call-done
  378.6 151.8 %all-gather.21.cloned.1.call-done = bf16[2048,3072]{1,0:T(8,128)(2,1)} async-done(((bf16[128,3072]{1,0:T(8,128)(2,1)}), bf16[2048,3072]{1,0:T(8,128)(2,1)}) %all-gather.21.cloned.1.call-update) | async-done | bytes 12582928 | tf_op jit(solution)/shard_map/all_gather | solution.py:163
  540.3 142.6 %all-gather.25.cloned.1.call-done = bf16[2048,3072]{1,0:T(8,128)(2,1)} async-done(((bf16[128,3072]{1,0:T(8,128)(2,1)}), bf16[2048,3072]{1,0:T(8,128)(2,1)}) %all-gather.25.cloned.1.call-update) | async-done | bytes 12582928 | tf_op jit(solution)/shard_map/all_gather | solution.py:172
  682.9 10.0 fusion.83
  692.8 142.4 %all-gather.23.cloned.1.call-done = bf16[2048,3072]{1,0:T(8,128)(2,1)} async-done(((bf16[128,3072]{1,0:T(8,128)(2,1)}), bf16[2048,3072]{1,0:T(8,128)(2,1)}) %all-gather.23.cloned.1.call-update) | async-done | bytes 12582928 | tf_op jit(solution)/shard_map/all_gather | solution.py:164
  835.2 10.9 multiply_convert_fusion.2
  874.2 24.1 all-reduce.10.cloned.1.call-done
  908.6 36.4 %while.29 = (s32[]{:T(128)}, f32[4,1,256,2,128]{2,4,3,1,0:T(8,128)}, bf16[4,1,1024,128]{2,3,0,1:T(8,128)(2,1)}, bf16[4,1,1024,128]{2,3,0,1:T(8,128)(2,1)}, bf16[...) while((s32[]{:T(128)}, ...), condition=%wide.region_13.14_spmd.clone, body=%wide.region_11.13_spmd.clone.sunk | while | flops 676396544 | bytes 28064952 | solution.py:314
  991.0 12.9 reduce-scatter.7.cloned.1.call-done
  1011.5 17.7 pad_maximum_fusion.1
  1029.3 14.7 fusion.118
  1044.1 10.3 fusion.119
  1054.4 10.4 convolution_bitcast_fusion.2
  1064.8 51.4 %pad_maximum_fusion = f32[2048,9216]{1,0:T(8,128)} fusion(f32[2048,3072]{1,0:T(8,128)} %convolution_bitcast_fusion.2, f32[2048,3072]{1,0:T(8,128)} %fusion.119, f32[2048,3072]{1,0:T(8,128)} %fusion.118), kind=kLoop, calls=%fused_computation.66 | loop fusion | flops 37748736 | bytes 150994944 | tf_op jit(solution)/shard_map/concatenate | solution.py:265
  1120.8 76.0 %all-reduce = (f32[2048]{0:T(1024)}, f32[2048]{0:T(1024)}, f32[2,128]{1,0:T(2,128)}) all-reduce(f32[2048]{0:T(1024)S(1)} %get-tuple-element.228, f32[2048]{0:T(1024)S(1)} %copy-done.37, bf16[2,128]{1,0:T(2,128)(2,1)S(1)} %psum.62), channel_id=1, replica_groups=mesh['fsdp'=4,'context'=4,'tensor'=2] {'fsdp','context'}, use_global_device_ids=true, to_apply=%region_21.22 | all-reduce | flops 4352 | bytes 34304 | tf_op jit(solution)/shard_map/psum | solution.py:378
  1200.0 193.3 %reduce-scatter.9.cloned.1.call-done = f32[128,3072]{0,1:T(8,128)} async-done(((f32[2048,3072]{0,1:T(8,128)}), f32[128,3072]{0,1:T(8,128)}) %reduce-scatter.9.cloned.1.call-update) | async-done | bytes 1572880 | tf_op jit(solution)/shard_map/reduce_scatter | solution.py:96
  1399.3 1034.2 %reduce-scatter.11.cloned.1.call-done = f32[128,9216]{1,0:T(8,128)} async-done(((f32[2048,9216]{1,0:T(8,128)}), f32[128,9216]{1,0:T(8,128)}) %reduce-scatter.11.cloned.1.call-update) | async-done | bytes 4718608 | tf_op jit(solution)/shard_map/reduce_scatter | solution.py:96
  (287 shorter events, 206.8 us)
Async XLA Ops:
  7.2 66.8 %all-gather.11.cloned.1.call-start = ((), (), s32[]{:S(2)}) async-start(), calls=%async_computation.4 | async-start | bytes 2228224 | tf_op jit(solution)/shard_map/all_gather | solution.py:147
  7.9 128.2 %all-gather.13.cloned.1.call-start = ((), (), s32[]{:S(2)}) async-start(), calls=%async_computation.5 | async-start | bytes 2228224 | tf_op jit(solution)/shard_map/all_gather | solution.py:146
  8.7 156.4 %all-gather.27.cloned.1.call-start = ((), (), s32[]{:S(2)}) async-start(), calls=%async_computation.18 | async-start | bytes 1310720 | tf_op jit(solution)/shard_map/all_gather | solution.py:204
  12.2 126.9 %copy-start.42 = (f32[128]{0:T(128)}, f32[128]{0:T(128)S(1)}, u32[]{:S(2)}) copy-start(f32[128]{0:T(128)S(1)} %get-tuple-element.310) | copy-start | bytes 1540
  12.2 260.7 %copy-start.35 = (f32[256]{0:T(256)}, f32[256]{0:T(256)S(1)}, u32[]{:S(2)}) copy-start(f32[256]{0:T(256)S(1)} %add_rsqrt_fusion.3) | copy-start | bytes 3076
  12.2 123.9 %copy-start = (bf16[1,256,2048]{2,1,0:T(8,128)(2,1)S(1)}, bf16[1,256,2048]{2,1,0:T(8,128)(2,1)}, u32[]{:S(2)}) copy-start(bf16[1,256,2048]{2,1,0:T(8,128)(2,1)} %param.16) | copy-start | bytes 3145732
  77.4 119.0 %all-gather.15.cloned.1.call-start = ((), (), s32[]{:S(2)}) async-start(), calls=%async_computation.6 | async-start | bytes 1310720 | tf_op jit(solution)/shard_map/all_gather | solution.py:201
  141.2 131.7 %all-gather.17.cloned.1.call-start = ((), (), s32[]{:S(2)}) async-start(), calls=%async_computation.7 | async-start | bytes 4456448 | tf_op jit(solution)/shard_map/all_gather | solution.py:145
  141.8 208.0 %all-gather.19.cloned.1.call-start = ((), (), s32[]{:S(2)}) async-start(), calls=%async_computation.8 | async-start | bytes 4456448 | tf_op jit(solution)/shard_map/all_gather | solution.py:155
  142.4 232.5 %all-reduce.6.cloned.1.call-start = ((), (), s32[]{:S(2)}) async-start(), calls=%async_computation.9 | async-start | bytes 4194304 | tf_op jit(solution)/shard_map/psum | solution.py:92
  294.2 60.5 %copy-start.6 = (bf16[4,1,1024,128]{3,2,1,0:T(8,128)(2,1)}, bf16[4,1,1024,128]{3,2,1,0:T(8,128)(2,1)S(1)}, u32[]{:S(2)}) copy-start(bf16[4,1,1024,128]{3,2,1,0:T(8,128)(2,1)S(1)} %get-tuple-element.501) | copy-start | bytes 3145732
  294.2 60.5 %copy-start.12 = (bf16[4,1,1024,128]{3,2,1,0:T(8,128)(2,1)}, bf16[4,1,1024,128]{3,2,1,0:T(8,128)(2,1)S(1)}, u32[]{:S(2)}) copy-start(bf16[4,1,1024,128]{3,2,1,0:T(8,128)(2,1)S(1)} %get-tuple-element.504) | copy-start | bytes 3145732
  294.2 60.5 %copy-start.33 = (s32[256]{0:T(256)}, s32[256]{0:T(256)S(1)}, u32[]{:S(2)}) copy-start(s32[256]{0:T(256)S(1)} %get-tuple-element.545) | copy-start | bytes 3076
  354.8 175.6 %all-gather.21.cloned.1.call-start = ((), (), s32[]{:S(2)}) async-start(), calls=%async_computation.10 | async-start | bytes 13369344 | tf_op jit(solution)/shard_map/all_gather | solution.py:163
  355.5 327.3 %all-gather.25.cloned.1.call-start = ((), (), s32[]{:S(2)}) async-start(), calls=%async_computation.12 | async-start | bytes 13369344 | tf_op jit(solution)/shard_map/all_gather | solution.py:172
  356.3 478.9 %all-gather.23.cloned.1.call-start = ((), (), s32[]{:S(2)}) async-start(), calls=%async_computation.11 | async-start | bytes 13369344 | tf_op jit(solution)/shard_map/all_gather | solution.py:164
  356.9 541.4 %all-reduce.10.cloned.1.call-start = ((), (), s32[]{:S(2)}) async-start(), calls=%async_computation.19 | async-start | bytes 8388608 | tf_op jit(solution)/shard_map/psum | solution.py:92
  846.2 16.0 copy-start.26
  871.6 104.2 %reduce-scatter.5.cloned.1.call-start = ((), (), s32[]{:S(2)}) async-start(), calls=%async_computation.13 | async-start | bytes 1310720 | tf_op jit(solution)/shard_map/reduce_scatter | solution.py:320
  947.2 56.7 %reduce-scatter.7.cloned.1.call-start = ((), (), s32[]{:S(2)}) async-start(), calls=%async_computation.14 | async-start | bytes 1310720 | tf_op jit(solution)/shard_map/reduce_scatter | solution.py:323
  962.9 155.9 %all-reduce.8.cloned.1.call-start = ((), (), s32[]{:S(2)}) async-start(), calls=%async_computation.15 | async-start | bytes 2097152 | tf_op jit(solution)/shard_map/psum | solution.py:358
  1008.0 385.3 %reduce-scatter.9.cloned.1.call-start = ((), (), s32[]{:S(2)}) async-start(), calls=%async_computation.16 | async-start | bytes 26738688 | tf_op jit(solution)/shard_map/reduce_scatter | solution.py:96
  1029.2 1404.2 %reduce-scatter.11.cloned.1.call-start = ((), (), s32[]{:S(2)}) async-start(), calls=%async_computation.17 | async-start | bytes 80216064 | tf_op jit(solution)/shard_map/reduce_scatter | solution.py:96
  1029.3 14.8 copy-start.8
  (45 other events, 136.2 us)
Sparse Core Ops, SparseCore 0:
  10.8 63.1 all-gather.10
  76.8 59.2 all-gather.12
  138.2 26.7 all-gather.26
  167.0 29.2 all-gather.14
  199.0 73.8 all-gather.16
  275.5 74.2 all-gather.18
  354.9 19.8 all-reduce.5
  377.7 152.6 all-gather.20
  533.2 149.6 all-gather.24
  685.6 149.6 all-gather.22
  871.7 26.5 all-reduce.9
  947.3 28.4 reduce-scatter.4
  978.1 25.7 reduce-scatter.6
  1008.1 17.9 all-reduce.7
  1031.7 361.5 reduce-scatter.8
  1399.1 1034.3 reduce-scatter.10
where the time goes:
time: 2450 us
  waiting for transfers between devices  2030 us (83%)
  matrix products  169 us (7%)
  other arithmetic  99.7 us (4%)
  blocking collectives  78.5 us (3%)
  local copies, waits for them, and re-layouts  47.4 us (2%)
    reduce_scatter x2, waiting for transfers between devices, owner_rows(): lax.psum_scatter(term_fn(jnp.int32(0), lax.axis_size(('fsdp', 'context'))...  1230 us
    all_gather x1, waiting for transfers between devices, mlp_rows(): lax.all_gather(gate_weight, ('fsdp', 'context'), axis=0, tiled=True)  152 us
    all_gather x1, waiting for transfers between devices, down_rows(): lax.all_gather(down_weight, ('fsdp', 'context'), axis=0, tiled=True)  143 us
    all_gather x1, waiting for transfers between devices, mlp_rows(): lax.all_gather(up_weight, ('fsdp', 'context'), axis=0, tiled=True)  142 us
    psum x1, blocking collectives, shards(): lax.psum((grad_gain_attn, grad_gain_mlp, grad_heads_gain), ('fsdp', 'cont...  76 us
    all_gather x1, waiting for transfers between devices, attn_rows(): lax.all_gather(query_weight, ('fsdp', 'context'), axis=0, tiled=True)  74.9 us
    all_gather x1, waiting for transfers between devices, attn_rows(): lax.all_gather(value_matrix, ('fsdp', 'context'), axis=0, tiled=True)  61.8 us
    all_gather x1, waiting for transfers between devices, attn_rows(): lax.all_gather(key_matrix, ('fsdp', 'context'), axis=0, tiled=True)  58.1 us
  transfers between devices with their start and end apart: 16, of which 15 were waited for; matrix products, arithmetic and copies ran while one was open for 9% of the time, Pallas kernels for 0%

commit v1 on v0

--- a/solution.py
+++ b/solution.py
@@ -401,9 +401,244 @@
     )
 
 
+def token_half(block, index, parts):
+    rows = block.shape[0] // parts
+    return lax.dynamic_slice_in_dim(block, index * rows, rows, axis=0)
+
+
+def gather_tokens(rows):
+    return lax.all_gather(rows, ("context", "tensor"), axis=0, tiled=True)
+
+
+def scatter_tokens(partial_sum):
+    return lax.psum_scatter(
+        partial_sum.astype(jnp.bfloat16), ("context", "tensor"), scatter_dimension=0, tiled=True
+    ).astype(jnp.float32)
+
+
+def join_cores(rows):
+    return lax.all_gather(rows, "tensor", axis=0, tiled=True)
+
+
+def column_parts(weights, parts):
+    return jnp.concatenate(
+        [w.reshape(w.shape[0], parts, w.shape[1] // parts) for w in weights], axis=2
+    )
+
+
+def fetch_columns(weights, parts):
+    pieces = column_parts(weights, parts)
+    rows, _, width = pieces.shape
+    lined = lax.all_to_all(pieces, "context", split_axis=1, concat_axis=0, tiled=True)
+    return lax.all_gather(lined.reshape(parts * rows, width), "fsdp", axis=0, tiled=True)
+
+
+def return_columns(grads, parts, widths):
+    own = lax.psum_scatter(grads, "fsdp", scatter_dimension=0, tiled=True)
+    rows = own.shape[0] // parts
+    back = lax.all_to_all(
+        own.reshape(parts, rows, own.shape[1]), "context", split_axis=0, concat_axis=0, tiled=True
+    )
+    outs = []
+    start = 0
+    for width in widths:
+        piece = back[:, :, start : start + width].astype(jnp.float32)
+        outs.append(piece.transpose(1, 0, 2).reshape(rows, parts * width))
+        start += width
+    return outs
+
+
+def line_shards(
+    tokens,
+    cotangent,
+    norm_gain_attn,
+    norm_gain_mlp,
+    head_gains,
+    query_weight,
+    key_matrix,
+    value_matrix,
+    output_weight,
+    gate_weight,
+    up_weight,
+    down_weight,
+):
+    seq_count, local_len, model_width = tokens.shape
+    parts = lax.axis_size("context")
+    cores = lax.axis_size("tensor")
+    core = lax.axis_index("tensor")
+    full_len = local_len * parts
+    q_cols = query_weight.shape[1] // parts
+    kv_cols = key_matrix.shape[1] // parts
+    h_cols = gate_weight.shape[1] // parts
+    q_heads = q_cols // HEAD_DIM
+    kv_heads = kv_cols // HEAD_DIM
+    head_group = q_heads // kv_heads
+    score_scale = 1.0 / math.sqrt(HEAD_DIM)
+    positions = jnp.arange(full_len, dtype=jnp.int32)
+    cosine_table, sine_table = rope_tables(positions, HEAD_DIM)
+    cosine_table = cosine_table[:, None, :]
+    sine_table = sine_table[:, None, :]
+    visible = positions[None, :] <= positions[:, None]
+    gain_attn = norm_gain_attn.astype(jnp.float32)
+    gain_mlp = norm_gain_mlp.astype(jnp.float32)
+    gain_heads = head_gains.astype(jnp.float32)
+
+    own_cot = token_half(cotangent.reshape(local_len, model_width), core, cores)
+    inputs = token_half(tokens.reshape(local_len, model_width), core, cores).astype(jnp.float32)
+    scale_attn = rms_scale(inputs)
+    hat_attn = inputs * scale_attn
+    normed_attn = gather_tokens((hat_attn * gain_attn).astype(jnp.bfloat16))
+    attn_weights = fetch_columns((query_weight, key_matrix, value_matrix, output_weight), parts)
+    grad_out = gather_tokens(own_cot)
+    mlp_in = fetch_columns((gate_weight, up_weight), parts)
+    mlp_down = fetch_columns((down_weight,), parts)
+
+    qkv_cols = q_cols + 2 * kv_cols
+    in_weights = attn_weights[:, :qkv_cols]
+    out_weights = attn_weights[:, qkv_cols:]
+    raw = jnp.dot(normed_attn, in_weights, preferred_element_type=jnp.float32)
+    query_split = raw[:, :q_cols].reshape(full_len, q_heads, HEAD_DIM)
+    query_scale = rms_scale(query_split)
+    query_hat = query_split * query_scale
+    queries = rotate(query_hat * gain_heads[0], cosine_table, sine_table).astype(jnp.bfloat16)
+    key_split = raw[:, q_cols : q_cols + kv_cols].reshape(full_len, kv_heads, HEAD_DIM)
+    key_scale = rms_scale(key_split)
+    key_hat = key_split * key_scale
+    keys = rotate(key_hat * gain_heads[1], cosine_table, sine_table).astype(jnp.bfloat16)
+    values = raw[:, q_cols + kv_cols :].astype(jnp.bfloat16).reshape(full_len, kv_heads, HEAD_DIM)
+    queries = queries.reshape(full_len, kv_heads, head_group, HEAD_DIM)
+
+    scores = (
+        jnp.einsum("ikgd,jkd->kgij", queries, keys, preferred_element_type=jnp.float32)
+        * score_scale
+    )
+    weights = jnp.where(visible, jnp.exp(scores), 0.0)
+    probs = weights / jnp.sum(weights, axis=-1, keepdims=True)
+    probs_low = probs.astype(jnp.bfloat16)
+    attended = (
+        jnp.einsum("kgij,jkd->ikgd", probs_low, values, preferred_element_type=jnp.float32)
+        .astype(jnp.bfloat16)
+        .reshape(full_len, q_cols)
+    )
+    residual = inputs + scatter_tokens(column_product(attended, out_weights))
+    scale_mlp = rms_scale(residual)
+    hat_mlp = residual * scale_mlp
+    normed_mlp = gather_tokens((hat_mlp * gain_mlp).astype(jnp.bfloat16))
+
+    both = jnp.dot(normed_mlp, mlp_in, preferred_element_type=jnp.float32)
+    gate_act = both[:, :h_cols]
+    upward = both[:, h_cols:]
+    sig_gate = jax.nn.sigmoid(gate_act)
+    activated = gate_act * sig_gate
+    hidden = (activated * upward).astype(jnp.bfloat16)
+    grad_hidden = jnp.dot(grad_out, mlp_down, preferred_element_type=jnp.float32)
+    derivative = sig_gate * (1.0 + gate_act * (1.0 - sig_gate))
+    grad_gate = (grad_hidden * upward * derivative).astype(jnp.bfloat16)
+    grad_up = (grad_hidden * activated).astype(jnp.bfloat16)
+    grad_both = jnp.concatenate([grad_gate, grad_up], axis=1)
+    grad_normed_mlp = scatter_tokens(column_product(grad_both, mlp_in))
+    result = residual + scatter_tokens(column_product(hidden, mlp_down))
+    mlp_terms = jnp.concatenate(
+        [
+            row_product(normed_mlp, grad_both).astype(jnp.bfloat16),
+            row_product(grad_out, hidden).astype(jnp.bfloat16),
+        ],
+        axis=1,
+    )
+    gate_grad, up_grad, down_grad = return_columns(mlp_terms, parts, (h_cols, h_cols, h_cols))
+
+    gain_mlp_part = jnp.sum(grad_normed_mlp * hat_mlp, axis=0)
+    grad_residual = own_cot.astype(jnp.float32) + norm_back(
+        grad_normed_mlp, hat_mlp, scale_mlp, gain_mlp
+    )
+    grad_branch = gather_tokens(grad_residual.astype(jnp.bfloat16))
+    grad_attended = (
+        jnp.dot(grad_branch, out_weights, preferred_element_type=jnp.float32)
+        .astype(jnp.bfloat16)
+        .reshape(full_len, kv_heads, head_group, HEAD_DIM)
+    )
+    grad_probs = jnp.einsum(
+        "ikgd,jkd->kgij", grad_attended, values, preferred_element_type=jnp.float32
+    )
+    delta = jnp.sum(probs * grad_probs, axis=-1, keepdims=True)
+    grad_scores = (probs * (grad_probs - delta)).astype(jnp.bfloat16)
+    grad_queries = (
+        jnp.einsum("kgij,jkd->ikgd", grad_scores, keys, preferred_element_type=jnp.float32)
+        * score_scale
+    ).reshape(full_len, q_heads, HEAD_DIM)
+    grad_keys = (
+        jnp.einsum("kgij,ikgd->jkd", grad_scores, queries, preferred_element_type=jnp.float32)
+        * score_scale
+    )
+    grad_values = jnp.einsum(
+        "kgij,ikgd->jkd", probs_low, grad_attended, preferred_element_type=jnp.float32
+    )
+    grad_query_hat = unrotate(grad_queries, cosine_table, sine_table)
+    grad_key_hat = unrotate(grad_keys, cosine_table, sine_table)
+    heads_part = jnp.stack(
+        [
+            jnp.sum(grad_query_hat * query_hat, axis=(0, 1)),
+            jnp.sum(grad_key_hat * key_hat, axis=(0, 1)),
+        ]
+    )
+    grad_raw = jnp.concatenate(
+        [
+            norm_back(grad_query_hat, query_hat, query_scale, gain_heads[0]).reshape(
+                full_len, q_cols
+            ),
+            norm_back(grad_key_hat, key_hat, key_scale, gain_heads[1]).reshape(full_len, kv_cols),
+            grad_values.reshape(full_len, kv_cols),
+        ],
+        axis=1,
+    ).astype(jnp.bfloat16)
+    grad_normed_attn = scatter_tokens(column_product(grad_raw, in_weights))
+    attn_terms = jnp.concatenate(
+        [
+            row_product(normed_attn, grad_raw).astype(jnp.bfloat16),
+            row_product(grad_branch, attended).astype(jnp.bfloat16),
+        ],
+        axis=1,
+    )
+    query_grad, key_grad, value_grad, output_grad = return_columns(
+        attn_terms, parts, (q_cols, kv_cols, kv_cols, q_cols)
+    )
+    gain_attn_part = jnp.sum(grad_normed_attn * hat_attn, axis=0)
+    grad_tokens = grad_residual + norm_back(grad_normed_attn, hat_attn, scale_attn, gain_attn)
+    total_attn, total_mlp, total_heads = lax.psum(
+        (gain_attn_part, gain_mlp_part, heads_part), ("fsdp", "context", "tensor")
+    )
+    return (
+        join_cores(result.astype(jnp.bfloat16)).reshape(tokens.shape),
+        join_cores(grad_tokens).reshape(tokens.shape),
+        total_attn,
+        total_mlp,
+        total_heads,
+        query_grad,
+        key_grad,
+        value_grad,
+        output_grad,
+        gate_grad,
+        up_grad,
+        down_grad,
+    )
+
+
+def layer(*operands):
+    tokens, key_matrix, gate_weight = operands[0], operands[6], operands[9]
+    parts = lax.axis_size("context")
+    cores = lax.axis_size("tensor")
+    fits = (
+        tokens.shape[0] == 1
+        and key_matrix.shape[1] % (parts * HEAD_DIM) == 0
+        and gate_weight.shape[1] % (parts * HEAD_DIM) == 0
+        and tokens.shape[1] % (cores * 16) == 0
+    )
+    return line_shards(*operands) if fits else shards(*operands)
+
+
 def solution(mesh):
     return jax.shard_map(
-        shards,
+        layer,
         mesh=mesh,
         in_specs=(
             P("fsdp", "context", None),

time: 2450 us -> 956 us (0.39)
  waiting for transfers between devices: 2030 us -> 560 us
  blocking collectives: 78.5 us -> 157 us
  matrix products: 169 us -> 99.2 us
  other arithmetic: 99.7 us -> 49.2 us
    reduce_scatter x4 -> x6, waiting for transfers between devices: 1250 us -> 276 us  [the longest x4 194 us: scatter_tokens(): lax.psum_scatter(partial_sum.astype(jnp.bfloat16), ('context', 'tensor'),...]
    all_gather x9, waiting for transfers between devices: 740 us -> 275 us  [the longest x4 166 us: gather_tokens(): return lax.all_gather(rows, ('context', 'tensor'), axis=0, tiled=True)]
    all_to_all x0 -> x3, blocking collectives: none -> 120 us  [fetch_columns(): lax.all_to_all(pieces, 'context', split_axis=1, concat_axis=0, tiled=True)]
    concatenate x2 -> x5, other arithmetic: 69.2 us -> 15.9 us  [the longest x1 11.4 us: line_shards(): jnp.concatenate([row_product(normed_mlp, grad_both).astype(jnp.bfloat16),...]
    psum x3 -> x0, waiting for transfers between devices: 41.6 us -> none  [the longest x2 41.6 us: tensor_total(): return lax.psum(partial_sum, 'tensor')]
    psum x2 -> x1, blocking collectives: 78.5 us -> 37.3 us  [line_shards(): lax.psum((gain_attn_part, gain_mlp_part, heads_part), ('fsdp', 'context',...]
    dot_general x7 -> x4, matrix products: 50.3 us -> 20.3 us  [row_product(): lax.dot_general(left, right, (((0,), (0,)), ((), ())), preferred_element_...]
    dot_general x35 -> x10, matrix products: 77 us -> 54.6 us  [the longest x1 11.6 us: line_shards(): both = jnp.dot(normed_mlp, mlp_in, preferred_element_type=jnp.float32)]
  transfers between devices with their start and end apart: 16 -> 17, of which waited for: 15 -> 14; matrix products, arithmetic and copies ran while one was open for 9% -> 15% of each run, Pallas kernels for 0% -> 0%
where the time goes in v1:
time: 956 us; the launch traced here: 945 us
  waiting for transfers between devices  560 us (59%)
  blocking collectives  157 us (16%)
  matrix products  99.2 us (10%)
  local copies, waits for them, and re-layouts  54.1 us (6%)
  other arithmetic  49.2 us (5%)
  between operations  15 us (2%)
  starting transfers between devices  10.8 us (1%)
    reduce_scatter x4, waiting for transfers between devices, scatter_tokens(): lax.psum_scatter(partial_sum.astype(jnp.bfloat16), ('context', 'tensor'),...  194 us
    all_gather x4, waiting for transfers between devices, gather_tokens(): return lax.all_gather(rows, ('context', 'tensor'), axis=0, tiled=True)  166 us
    all_to_all x3, blocking collectives, fetch_columns(): lax.all_to_all(pieces, 'context', split_axis=1, concat_axis=0, tiled=True)  120 us
    all_gather x3, waiting for transfers between devices, fetch_columns(): lax.all_gather(lined.reshape(parts * rows, width), 'fsdp', axis=0, tiled=...  108 us
    reduce_scatter x2, waiting for transfers between devices, return_columns(): own = lax.psum_scatter(grads, 'fsdp', scatter_dimension=0, tiled=True)  81.7 us
    psum x1, blocking collectives, line_shards(): lax.psum((gain_attn_part, gain_mlp_part, heads_part), ('fsdp', 'context',...  37.3 us
    unnamed x94, local copies, waits for them, and re-layouts  34.3 us
    dot_general x4, matrix products, column_product(): lax.dot_general(left, right, (((1,), (1,)), ((), ())), preferred_element_...  24.3 us
  transfers between devices with their start and end apart: 17, of which 14 were waited for; matrix products, arithmetic and copies ran while one was open for 15% of the time, Pallas kernels for 0%

profile of v1, /device:TPU:0, one launch (start us, length us, event | category | flops | bytes accessed | tf_op | source)
XLA Modules:
  0.0 945.4 jit_solution(16933035054668553200)
XLA Ops:
  11.7 26.3 %all_to_all.55 = bf16[128,4,768]{0,2,1:T(8,128)(2,1)S(1)} all-to-all(bf16[128,4,768]{0,2,1:T(8,128)(2,1)S(1)} %pad_maximum_fusion.8), channel_id=1, replica_groups=mesh['fsdp'=4,'context'=4,'tensor'=2] {'context'}, dimensions={1} | all-to-all | bytes 1572864 | tf_op jit(solution)/shard_map/all_to_all | solution.py:432
  45.4 36.9 %all-gather.13.cloned.1.call-done = bf16[2048,768]{1,0:T(8,128)(2,1)} async-done(((bf16[512,768]{1,0:T(8,128)(2,1)}), bf16[2048,768]{1,0:T(8,128)(2,1)}) %all-gather.13.cloned.1.call-update) | async-done | bytes 3145744 | tf_op jit(solution)/shard_map/all_gather | solution.py:433
  82.3 49.1 %all-gather.11.cloned.1.call-done = bf16[1024,2048]{1,0:T(8,128)(2,1)} async-done(((bf16[128,2048]{1,0:T(8,128)(2,1)}), bf16[1024,2048]{1,0:T(8,128)(2,1)}) %all-gather.11.cloned.1.call-update) | async-done | bytes 4194320 | tf_op jit(solution)/shard_map/all_gather | solution.py:410
  162.9 66.5 %all_to_all.56 = bf16[128,4,1536]{0,2,1:T(8,128)(2,1)} all-to-all(bf16[128,4,1536]{0,2,1:T(8,128)(2,1)S(1)} %pad_maximum_fusion.5), channel_id=1, replica_groups=mesh['fsdp'=4,'context'=4,'tensor'=2] {'context'}, dimensions={1} | all-to-all | bytes 3145728 | tf_op jit(solution)/shard_map/all_to_all | solution.py:432
  240.7 27.0 %all_to_all.57 = bf16[128,4,768]{0,2,1:T(8,128)(2,1)} all-to-all(bf16[128,4,768]{0,2,1:T(8,128)(2,1)} %bitcast.255), channel_id=1, replica_groups=mesh['fsdp'=4,'context'=4,'tensor'=2] {'context'}, dimensions={1} | all-to-all | bytes 1572864 | tf_op jit(solution)/shard_map/all_to_all | solution.py:432
  272.0 38.0 %all-gather.17.cloned.1.call-done = bf16[2048,1536]{1,0:T(8,128)(2,1)} async-done(((bf16[512,1536]{1,0:T(8,128)(2,1)}), bf16[2048,1536]{1,0:T(8,128)(2,1)}) %all-gather.17.cloned.1.call-update) | async-done | bytes 6291472 | tf_op jit(solution)/shard_map/all_gather | solution.py:433
  310.1 48.9 %all-gather.15.cloned.1.call-done = bf16[1024,2048]{1,0:T(8,128)(2,1)} async-done(((bf16[128,2048]{1,0:T(8,128)(2,1)}), bf16[1024,2048]{1,0:T(8,128)(2,1)}) %all-gather.15.cloned.1.call-update) | async-done | bytes 4194320 | tf_op jit(solution)/shard_map/all_gather | solution.py:410
  359.0 11.6 %fusion.93 = f32[1024,1536]{1,0:T(8,128)} fusion(bf16[1024,2048]{1,0:T(8,128)(2,1)} %all-gather.15.cloned.1.call-done, bf16[2048,1536]{1,0:T(8,128)(2,1)} %all-gather.17.cloned.1.call-done), kind=kOutput, calls=%fused_computation.165 | convolution fusion | flops 6442450944 | bytes 16777216 | tf_op jit(solution)/shard_map/dot_general | solution.py:528
  370.6 33.3 %all-gather.19.cloned.1.call-done = bf16[2048,768]{1,0:T(8,128)(2,1)} async-done(((bf16[512,768]{1,0:T(8,128)(2,1)}), bf16[2048,768]{1,0:T(8,128)(2,1)}) %all-gather.19.cloned.1.call-update) | async-done | bytes 3145744 | tf_op jit(solution)/shard_map/all_gather | solution.py:433
  403.9 49.1 %all-gather.27.cloned.1.call-done = bf16[1,1024,2048]{2,1,0:T(8,128)(2,1)} async-done(((bf16[1,128,2048]{2,1,0:T(8,128)(2,1)}), bf16[1,1024,2048]{2,1,0:T(8,128)(2,1)}) %all-gather.27.cloned.1.call-update) | async-done | bytes 4194320 | tf_op jit(solution)/shard_map/all_gather | solution.py:410
  453.0 10.5 %multiply_convert_fusion.1 = (bf16[1024,768]{1,0:T(8,128)(2,1)S(1)}, bf16[1024,768]{1,0:T(8,128)(2,1)S(1)}, bf16[1024,768]{1,0:T(8,128)(2,1)}) fusion(f32[1024,1536]{1,0:T(8,128)} %fusion.93, bf16[2048,768]{1,0:T(8,128)(2,1)} %all-gather.19.cloned.1.call-done, bf16[1,1024,2048]{2,1,0:T(8,128)(2,1)} %all-gather.27.cloned.1.call-done), kind=kOutput, calls=%fused_computation.29 | convolution fusion | flops 3233021952 | bytes 18350080 | tf_op jit(solution)/shard_map/dot_general | solution.py:534
  465.2 8.3 convolution_convert_fusion.1
  473.6 48.8 %reduce-scatter.11.cloned.1.call-done = bf16[128,2048]{1,0:T(8,128)(2,1)} async-done(((bf16[1024,2048]{1,0:T(8,128)(2,1)}), bf16[128,2048]{1,0:T(8,128)(2,1)}) %reduce-scatter.11.cloned.1.call-update) | async-done | bytes 524304 | tf_op jit(solution)/shard_map/reduce_scatter | solution.py:414
  527.0 6.3 fusion.14
  533.4 7.8 convolution_convert_fusion
  541.2 11.4 %pad_maximum_fusion = bf16[2048,2304]{0,1:T(8,128)(2,1)} fusion(bf16[2048,768]{0,1:T(8,128)(2,1)S(1)} %fusion.14, bf16[2048,1536]{0,1:T(8,128)(2,1)S(1)} %convolution_convert_fusion), kind=kLoop, calls=%fused_computation | loop fusion | flops 18874368 | bytes 18874368 | tf_op jit(solution)/shard_map/concatenate | solution.py:541
  552.8 19.4 %all-gather.23.cloned.1.call-done = bf16[1024,2048]{1,0:T(8,128)(2,1)} async-done(((bf16[128,2048]{1,0:T(8,128)(2,1)}), bf16[1024,2048]{1,0:T(8,128)(2,1)}) %all-gather.23.cloned.1.call-update) | async-done | bytes 4194320 | tf_op jit(solution)/shard_map/all_gather | solution.py:410
  612.7 7.0 convolution_convert_fusion.4
  628.8 40.1 %reduce-scatter.17.cloned.1.call-done = bf16[512,2304]{0,1:T(8,128)(2,1)} async-done(((bf16[2048,2304]{0,1:T(8,128)(2,1)}), bf16[512,2304]{0,1:T(8,128)(2,1)}) %reduce-scatter.17.cloned.1.call-update) | async-done | bytes 2359312 | tf_op jit(solution)/shard_map/reduce_scatter | solution.py:437
  677.2 89.3 %reduce-scatter.13.cloned.1.call-done = bf16[128,2048]{1,0:T(8,128)(2,1)} async-done(((bf16[1024,2048]{1,0:T(8,128)(2,1)}), bf16[128,2048]{1,0:T(8,128)(2,1)}) %reduce-scatter.13.cloned.1.call-update) | async-done | bytes 524304 | tf_op jit(solution)/shard_map/reduce_scatter | solution.py:414
  767.9 53.6 %reduce-scatter.9.cloned.1.call-done = bf16[128,2048]{1,0:T(8,128)(2,1)} async-done(((bf16[1024,2048]{1,0:T(8,128)(2,1)}), bf16[128,2048]{1,0:T(8,128)(2,1)}) %reduce-scatter.9.cloned.1.call-update) | async-done | bytes 524304 | tf_op jit(solution)/shard_map/reduce_scatter | solution.py:414
  825.3 41.6 %reduce-scatter.15.cloned.1.call-done = bf16[512,768]{0,1:T(8,128)(2,1)} async-done(((bf16[2048,768]{0,1:T(8,128)(2,1)}), bf16[512,768]{0,1:T(8,128)(2,1)}) %reduce-scatter.15.cloned.1.call-update) | async-done | bytes 786448 | tf_op jit(solution)/shard_map/reduce_scatter | solution.py:437
  885.2 8.4 all-to-all-done.3
  897.4 37.3 %all-reduce = (f32[2048]{0:T(1024)}, f32[2048]{0:T(1024)}, f32[2,128]{1,0:T(2,128)}) all-reduce(f32[2048]{0:T(1024)S(1)} %get-tuple-element.40, f32[2048]{0:T(1024)S(1)} %get-tuple-element.38, f32[2,128]{1,0:T(2,128)S(1)} %pad_maximum_fusion.15), channel_id=1, replica_groups=mesh['fsdp'=4,'context'=4,'tensor'=2] {'fsdp','context','tensor'}, use_global_device_ids=true, to_apply=%region_15.16 | all-reduce | flops 4352 | bytes 34816 | tf_op jit(solution)/shard_map/psum | solution.py:607
  (198 shorter events, 153.9 us)
Async XLA Ops:
  7.2 75.1 %all-gather.13.cloned.1.call-start = ((), (), s32[]{:S(2)}) async-start(), calls=%async_computation.12 | async-start | bytes 3932160 | tf_op jit(solution)/shard_map/all_gather | solution.py:433
  11.7 29.3 %copy-start.29 = (bf16[2,128]{1,0:T(2,128)(2,1)S(1)}, bf16[2,128]{1,0:T(2,128)(2,1)}, u32[]{:S(2)}) copy-start(bf16[2,128]{1,0:T(2,128)(2,1)} %param.16) | copy-start | bytes 1540
  39.2 92.2 %all-gather.11.cloned.1.call-start = ((), (), s32[]{:S(2)}) async-start(), calls=%async_computation.11 | async-start | bytes 4718592 | tf_op jit(solution)/shard_map/all_gather | solution.py:410
  39.2 43.0 %copy-start.20 = (f32[2048]{0:T(1024)}, f32[2048]{0:T(1024)S(1)}, u32[]{:S(2)}) copy-start(f32[2048]{0:T(1024)S(1)} %convert_element_type.151) | copy-start | bytes 24580
  41.0 194.0 %reduce-scatter.7.cloned.1.call-start = ((), (), s32[]{:S(2)}) async-start(), calls=%async_computation.13 | async-start | bytes 4718592 | tf_op jit(solution)/shard_map/reduce_scatter | solution.py:414
  156.3 153.7 %all-gather.17.cloned.1.call-start = ((), (), s32[]{:S(2)}) async-start(), calls=%async_computation.15 | async-start | bytes 7864320 | tf_op jit(solution)/shard_map/all_gather | solution.py:433
  232.1 126.9 %all-gather.15.cloned.1.call-start = ((), (), s32[]{:S(2)}) async-start(), calls=%async_computation.14 | async-start | bytes 4718592 | tf_op jit(solution)/shard_map/all_gather | solution.py:410
  238.4 165.6 %all-gather.19.cloned.1.call-start = ((), (), s32[]{:S(2)}) async-start(), calls=%async_computation.16 | async-start | bytes 3932160 | tf_op jit(solution)/shard_map/all_gather | solution.py:433
  270.0 183.0 %all-gather.27.cloned.1.call-start = ((), (), s32[]{:S(2)}) async-start(), calls=%async_computation.25 | async-start | bytes 4718592 | tf_op jit(solution)/shard_map/all_gather | solution.py:410
  272.0 250.5 %reduce-scatter.11.cloned.1.call-start = ((), (), s32[]{:S(2)}) async-start(), calls=%async_computation.19 | async-start | bytes 4718592 | tf_op jit(solution)/shard_map/reduce_scatter | solution.py:414
  473.6 98.7 %all-gather.23.cloned.1.call-start = ((), (), s32[]{:S(2)}) async-start(), calls=%async_computation.20 | async-start | bytes 4718592 | tf_op jit(solution)/shard_map/all_gather | solution.py:410
  526.8 142.2 %reduce-scatter.17.cloned.1.call-start = ((), (), s32[]{:S(2)}) async-start(), calls=%async_computation.24 | async-start | bytes 11796480 | tf_op jit(solution)/shard_map/reduce_scatter | solution.py:437
  552.5 213.9 %reduce-scatter.13.cloned.1.call-start = ((), (), s32[]{:S(2)}) async-start(), calls=%async_computation.21 | async-start | bytes 4718592 | tf_op jit(solution)/shard_map/reduce_scatter | solution.py:414
  611.3 210.2 %reduce-scatter.9.cloned.1.call-start = ((), (), s32[]{:S(2)}) async-start(), calls=%async_computation.17 | async-start | bytes 4718592 | tf_op jit(solution)/shard_map/reduce_scatter | solution.py:414
  619.7 247.2 %reduce-scatter.15.cloned.1.call-start = ((), (), s32[]{:S(2)}) async-start(), calls=%async_computation.23 | async-start | bytes 3932160 | tf_op jit(solution)/shard_map/reduce_scatter | solution.py:437
  672.4 94.0 %copy-start.21 = (f32[2048]{0:T(1024)S(1)}, f32[2048]{0:T(1024)}, u32[]{:S(2)}) copy-start(f32[2048]{0:T(1024)} %copy-done.20) | copy-start | bytes 24580
  672.4 94.0 %copy-start.23 = (f32[128]{0:T(128)S(1)}, f32[128]{0:T(128)}, u32[]{:S(2)}) copy-start(f32[128]{0:T(128)} %copy-done.22) | copy-start | bytes 1540
  672.4 149.1 %copy-start.2 = (bf16[128,2048]{1,0:T(8,128)(2,1)S(1)}, bf16[128,2048]{1,0:T(8,128)(2,1)}, u32[]{:S(2)}) copy-start(bf16[128,2048]{1,0:T(8,128)(2,1)} %reduce-scatter.7.cloned.1.call-done) | copy-start | bytes 1572868
  672.4 149.1 %copy-start.5 = (bf16[128,2048]{1,0:T(8,128)(2,1)S(1)}, bf16[128,2048]{1,0:T(8,128)(2,1)}, u32[]{:S(2)}) copy-start(bf16[128,2048]{1,0:T(8,128)(2,1)} %reduce-scatter.11.cloned.1.call-done) | copy-start | bytes 1572868
  672.4 149.1 %copy-start.11 = (bf16[1,256,2048]{2,1,0:T(8,128)(2,1)S(1)}, bf16[1,256,2048]{2,1,0:T(8,128)(2,1)}, u32[]{:S(2)}) copy-start(bf16[1,256,2048]{2,1,0:T(8,128)(2,1)} %param.13) | copy-start | bytes 3145732
  672.5 196.6 %all-to-all-start.4 = ((bf16[4,128,2304]{1,2,0:T(8,128)(2,1)}), bf16[4,128,2304]{1,2,0:T(8,128)(2,1)}, u32[]{:S(2)}, u32[]{:S(2)}) async-start(bf16[4,128,2304]{1,2,0:T(8,128)(2,1)} %copy_bitcast_fusion), calls=%async_computation.10 | async-start | bytes 4718592 | tf_op jit(solution)/shard_map/all_to_all | solution.py:439
  677.2 257.4 %all-gather.21.cloned.1.call-start = ((), (), s32[]{:S(2)}) async-start(), calls=%async_computation.18 | async-start | bytes 1572864 | tf_op jit(solution)/shard_map/all_gather | solution.py:420
  824.7 109.9 %all-gather.25.cloned.1.call-start = ((), (), s32[]{:S(2)}) async-start(), calls=%async_computation.22 | async-start | bytes 3145728 | tf_op jit(solution)/shard_map/all_gather | solution.py:420
  869.1 24.5 %all-to-all-start.3 = ((bf16[4,128,768]{1,2,0:T(8,128)(2,1)}), bf16[4,128,768]{1,2,0:T(8,128)(2,1)S(1)}, u32[]{:S(2)}, u32[]{:S(2)}) async-start(bf16[4,128,768]{1,2,0:T(8,128)(2,1)} %copy_bitcast_fusion.1), calls=%async_computation.8 | async-start | bytes 1572864 | tf_op jit(solution)/shard_map/all_to_all | solution.py:439
  (32 other events, 171.9 us)
Sparse Core Ops, SparseCore 0:
  39.3 42.9 all-gather.12
  84.4 46.8 all-gather.10
  156.5 78.4 reduce-scatter.6
  237.3 72.7 all-gather.16
  312.1 46.8 all-gather.14
  361.3 42.6 all-gather.18
  406.1 46.8 all-gather.26
  473.7 48.7 reduce-scatter.10
  526.9 45.3 all-gather.22
  575.2 93.6 reduce-scatter.16
  671.2 95.1 reduce-scatter.12
  768.6 52.8 reduce-scatter.8
  824.5 42.3 reduce-scatter.14
  868.3 9.0 all-gather.20
  879.3 11.7 all-gather.24

commit v2 on v1

--- a/solution.py
+++ b/solution.py
@@ -1,8 +1,11 @@
+import functools
 import math
 
 import jax
 import jax.numpy as jnp
 from jax import lax
+from jax.experimental import pallas as pl
+from jax.experimental.pallas import tpu as pltpu
 from jax.sharding import PartitionSpec as P
 
 HEAD_DIM = 128
@@ -401,51 +404,768 @@
     )
 
 
+LINE_CHUNKS = 8
+LINE_LAG = 2
+LINE_START_TURNS = 6
+MESH = pl.DeviceIdType.MESH
+
+
+def line_copy(src, dst, send, recv, device):
+    return pltpu.make_async_remote_copy(
+        src_ref=src,
+        dst_ref=dst,
+        send_sem=send,
+        recv_sem=recv,
+        device_id=device,
+        device_id_type=MESH,
+    )
+
+
+def line_barrier(n, place, core, fetching):
+    barrier = pltpu.get_barrier_semaphore()
+
+    def greet(device):
+        pl.semaphore_signal(barrier, inc=1, device_id=device, device_id_type=MESH)
+
+    greet({"tensor": 1 - core})
+    if fetching:
+        group = lax.axis_index("fsdp")
+        greet({"fsdp": jnp.bitwise_xor(group, 1)})
+        greet({"fsdp": jnp.bitwise_xor(group, 2)})
+        for shift in range(1, n):
+            greet({"context": lax.rem(place + shift, n)})
+        pl.semaphore_wait(barrier, n + 2)
+        return
+
+    @pl.when(place > 0)
+    def _():
+        greet({"context": place - 1})
+
+    @pl.when(place < n - 1)
+    def _():
+        greet({"context": place + 1})
+
+    ends = jnp.where(place > 0, 1, 0) + jnp.where(place < n - 1, 1, 0)
+    pl.semaphore_wait(barrier, ends + 1)
+
+
+def fetch_steps(n, place, groups, weights, outs, sems, turns, start_turns):
+    own_send, line_send, line_recv, near_send, near_recv, far_send, far_recv = sems
+    group = lax.axis_index("fsdp")
+    rows = weights[0].shape[0]
+    neighbours = ({"fsdp": jnp.bitwise_xor(group, 1)}, {"fsdp": jnp.bitwise_xor(group, 2)})
+    spans = []
+    for g, members in enumerate(groups):
+        start = 0
+        for a in members:
+            width = weights[a].shape[1] // n
+            spans.append((a, g, start, width))
+            start += width
+
+    def block(out, of_group, at):
+        return out.at[pl.ds(pl.multiple_of((of_group * n + at) * rows, rows), rows)]
+
+    def held(s):
+        return lax.rem(place + n - s, n)
+
+    def columns(a, at, width):
+        return weights[a].at[:, pl.ds(pl.multiple_of(at * width, 128), width)]
+
+    def own_copy(a, g, start, width):
+        return pltpu.make_async_copy(
+            columns(a, place, width),
+            block(outs[g], group, place).at[:, pl.ds(start, width)],
+            own_send.at[a],
+        )
+
+    def line_move(a, g, start, width, s):
+        to = lax.rem(place + s, n)
+        return line_copy(
+            columns(a, to, width),
+            block(outs[g], group, place).at[:, pl.ds(start, width)],
+            line_send.at[a, s - 1],
+            line_recv.at[a, s - 1],
+            {"context": to},
+        )
+
+    def line_arrival(a, g, start, width, s):
+        return line_copy(
+            columns(a, place, width),
+            block(outs[g], group, held(s)).at[:, pl.ds(start, width)],
+            line_send.at[a, s - 1],
+            line_recv.at[a, s - 1],
+            {"context": held(s)},
+        )
+
+    def near_copy(way, g, s, of_group):
+        piece = block(outs[g], of_group, held(s))
+        return line_copy(
+            piece, piece, near_send.at[way, g, s], near_recv.at[way, g, s], neighbours[way]
+        )
+
+    def far_copy(g, s, of_group):
+        way = 1 if s < n // 2 else 0
+        piece = block(outs[g], of_group, held(s))
+        return line_copy(piece, piece, far_send.at[g, s], far_recv.at[g, s], neighbours[way])
+
+    def own_start():
+        for span in spans:
+            own_copy(*span).start()
+
+    def line_start(span, s):
+        return lambda: line_move(*span, s).start()
+
+    def spread(g, s):
+        def step():
+            for span in spans:
+                if span[1] == g:
+                    if s == 0:
+                        own_copy(*span).wait()
+                    else:
+                        line_arrival(*span, s).wait_recv()
+            near_copy(0, g, s, group).start()
+            near_copy(1, g, s, group).start()
+
+        return step
+
+    def pass_on(g, s):
+        came = 0 if s < n // 2 else 1
+        flip = 1 if came == 0 else 2
+
+        def step():
+            source = jnp.bitwise_xor(group, flip)
+            near_copy(came, g, s, source).wait_recv()
+            far_copy(g, s, source).start()
+
+        return step
+
+    def settle():
+        for g in range(len(groups)):
+            for s in range(n):
+                came = 0 if s < n // 2 else 1
+                rest = 1 - came
+                flip = 1 if rest == 0 else 2
+                near_copy(rest, g, s, jnp.bitwise_xor(group, flip)).wait_recv()
+                far_copy(g, s, jnp.bitwise_xor(group, 3)).wait_recv()
+                near_copy(0, g, s, group).wait_send()
+                near_copy(1, g, s, group).wait_send()
+                far_copy(g, s, group).wait_send()
+        for span in spans:
+            for s in range(1, n):
+                line_move(*span, s).wait_send()
+
+    issue = [(span, s) for s in range(1, n) for span in spans]
+    at_turn = {(span[0], s): i * start_turns // len(issue) for i, (span, s) in enumerate(issue)}
+    plan = [[] for _ in range(turns)]
+    for span, s in issue:
+        plan[at_turn[span[0], s]].append(line_start(span, s))
+    order = [(g, s) for s in range(n) for g in range(len(groups))]
+    moves = []
+    for i, (g, s) in enumerate(order):
+        ready = [at_turn[a, s] + 1 for a in groups[g]] if s else [0]
+        moves.append((max(ready), spread(g, s)))
+        if i >= 2:
+            moves.append((0, pass_on(*order[i - 2])))
+    moves += [(0, pass_on(*order[-2])), (0, pass_on(*order[-1]))]
+    turn = 0
+    for i, (ready, step) in enumerate(moves):
+        turn = min(max(turn, ready, i * turns // len(moves)), turns - 1)
+        plan[turn].append(step)
+    return own_start, plan, settle
+
+
+def piece_rows(count, body):
+    @pl.loop(0, count // 16)
+    def _(r):
+        body(pl.ds(pl.multiple_of(r * 16, 16), 16))
+
+
+def give_steps(n, place, groups, grads, outs, bufs, sems, turns):
+    first_send, first_recv, second_send, second_recv, line_send, line_recv = sems
+    group = lax.axis_index("fsdp")
+    rows = outs[0].shape[0]
+
+    def flips(s):
+        return (1, 2) if s < n // 2 else (2, 1)
+
+    def part(g, of_group, s):
+        block = of_group * n + lax.rem(place + s, n)
+        return grads[g].at[pl.ds(pl.multiple_of(block * rows, rows), rows)]
+
+    def first_copy(g, s, k):
+        one, two = flips(s)
+        target = jnp.bitwise_xor(group, one if k == 0 else 3)
+        return line_copy(
+            part(g, target, s),
+            bufs[g]["first"].at[s, k],
+            first_send.at[g, s, k],
+            first_recv.at[g, s, k],
+            {"fsdp": jnp.bitwise_xor(group, one)},
+        )
+
+    def second_copy(g, s):
+        return line_copy(
+            bufs[g]["second_out"].at[s],
+            bufs[g]["second"].at[s],
+            second_send.at[g, s],
+            second_recv.at[g, s],
+            {"fsdp": jnp.bitwise_xor(group, flips(s)[1])},
+        )
+
+    def line_move(g, s):
+        return line_copy(
+            bufs[g]["line_out"].at[s - 1],
+            bufs[g]["line"].at[s - 1],
+            line_send.at[g, s - 1],
+            line_recv.at[g, s - 1],
+            {"context": lax.rem(place + s, n)},
+        )
+
+    def store(g, quarter, at, values):
+        start = 0
+        for a in groups[g]:
+            width = outs[a].shape[1] // n
+            cols = pl.ds(pl.multiple_of(quarter * width, 128), width)
+            outs[a][at, cols] = values[:, start : start + width]
+            start += width
+
+    def begin():
+        for s in order_s:
+            for g in range(len(groups)):
+                first_copy(g, s, 1).start()
+                first_copy(g, s, 0).start()
+
+    def across(g, s):
+        def step():
+            first_copy(g, s, 1).wait_recv()
+            own = part(g, jnp.bitwise_xor(group, flips(s)[1]), s)
+            came = bufs[g]["first"].at[s, 1]
+            out = bufs[g]["second_out"].at[s]
+
+            def add(at):
+                out[at, :] = (
+                    own[at, :].astype(jnp.float32) + came[at, :].astype(jnp.float32)
+                ).astype(jnp.bfloat16)
+
+            piece_rows(rows, add)
+            second_copy(g, s).start()
+
+        return step
+
+    def total(g, s):
+        def step():
+            first_copy(g, s, 0).wait_recv()
+            second_copy(g, s).wait_recv()
+            own = part(g, group, s)
+            one = bufs[g]["first"].at[s, 0]
+            two = bufs[g]["second"].at[s]
+
+            def add(at):
+                value = own[at, :].astype(jnp.float32)
+                value = value + one[at, :].astype(jnp.float32) + two[at, :].astype(jnp.float32)
+                if s == 0:
+                    store(g, place, at, value)
+                else:
+                    bufs[g]["line_out"][s - 1, at, :] = value.astype(jnp.bfloat16)
+
+            piece_rows(rows, add)
+            if s:
+                line_move(g, s).start()
+
+        return step
+
+    def arrive(g, s):
+        def step():
+            line_move(g, s).wait_recv()
+            quarter = lax.rem(place + n - s, n)
+
+            def widen(at):
+                store(g, quarter, at, bufs[g]["line"][s - 1, at, :].astype(jnp.float32))
+
+            piece_rows(rows, widen)
+
+        return step
+
+    def settle():
+        for g in range(len(groups)):
+            for s in range(n):
+                first_copy(g, s, 0).wait_send()
+                first_copy(g, s, 1).wait_send()
+                second_copy(g, s).wait_send()
+                if s:
+                    line_move(g, s).wait_send()
+
+    order_s = list(range(1, n)) + [0]
+    order = [(g, s) for s in order_s for g in range(len(groups))]
+    steps = []
+    for i in range(len(order) + 4):
+        if i < len(order):
+            steps.append(across(*order[i]))
+        if 0 <= i - 1 < len(order):
+            steps.append(total(*order[i - 1]))
+        if 0 <= i - 4 < len(order) and order[i - 4][1]:
+            steps.append(arrive(*order[i - 4]))
+    plan = [[] for _ in range(turns)]
+    for i, step in enumerate(steps):
+        plan[1 + i * (turns - 1) // len(steps)].append(step)
+    return begin, plan, settle
+
+
+def line_body(n, chunks, n_part, gather, n_in, n_join, n_rest, groups, giving, extra, finish, *refs):
+    refs = list(refs)
+    take = lambda count: [refs.pop(0) for _ in range(count)]
+    reduce = n_part > 0
+    fetching = bool(groups) and not giving
+    arrays = sum(len(members) for members in groups)
+    parts = take(n_part)
+    ins = take(n_in)
+    weights = take(arrays) if fetching else []
+    grads = take(len(groups)) if giving else []
+    others = take(1)[0] if extra else None
+    gathered = take(1)[0] if gather else None
+    joined = take(n_join)
+    rest = take(n_rest)
+    fetched = take(len(groups)) if fetching else []
+    given = take(arrays) if giving else []
+    gains_out = take(1)[0] if extra else None
+    if reduce:
+        across, sums_in, sums_out, summed = take(4)
+        cross_send, cross_recv, sum_send, sum_recv = take(4)
+    if gather:
+        row_send, row_recv, pair_send, pair_recv = take(4)
+    if n_join:
+        join_send, join_recv = take(2)
+    fetch_sems = take(7) if fetching else None
+    if giving:
+        names = ("first", "second_out", "second", "line_out", "line")
+        give_bufs = [dict(zip(names, take(5))) for _ in groups]
+        give_sems = take(6)
+    if extra:
+        gain_own, gain_came, gain_line, gain_send, gain_recv, gain_line_send, gain_line_recv = take(7)
+
+    place = lax.axis_index("context")
+    core = lax.axis_index("tensor")
+    other = {"tensor": 1 - core}
+    step_rows = (ins[0].shape[0]) // chunks
+
+    def rows(j):
+        return pl.ds(j * step_rows, step_rows)
+
+    line_barrier(n, place, core, bool(groups))
+    lag = LINE_LAG if reduce else 0
+    turns = chunks * max(n_part, 1) + lag + n
+    plan = [[] for _ in range(turns)]
+    if fetching:
+        start_turns = min(LINE_START_TURNS, chunks) if reduce else 1
+        own_start, plan, settle = fetch_steps(
+            n, place, groups, weights, fetched, fetch_sems, turns, start_turns
+        )
+    if fetching:
+        own_start()
+    if giving:
+        begin, plan, settle = give_steps(
+            n, place, groups, grads, given, give_bufs, give_sems, turns
+        )
+        begin()
+
+    def cross(j):
+        return line_copy(
+            parts[j // chunks].at[:, 1 - core, rows(j % chunks)],
+            across.at[:, rows(j)],
+            cross_send.at[j],
+            cross_recv.at[j],
+            other,
+        )
+
+    def sum_copy(way, k, j):
+        return line_copy(
+            sums_out.at[way, k, rows(j)],
+            sums_in.at[way, k, rows(j)],
+            sum_send.at[way, k, j],
+            sum_recv.at[way, k, j],
+            {"context": place + 1 - 2 * way},
+        )
+
+    def own_term(target, j):
+        return parts[j // chunks][target, core, rows(j % chunks), :].astype(jnp.float32) + across[
+            target, rows(j), :
+        ].astype(jnp.float32)
+
+    def send_sums(way, j):
+        first = place == (n - 1) * way
+        for k in range(n - 1):
+            target = jnp.where(way == 0, n - 1 - k, k)
+            passes = jnp.where(way == 0, target - place, place - target) > 0
+
+            @pl.when(passes & first)
+            def _(k=k, target=target):
+                sums_out[way, k, rows(j), :] = own_term(target, j).astype(jnp.bfloat16)
+                sum_copy(way, k, j).start()
+
+            @pl.when(passes & jnp.logical_not(first))
+            def _(k=k, target=target):
+                sum_copy(way, k, j).wait_recv()
+                sums_out[way, k, rows(j), :] = (
+                    own_term(target, j) + sums_in[way, k, rows(j), :].astype(jnp.float32)
+                ).astype(jnp.bfloat16)
+                sum_copy(way, k, j).start()
+
+    def row_copy(way, k, j):
+        block = place - k if way == 0 else place + k
+        device = {"context": place + 1 if way == 0 else place - 1}
+        ref = gathered.at[block, core, rows(j)]
+        return line_copy(ref, ref, row_send.at[way, k, j], row_recv.at[way, k, j], device)
+
+    def row_arrival(way, k, j):
+        block = place - 1 - k if way == 0 else place + 1 + k
+        ref = gathered.at[block, core, rows(j)]
+        return line_copy(
+            ref, ref, row_send.at[way, k, j], row_recv.at[way, k, j], other
+        )
+
+    def pair_copy(block, half, j):
+        ref = gathered.at[block, half, rows(j)]
+        return line_copy(ref, ref, pair_send.at[block, j], pair_recv.at[block, j], other)
+
+    def finish_rows(j):
+        total = None
+        if reduce:
+
+            summed[...] = own_term(place, j)
+
+            @pl.when(place > 0)
+            def _():
+                sum_copy(0, n - 1 - place, j).wait_recv()
+                summed[...] += sums_in[0, n - 1 - place, rows(j), :].astype(jnp.float32)
+
+            @pl.when(place < n - 1)
+            def _():
+                sum_copy(1, place, j).wait_recv()
+                summed[...] += sums_in[1, place, rows(j), :].astype(jnp.float32)
+
+            total = summed[...]
+        made = finish(j, rows(j % chunks), total, ins, rest)
+        made = made if isinstance(made, tuple) else (made,)
+        made = list(made)
+        if gather:
+            gathered[place, core, rows(j), :] = made.pop(0)
+
+            @pl.when(place < n - 1)
+            def _():
+                row_copy(0, 0, j).start()
+
+            @pl.when(place > 0)
+            def _():
+                row_copy(1, 0, j).start()
+
+            pair_copy(place, core, j).start()
+        if n_join:
+            i = j // chunks
+            joined[i][core, rows(j % chunks), :] = made.pop(0)
+            join_copy(i, core, j % chunks).start()
+
+    def join_copy(i, half, j):
+        ref = joined[i].at[half, rows(j)]
+        return line_copy(ref, ref, join_send.at[i, j], join_recv.at[i, j], other)
+
+    def pass_rows(k, j):
+        for way in (0, 1):
+            block = place - 1 - k if way == 0 else place + 1 + k
+            here = block >= 0 if way == 0 else block <= n - 1
+            onward = place < n - 1 if way == 0 else place > 0
+
+            @pl.when(here)
+            def _(way=way, block=block):
+                row_arrival(way, k, j).wait_recv()
+
+            if k + 1 <= n - 2:
+
+                @pl.when(here & onward)
+                def _(way=way):
+                    row_copy(way, k + 1, j).start()
+
+            @pl.when(here)
+            def _(way=way, block=block):
+                pair_copy(block, core, j).start()
+
+    all_chunks = chunks * max(n_part, 1)
+    if reduce:
+        for j in range(all_chunks):
+            cross(j).start()
+    def gains_plan():
+        group = lax.axis_index("fsdp")
+        hops = (
+            other,
+            {"fsdp": jnp.bitwise_xor(group, 1)},
+            {"fsdp": jnp.bitwise_xor(group, 2)},
+        )
+
+        def hop(h):
+            return line_copy(
+                gain_own.at[h], gain_came.at[h], gain_send.at[h], gain_recv.at[h], hops[h]
+            )
+
+        def line_hop(s):
+            return line_copy(
+                gain_line.at[place],
+                gain_line.at[place],
+                gain_line_send.at[s - 1],
+                gain_line_recv.at[s - 1],
+                {"context": lax.rem(place + s, n)},
+            )
+
+        def line_hop_in(s):
+            ref = gain_line.at[lax.rem(place + n - s, n)]
+            return line_copy(
+                ref, ref, gain_line_send.at[s - 1], gain_line_recv.at[s - 1], other
+            )
+
+        def first():
+            gain_own[0] = others[...]
+            gain_own[0, 0:1, :] = rest[0][...]
+            hop(0).start()
+
+        def next_hop(h):
+            def step():
+                hop(h).wait_recv()
+                value = gain_own[h] + gain_came[h]
+                if h < 2:
+                    gain_own[h + 1] = value
+                    hop(h + 1).start()
+                else:
+                    gain_line[place] = value
+                    for s in range(1, n):
+                        line_hop(s).start()
+
+            return step
+
+        def last():
+            for s in range(1, n):
+                line_hop_in(s).wait_recv()
+            value = gain_line[0]
+            for p in range(1, n):
+                value = value + gain_line[p]
+            gains_out[...] = value
+            for h in range(3):
+                hop(h).wait_send()
+            for s in range(1, n):
+                line_hop(s).wait_send()
+
+        return [first, next_hop(0), next_hop(1), next_hop(2), last]
+
+    near = jnp.where(place < n // 2, 0, 1)
+    gain_steps = gains_plan() if extra else []
+    for i in range(turns):
+        for step in plan[i]:
+            step()
+        if reduce and i < all_chunks:
+            cross(i).wait_recv()
+            send_sums(near, i)
+        if reduce and 0 <= i - 1 < all_chunks:
+            send_sums(1 - near, i - 1)
+        if 0 <= i - lag < all_chunks:
+            finish_rows(i - lag)
+        if extra and i - lag >= chunks and gain_steps:
+            gain_steps.pop(0)()
+        if gather:
+            for k in range(n - 1):
+                if 0 <= i - lag - 1 - k < chunks:
+                    pass_rows(k, i - lag - 1 - k)
+
+    for step in gain_steps:
+        step()
+    if groups:
+        settle()
+    for j in range(all_chunks):
+        if reduce:
+            cross(j).wait_send()
+            for k in range(n - 1):
+
+                @pl.when(place < n - 1 - k)
+                def _(k=k, j=j):
+                    sum_copy(0, k, j).wait_send()
+
+                @pl.when(place > k)
+                def _(k=k, j=j):
+                    sum_copy(1, k, j).wait_send()
+
+        if gather:
+            for block in range(n):
+                pair_copy(block, 1 - core, j).wait_recv()
+                pair_copy(block, core, j).wait_send()
+            for k in range(n - 1):
+
+                @pl.when((place < n - 1) & (place >= k))
+                def _(k=k, j=j):
+                    row_copy(0, k, j).wait_send()
+
+                @pl.when((place > 0) & (place + k <= n - 1))
+                def _(k=k, j=j):
+                    row_copy(1, k, j).wait_send()
+
+        if n_join:
+            join_copy(j // chunks, 1 - core, j % chunks).wait_recv()
+            join_copy(j // chunks, core, j % chunks).wait_send()
+
+
+def line_call(
+    n,
+    collective,
+    finish,
+    part,
+    ins,
+    gather=False,
+    joins=(),
+    rests=(),
+    chunks=LINE_CHUNKS,
+    groups=(),
+    weights=(),
+    grads=(),
+    extra=None,
+):
+    parts = () if part is None else part if isinstance(part, tuple) else (part,)
+    reduce = len(parts) > 0
+    giving = len(grads) > 0
+    row_count, model_width = ins[0].shape
+    vmem = pl.BlockSpec(memory_space=pltpu.VMEM)
+    outs = []
+    if gather:
+        outs.append(jax.ShapeDtypeStruct((n, 2, row_count, model_width), jnp.bfloat16))
+    outs += [jax.ShapeDtypeStruct((2, row_count, model_width), kind) for kind in joins]
+    outs += list(rests)
+    out_specs = [vmem] * len(outs)
+    for members in groups if not giving else ():
+        rows = weights[0].shape[0] * n * lax.axis_size("fsdp")
+        width = sum(weights[a].shape[1] for a in members) // n
+        outs.append(jax.ShapeDtypeStruct((rows, width), jnp.bfloat16))
+        out_specs.append(pl.BlockSpec(memory_space=pl.ANY))
+    dma = pltpu.SemaphoreType.DMA
+    if giving:
+        owned = grads[0].shape[0] // (n * lax.axis_size("fsdp"))
+        for width in weights:
+            outs.append(jax.ShapeDtypeStruct((owned, width * n), jnp.float32))
+            out_specs.append(vmem)
+    if extra is not None:
+        outs.append(jax.ShapeDtypeStruct(extra.shape, jnp.float32))
+        out_specs.append(vmem)
+    total_chunks = chunks * max(len(parts), 1)
+    sum_rows = row_count * max(len(parts), 1)
+    scratch = []
+    if reduce:
+        slot = pltpu.VMEM((2, n - 1, sum_rows, model_width), jnp.bfloat16)
+        scratch += [pltpu.VMEM((n, sum_rows, model_width), jnp.bfloat16), slot, slot]
+        scratch += [pltpu.VMEM((row_count // chunks, model_width), jnp.float32)]
+        tally = (2, n - 1, total_chunks)
+        scratch += [dma((total_chunks,)), dma((total_chunks,)), dma(tally), dma(tally)]
+    if gather:
+        scratch += [dma((2, n - 1, chunks)), dma((2, n - 1, chunks)), dma((n, chunks)), dma((n, chunks))]
+    if joins:
+        scratch += [dma((len(joins), chunks)), dma((len(joins), chunks))]
+    if groups and not giving:
+        arrays = len(weights)
+        pieces = (2, len(groups), n)
+        scratch += [dma((arrays,)), dma((arrays, n - 1)), dma((arrays, n - 1))]
+        scratch += [dma(pieces), dma(pieces), dma(pieces[1:]), dma(pieces[1:])]
+    if giving:
+        for grad in grads:
+            piece = (owned, grad.shape[1])
+            for lead in ((n, 2), (n,), (n,), (n - 1,), (n - 1,)):
+                scratch.append(pltpu.VMEM(lead + piece, jnp.bfloat16))
+        count = len(groups)
+        scratch += [dma((count, n, 2)), dma((count, n, 2)), dma((count, n)), dma((count, n))]
+        scratch += [dma((count, n - 1)), dma((count, n - 1))]
+    if extra is not None:
+        stack = pltpu.VMEM((3,) + extra.shape, jnp.float32)
+        scratch += [stack, stack, pltpu.VMEM((n,) + extra.shape, jnp.float32)]
+        scratch += [dma((3,)), dma((3,)), dma((n - 1,)), dma((n - 1,))]
+    operands = list(parts) + list(ins) + (list(grads) if giving else list(weights))
+    operands += [] if extra is None else [extra]
+    moved = row_count * model_width * 2 * n * (2 * reduce + 2 * gather)
+    return pl.pallas_call(
+        functools.partial(
+            line_body,
+            n,
+            chunks,
+            len(parts),
+            gather,
+            len(ins),
+            len(joins),
+            len(rests),
+            groups,
+            giving,
+            extra is not None,
+            finish,
+        ),
+        out_shape=tuple(outs),
+        in_specs=[vmem] * len(operands),
+        out_specs=tuple(out_specs),
+        scratch_shapes=scratch,
+        compiler_params=pltpu.CompilerParams(
+            collective_id=collective, has_side_effects=True, vmem_limit_bytes=56 << 20
+        ),
+        cost_estimate=pl.CostEstimate(
+            flops=moved, bytes_accessed=20 * moved, transcendentals=0
+        ),
+        name="line_%d" % collective,
+    )(*operands)
+
+
+def finish_gather(j, rows, total, ins, rest):
+    values = ins[0][rows, :].astype(jnp.float32)
+    return (values * rms_scale(values) * ins[1][...]).astype(jnp.bfloat16)
+
+
+def finish_attention(j, rows, total, ins, rest):
+    residual = ins[0][rows, :].astype(jnp.float32) + total
+    rest[0][rows, :] = residual
+    return (residual * rms_scale(residual) * ins[1][...]).astype(jnp.bfloat16)
+
+
+def gain_rows(j, rest, terms):
+    sums = jnp.sum(terms, axis=0, keepdims=True)
+    rest[...] = sums if j == 0 else rest[...] + sums
+
+
+def finish_mlp_back(j, rows, total, ins, rest):
+    residual = ins[0][rows, :]
+    scale = rms_scale(residual)
+    hat = residual * scale
+    grad = ins[1][rows, :].astype(jnp.float32) + norm_back(total, hat, scale, ins[2][...])
+    rest[0][rows, :] = grad
+    gain_rows(j, rest[1], total * hat)
+    return grad.astype(jnp.bfloat16)
+
+
+def finish_ends(j, rows, total, ins, rest):
+    if j >= LINE_CHUNKS:
+        return (ins[3][rows, :] + total).astype(jnp.bfloat16)
+    values = ins[1][rows, :].astype(jnp.float32)
+    scale = rms_scale(values)
+    hat = values * scale
+    gain_rows(j, rest[0], total * hat)
+    return ins[0][rows, :] + norm_back(total, hat, scale, ins[2][...])
+
+
+def permuted_tokens(rows):
+    n = lax.axis_size("context")
+    place = lax.axis_index("context")
+    core = lax.axis_index("tensor")
+    shape = rows.shape
+    near = jnp.zeros((n,) + shape, rows.dtype)
+    for s in range(n):
+        ring = [(i, (i + s) % n) for i in range(n)]
+        came = lax.ppermute(rows, "context", ring) if s else rows
+        near = lax.dynamic_update_slice(near, came[None], (lax.rem(place + n - s, n), 0, 0))
+    far = lax.ppermute(near, "tensor", [(0, 1), (1, 0)])
+    both = jnp.zeros((n, 2) + shape, rows.dtype)
+    both = lax.dynamic_update_slice(both, near[:, None], (0, core, 0, 0))
+    both = lax.dynamic_update_slice(both, far[:, None], (0, 1 - core, 0, 0))
+    return both.reshape(n * 2 * shape[0], shape[1])
+
+
 def token_half(block, index, parts):
     rows = block.shape[0] // parts
     return lax.dynamic_slice_in_dim(block, index * rows, rows, axis=0)
-
-
-def gather_tokens(rows):
-    return lax.all_gather(rows, ("context", "tensor"), axis=0, tiled=True)
-
-
-def scatter_tokens(partial_sum):
-    return lax.psum_scatter(
-        partial_sum.astype(jnp.bfloat16), ("context", "tensor"), scatter_dimension=0, tiled=True
-    ).astype(jnp.float32)
-
-
-def join_cores(rows):
-    return lax.all_gather(rows, "tensor", axis=0, tiled=True)
-
-
-def column_parts(weights, parts):
-    return jnp.concatenate(
-        [w.reshape(w.shape[0], parts, w.shape[1] // parts) for w in weights], axis=2
-    )
-
-
-def fetch_columns(weights, parts):
-    pieces = column_parts(weights, parts)
-    rows, _, width = pieces.shape
-    lined = lax.all_to_all(pieces, "context", split_axis=1, concat_axis=0, tiled=True)
-    return lax.all_gather(lined.reshape(parts * rows, width), "fsdp", axis=0, tiled=True)
-
-
-def return_columns(grads, parts, widths):
-    own = lax.psum_scatter(grads, "fsdp", scatter_dimension=0, tiled=True)
-    rows = own.shape[0] // parts
-    back = lax.all_to_all(
-        own.reshape(parts, rows, own.shape[1]), "context", split_axis=0, concat_axis=0, tiled=True
-    )
-    outs = []
-    start = 0
-    for width in widths:
-        piece = back[:, :, start : start + width].astype(jnp.float32)
-        outs.append(piece.transpose(1, 0, 2).reshape(rows, parts * width))
-        start += width
-    return outs
 
 
 def line_shards(
@@ -479,23 +1199,32 @@
     cosine_table = cosine_table[:, None, :]
     sine_table = sine_table[:, None, :]
     visible = positions[None, :] <= positions[:, None]
-    gain_attn = norm_gain_attn.astype(jnp.float32)
-    gain_mlp = norm_gain_mlp.astype(jnp.float32)
+    gain_attn = norm_gain_attn.astype(jnp.float32)[None]
+    gain_mlp = norm_gain_mlp.astype(jnp.float32)[None]
     gain_heads = head_gains.astype(jnp.float32)
 
+    def line_parts(left, right):
+        product = column_product(left, right).astype(jnp.bfloat16)
+        return product.reshape(parts, cores, half_len, model_width)
+
     own_cot = token_half(cotangent.reshape(local_len, model_width), core, cores)
-    inputs = token_half(tokens.reshape(local_len, model_width), core, cores).astype(jnp.float32)
-    scale_attn = rms_scale(inputs)
-    hat_attn = inputs * scale_attn
-    normed_attn = gather_tokens((hat_attn * gain_attn).astype(jnp.bfloat16))
-    attn_weights = fetch_columns((query_weight, key_matrix, value_matrix, output_weight), parts)
-    grad_out = gather_tokens(own_cot)
-    mlp_in = fetch_columns((gate_weight, up_weight), parts)
-    mlp_down = fetch_columns((down_weight,), parts)
-
-    qkv_cols = q_cols + 2 * kv_cols
-    in_weights = attn_weights[:, :qkv_cols]
-    out_weights = attn_weights[:, qkv_cols:]
+    inputs = token_half(tokens.reshape(local_len, model_width), core, cores)
+    half_len = local_len // cores
+    rows_f32 = jax.ShapeDtypeStruct((half_len, model_width), jnp.float32)
+    sums_f32 = jax.ShapeDtypeStruct((1, model_width), jnp.float32)
+    normed_attn, in_weights, out_weights = line_call(
+        parts,
+        1,
+        finish_gather,
+        None,
+        (inputs, gain_attn),
+        gather=True,
+        groups=((0, 1, 2), (3,)),
+        weights=(query_weight, key_matrix, value_matrix, output_weight),
+    )
+    normed_attn = normed_attn.reshape(full_len, model_width)
+    grad_out = permuted_tokens(own_cot)
+
     raw = jnp.dot(normed_attn, in_weights, preferred_element_type=jnp.float32)
     query_split = raw[:, :q_cols].reshape(full_len, q_heads, HEAD_DIM)
     query_scale = rms_scale(query_split)
@@ -520,10 +1249,18 @@
         .astype(jnp.bfloat16)
         .reshape(full_len, q_cols)
     )
-    residual = inputs + scatter_tokens(column_product(attended, out_weights))
-    scale_mlp = rms_scale(residual)
-    hat_mlp = residual * scale_mlp
-    normed_mlp = gather_tokens((hat_mlp * gain_mlp).astype(jnp.bfloat16))
+    normed_mlp, residual, mlp_in, mlp_down = line_call(
+        parts,
+        2,
+        finish_attention,
+        line_parts(attended, out_weights),
+        (inputs, gain_mlp),
+        gather=True,
+        rests=(rows_f32,),
+        groups=((0, 1), (2,)),
+        weights=(gate_weight, up_weight, down_weight),
+    )
+    normed_mlp = normed_mlp.reshape(full_len, model_width)
 
     both = jnp.dot(normed_mlp, mlp_in, preferred_element_type=jnp.float32)
     gate_act = both[:, :h_cols]
@@ -536,22 +1273,21 @@
     grad_gate = (grad_hidden * upward * derivative).astype(jnp.bfloat16)
     grad_up = (grad_hidden * activated).astype(jnp.bfloat16)
     grad_both = jnp.concatenate([grad_gate, grad_up], axis=1)
-    grad_normed_mlp = scatter_tokens(column_product(grad_both, mlp_in))
-    result = residual + scatter_tokens(column_product(hidden, mlp_down))
-    mlp_terms = jnp.concatenate(
-        [
-            row_product(normed_mlp, grad_both).astype(jnp.bfloat16),
-            row_product(grad_out, hidden).astype(jnp.bfloat16),
-        ],
-        axis=1,
-    )
-    gate_grad, up_grad, down_grad = return_columns(mlp_terms, parts, (h_cols, h_cols, h_cols))
-
-    gain_mlp_part = jnp.sum(grad_normed_mlp * hat_mlp, axis=0)
-    grad_residual = own_cot.astype(jnp.float32) + norm_back(
-        grad_normed_mlp, hat_mlp, scale_mlp, gain_mlp
-    )
-    grad_branch = gather_tokens(grad_residual.astype(jnp.bfloat16))
+    grad_in = row_product(normed_mlp, grad_both).astype(jnp.bfloat16)
+    grad_down = row_product(grad_out, hidden).astype(jnp.bfloat16)
+    grad_branch, grad_residual, gain_mlp_part, gate_grad, up_grad, down_grad = line_call(
+        parts,
+        3,
+        finish_mlp_back,
+        line_parts(grad_both, mlp_in),
+        (residual, own_cot, gain_mlp),
+        gather=True,
+        rests=(rows_f32, sums_f32),
+        groups=((0, 1), (2,)),
+        weights=(h_cols, h_cols, h_cols),
+        grads=(grad_in, grad_down),
+    )
+    grad_branch = grad_branch.reshape(full_len, model_width)
     grad_attended = (
         jnp.dot(grad_branch, out_weights, preferred_element_type=jnp.float32)
         .astype(jnp.bfloat16)
@@ -591,28 +1327,36 @@
         ],
         axis=1,
     ).astype(jnp.bfloat16)
-    grad_normed_attn = scatter_tokens(column_product(grad_raw, in_weights))
-    attn_terms = jnp.concatenate(
+    attn_in_grad = row_product(normed_attn, grad_raw).astype(jnp.bfloat16)
+    attn_out_grad = row_product(grad_branch, attended).astype(jnp.bfloat16)
+    gains = jnp.concatenate(
         [
-            row_product(normed_attn, grad_raw).astype(jnp.bfloat16),
-            row_product(grad_branch, attended).astype(jnp.bfloat16),
+            jnp.zeros((1, model_width), jnp.float32),
+            gain_mlp_part,
+            jnp.pad(heads_part.reshape(1, -1), ((0, 0), (0, model_width - heads_part.size))),
+            jnp.zeros((5, model_width), jnp.float32),
         ],
-        axis=1,
-    )
-    query_grad, key_grad, value_grad, output_grad = return_columns(
-        attn_terms, parts, (q_cols, kv_cols, kv_cols, q_cols)
-    )
-    gain_attn_part = jnp.sum(grad_normed_attn * hat_attn, axis=0)
-    grad_tokens = grad_residual + norm_back(grad_normed_attn, hat_attn, scale_attn, gain_attn)
-    total_attn, total_mlp, total_heads = lax.psum(
-        (gain_attn_part, gain_mlp_part, heads_part), ("fsdp", "context", "tensor")
+        axis=0,
+    )
+    grad_tokens, out, _, query_grad, key_grad, value_grad, output_grad, totals = line_call(
+        parts,
+        4,
+        finish_ends,
+        (line_parts(grad_raw, in_weights), line_parts(hidden, mlp_down)),
+        (grad_residual, inputs, gain_attn, residual),
+        joins=(jnp.float32, jnp.bfloat16),
+        rests=(sums_f32,),
+        groups=((0, 1, 2), (3,)),
+        weights=(q_cols, kv_cols, kv_cols, q_cols),
+        grads=(attn_in_grad, attn_out_grad),
+        extra=gains,
     )
     return (
-        join_cores(result.astype(jnp.bfloat16)).reshape(tokens.shape),
-        join_cores(grad_tokens).reshape(tokens.shape),
-        total_attn,
-        total_mlp,
-        total_heads,
+        out.reshape(tokens.shape),
+        grad_tokens.reshape(tokens.shape),
+        totals[0],
+        totals[1],
+        totals[2, : heads_part.size].reshape(heads_part.shape),
         query_grad,
         key_grad,
         value_grad,
@@ -631,7 +1375,9 @@
         tokens.shape[0] == 1
         and key_matrix.shape[1] % (parts * HEAD_DIM) == 0
         and gate_weight.shape[1] % (parts * HEAD_DIM) == 0
-        and tokens.shape[1] % (cores * 16) == 0
+        and tokens.shape[1] % (cores * LINE_CHUNKS * 16) == 0
+        and cores == 2
+        and lax.axis_size("fsdp") == 4
     )
     return line_shards(*operands) if fits else shards(*operands)
 

time: 956 us -> 695 us (0.73)
  waiting for transfers between devices: 560 us -> 0.01 us
  Pallas kernels: 0 us -> 538 us
  blocking collectives: 157 us -> 0 us
  other arithmetic: 49.2 us -> 15.1 us
  local copies, waits for them, and re-layouts: 54.1 us -> 33 us
  between operations: 15 us -> 1.69 us
    pallas_call x0 -> x4, Pallas kernels: none -> 538 us  [line_call(): pl.pallas_call(functools.partial(line_body, n, chunks, len(parts), gather...]
    reduce_scatter x6 -> x0, waiting for transfers between devices: 276 us -> none  [the longest x4 194 us: scatter_tokens(): lax.psum_scatter(partial_sum.astype(jnp.bfloat16), ('context', 'tensor'),...]
    all_gather x9 -> x0, waiting for transfers between devices: 275 us -> none  [the longest x4 166 us: gather_tokens(): return lax.all_gather(rows, ('context', 'tensor'), axis=0, tiled=True)]
    all_to_all x3 -> x0, blocking collectives: 120 us -> none  [fetch_columns(): lax.all_to_all(pieces, 'context', split_axis=1, concat_axis=0, tiled=True)]
    psum x1 -> x0, blocking collectives: 37.3 us -> none  [line_shards(): lax.psum((gain_attn_part, gain_mlp_part, heads_part), ('fsdp', 'context',...]
    unnamed x94 -> x89, local copies, waits for them, and re-layouts: 34.3 us -> 13 us
    concatenate x4 -> x1, other arithmetic: 14.8 us -> 0.71 us  [line_shards(): jnp.concatenate([jnp.zeros((1, model_width), jnp.float32), gain_mlp_part,...]
  transfers between devices with their start and end apart: 17 -> 4, of which waited for: 14 -> 0; matrix products, arithmetic and copies ran while one was open for 15% -> 6% of each run, Pallas kernels for 0% -> 34%
where the time goes in v2:
time: 695 us; the launch traced here: 688 us
  Pallas kernels  538 us (77%)
  matrix products  93 us (13%)
  local copies, waits for them, and re-layouts  33 us (5%)
  other arithmetic  15.1 us (2%)
  starting transfers between devices  6.99 us (1%)
    pallas_call x4, Pallas kernels, line_call(): pl.pallas_call(functools.partial(line_body, n, chunks, len(parts), gather...  538 us
    dot_general x4, matrix products, row_product(): lax.dot_general(left, right, (((0,), (0,)), ((), ())), preferred_element_...  22.8 us
    dot_general x4, matrix products, column_product(): lax.dot_general(left, right, (((1,), (1,)), ((), ())), preferred_element_...  21.8 us
  transfers between devices with their start and end apart: 4, of which 0 were waited for; matrix products, arithmetic and copies ran while one was open for 6% of the time, Pallas kernels for 34%

profile of v2, /device:TPU:0, one launch (start us, length us, event | category | flops | bytes accessed | tf_op | source)
XLA Modules:
  0.0 688.2 jit_solution(14615112396922889724)
XLA Ops:
  4.4 3.1 collective-permute-start
  7.4 2.6 collective-permute-start.1
  12.8 103.2 %line_1.1 = (bf16[4,2,128,2048]{3,2,1,0:T(8,128)(2,1)}, bf16[2048,512]{1,0:T(8,128)(2,1)}, bf16[2048,256]{1,0:T(8,128)(2,1)}) custom-call(bf16[128,2048]{1,0:T(8,128)(2,1)} %dynamic-slice_bitcast_fusion.refs_0_.refs_1_.refs_3_, f32[1,2048]{1,0:T(1,128)} %bitcast.212, bf16[128,1024]{1,0:T(8,128)(2,1)} %refs_2_.1, bf16[128,512]{1,0:T(8,128)(2,1)} %refs_3_.2, ...), custom_call_target="tpu_custom_call" | custom-call | flops 4194304 | bytes 83886080 | tf_op jit(solution)/shard_map/line_1/pallas_call | solution.py:1084
  116.1 5.2 fusion.65
  129.7 2.6 fusion.4
  132.4 2.8 fusion.13
  135.7 3.3 convolution_convert_fusion.3
  139.7 133.4 %line_2.1 = (bf16[4,2,128,2048]{3,2,1,0:T(8,128)(2,1)}, f32[128,2048]{1,0:T(8,128)}, bf16[2048,1536]{1,0:T(8,128)(2,1)}, bf16[2048,768]{1,0:T(8,128)(2,1)}) custom-call(bf16[4,2,128,2048]{3,2,1,0:T(8,128)(2,1)} %bitcast.197, bf16[128,2048]{1,0:T(8,128)(2,1)} %dynamic-slice_bitcast_fusion.refs_0_.refs_1_.refs_3_, f32[1,2048]{1,0:T(1,128)} %bitcast.210, ...), custom_call_target="tpu_custom_call" | custom-call | flops 8388608 | bytes 167772160 | tf_op jit(solution)/shard_map/line_2/pallas_call | solution.py:1084
  278.8 11.7 %fusion.66 = f32[1024,1536]{0,1:T(8,128)} fusion(bf16[1024,2048]{1,0:T(8,128)(2,1)} %bitcast.224, bf16[2048,1536]{1,0:T(8,128)(2,1)} %get-tuple-element.37), kind=kOutput, calls=%fused_computation.124 | convolution fusion | flops 6442450944 | bytes 16777216 | tf_op jit(solution)/shard_map/dot_general | solution.py:1265
  293.2 9.0 %multiply_convert_fusion.2 = (bf16[1024,768]{0,1:T(8,128)(2,1)}, bf16[1024,768]{0,1:T(8,128)(2,1)}, bf16[1024,768]{0,1:T(8,128)(2,1)S(1)}) fusion(f32[1024,1536]{0,1:T(8,128)} %fusion.66, bf16[1024,2048]{1,0:T(8,128)(2,1)S(1)} %bitcast.203, bf16[2048,768]{1,0:T(8,128)(2,1)} %get-tuple-element.35), kind=kOutput, calls=%fused_computation.24 | convolution fusion | flops 3233021952 | bytes 18350080 | tf_op jit(solution)/shard_map/dot_general | solution.py:1271
  302.2 10.7 %convolution_convert_fusion.refs_4_ = bf16[2048,1536]{1,0:T(8,128)(2,1)} fusion(bf16[1024,2048]{1,0:T(8,128)(2,1)S(1)} %bitcast.225, bf16[1024,768]{0,1:T(8,128)(2,1)} %get-tuple-element.57, bf16[1024,768]{0,1:T(8,128)(2,1)} %get-tuple-element.56), kind=kOutput, calls=%fused_computation.6 | convolution fusion | flops 6451888128 | bytes 13631488 | tf_op jit(solution)/shard_map/dot_general | solution.py:63
  312.9 8.7 %convolution_convert_fusion.1 = bf16[1024,2048]{1,0:T(8,128)(2,1)} fusion(bf16[2048,1536]{1,0:T(8,128)(2,1)S(1)} %bitcast.221, bf16[1024,768]{0,1:T(8,128)(2,1)S(1)} %copy-done.35, bf16[1024,768]{0,1:T(8,128)(2,1)S(1)} %copy-done.34), kind=kOutput, calls=%fused_computation.15 | convolution fusion | flops 6450839552 | bytes 13631488 | tf_op jit(solution)/shard_map/dot_general | solution.py:69
  321.6 4.9 convolution_convert_fusion.5.refs_5_
  326.5 181.6 %line_3.1 = (bf16[4,2,128,2048]{3,2,1,0:T(8,128)(2,1)}, f32[128,2048]{1,0:T(8,128)}, f32[1,2048]{1,0:T(1,128)}, f32[128,3072]{1,0:T(8,128)}, f32[128,3072]{1,0:T(8,128)}, /*index=5*/f32[128,3072]{1,0:T(8,128)}) custom-call(bf16[4,2,128,2048]{3,2,1,0:T(8,128)(2,1)} %bitcast.202, f32[128,2048]{1,0:T(8,128)} %get-tuple-element.38.refs_1_.refs_5_, ...), custom_call_target="tpu_custom_call" | custom-call | flops 8388608 | bytes 167772160 | tf_op jit(solution)/shard_map/line_3/pallas_call | solution.py:1084
  508.2 3.6 convolution_convert_fusion.8
  511.8 5.6 fusion
  517.7 2.7 fusion.5
  522.3 2.7 fusion.20
  524.9 3.4 fusion.24
  530.7 5.3 convolution_convert_fusion.4
  542.6 4.8 convolution_convert_fusion.6.refs_6_
  547.5 4.4 convolution_convert_fusion.2
  552.6 120.1 %line_4.1 = (f32[2,128,2048]{2,1,0:T(8,128)}, bf16[2,128,2048]{2,1,0:T(8,128)(2,1)}, f32[1,2048]{1,0:T(1,128)}, f32[128,1024]{1,0:T(8,128)}, f32[128,512]{1,0:T(...) custom-call(bf16[4,2,128,2048]{3,2,1,0:T(8,128)(2,1)} %bitcast.201, ...), custom_call_target="tpu_custom_call" | custom-call | flops 4194304 | bytes 83886080 | tf_op jit(solution)/shard_map/line_4/pallas_call | solution.py:1084
  678.1 3.3 copy.97
  (143 shorter events, 47.7 us)
Async XLA Ops:
  0.6 10.7 %copy-start = (bf16[1,256,2048]{2,1,0:T(8,128)(2,1)S(1)}, bf16[1,256,2048]{2,1,0:T(8,128)(2,1)}, u32[]{:S(2)}) copy-start(bf16[1,256,2048]{2,1,0:T(8,128)(2,1)} %param.12) | copy-start | bytes 3145732
  0.7 11.6 %copy-start.25 = (bf16[2048]{0:T(1024)(128)(2,1)S(1)}, bf16[2048]{0:T(1024)(128)(2,1)}, u32[]{:S(2)}) copy-start(bf16[2048]{0:T(1024)(128)(2,1)} %param.14) | copy-start | bytes 12292
  4.4 268.7 %collective-permute-start = (bf16[128,2048]{1,0:T(8,128)(2,1)}, bf16[128,2048]{1,0:T(8,128)(2,1)}, u32[]{:S(2)}, u32[]{:S(2)}) collective-permute-start(bf16[128,2048]{1,0:T(8,128)(2,1)} %get-tuple-element.65.refs_2_), channel_id=1, source_target_pairs={{0,2},{2,4},{4,6},{6,0},{1,3},{3,5},{5,7},{7,1},{8,10},{10,12},{12... | collective-permute-start | bytes 1572872 | tf_op jit(solution)/shard_map/ppermute | solution.py:1157
  7.4 267.6 %collective-permute-start.1 = (bf16[128,2048]{1,0:T(8,128)(2,1)}, bf16[128,2048]{1,0:T(8,128)(2,1)}, u32[]{:S(2)}, u32[]{:S(2)}) collective-permute-start(bf16[128,2048]{1,0:T(8,128)(2,1)} %get-tuple-element.65.refs_2_), channel_id=1, source_target_pairs={{0,4},{2,6},{4,0},{6,2},{1,5},{3,7},{5,1},{7,3},{8,12},{10,14},{12... | collective-permute-start | bytes 1572872 | tf_op jit(solution)/shard_map/ppermute | solution.py:1157
  10.0 266.9 %collective-permute-start.2 = (bf16[128,2048]{1,0:T(8,128)(2,1)}, bf16[128,2048]{1,0:T(8,128)(2,1)}, u32[]{:S(2)}, u32[]{:S(2)}) collective-permute-start(bf16[128,2048]{1,0:T(8,128)(2,1)} %get-tuple-element.65.refs_2_), channel_id=1, source_target_pairs={{0,6},{2,0},{4,2},{6,4},{1,7},{3,1},{5,3},{7,5},{8,14},{10,8},{12,... | collective-permute-start | bytes 1572872 | tf_op jit(solution)/shard_map/ppermute | solution.py:1157
  278.8 14.1 %collective-permute-start.3 = (bf16[4,128,2048]{2,1,0:T(8,128)(2,1)}, bf16[4,128,2048]{2,1,0:T(8,128)(2,1)S(1)}, u32[]{:S(2)}, u32[]{:S(2)}) collective-permute-start(bf16[4,128,2048]{2,1,0:T(8,128)(2,1)} %bitcast_dynamic-update-slice_fusion.2), channel_id=1, source_target_pairs={{0,1},{1,0},{2,3},{3,2},{4,5},{5,4},{6,7},{7,6},{8,9},{9,8},{10,11... | collective-permute-start | bytes 6291464 | tf_op jit(solution)/shard_map/ppermute | solution.py:1159
  292.9 20.0 %slice-start.2 = ((s8[6291456]{0:T(1024)(128)(4,1)}), s8[4194304]{0:T(1024)(128)(4,1)S(1)}, s32[]{:S(2)}) async-start(s8[6291456]{0:T(1024)(128)(4,1)} %bitcast.220), calls=%async_computation.2 | async-start | bytes 8388608
  293.2 9.0 %copy-start.28 = (bf16[4,2,128,2048]{3,2,1,0:T(8,128)(2,1)S(1)}, bf16[4,2,128,2048]{3,2,1,0:T(8,128)(2,1)}, u32[]{:S(2)}) copy-start(bf16[4,2,128,2048]{3,2,1,0:T(8,128)(2,1)} %get-tuple-element.36) | copy-start | bytes 12582916
  293.2 19.7 %slice-start.3 = ((s8[6291456]{0:T(1024)(128)(4,1)}), s8[2097152]{0:T(1024)(128)(4,1)S(1)}, s32[]{:S(2)}) async-start(s8[6291456]{0:T(1024)(128)(4,1)} %bitcast.220), calls=%async_computation.3 | async-start | bytes 4194304
  302.2 10.7 %copy-start.34 = (bf16[1024,768]{0,1:T(8,128)(2,1)S(1)}, bf16[1024,768]{0,1:T(8,128)(2,1)}, u32[]{:S(2)}) copy-start(bf16[1024,768]{0,1:T(8,128)(2,1)} %get-tuple-element.56) | copy-start | bytes 4718596
  302.2 10.7 %copy-start.35 = (bf16[1024,768]{0,1:T(8,128)(2,1)S(1)}, bf16[1024,768]{0,1:T(8,128)(2,1)}, u32[]{:S(2)}) copy-start(bf16[1024,768]{0,1:T(8,128)(2,1)} %get-tuple-element.57) | copy-start | bytes 4718596
  326.5 181.7 %copy-start.19 = (bf16[2048,256]{1,0:T(8,128)(2,1)S(1)}, bf16[2048,256]{1,0:T(8,128)(2,1)}, u32[]{:S(2)}) copy-start(bf16[2048,256]{1,0:T(8,128)(2,1)} %get-tuple-element.34) | copy-start | bytes 3145732
  511.8 5.6 slice-start
  511.8 5.9 slice-start.1
  530.7 5.3 copy-start.4
  530.7 5.3 copy-start.6
  542.6 4.9 copy-start.31
  542.6 4.8 copy-start.33
  672.7 8.6 %copy-start.21 = (f32[128,1024]{1,0:T(8,128)S(1)}, f32[128,1024]{1,0:T(8,128)}, u32[]{:S(2)}) copy-start(f32[128,1024]{1,0:T(8,128)} %get-tuple-element.98) | copy-start | bytes 1572868
  672.7 9.4 %copy-start.23 = (f32[128,512]{1,0:T(8,128)S(1)}, f32[128,512]{1,0:T(8,128)}, u32[]{:S(2)}) copy-start(f32[128,512]{1,0:T(8,128)} %get-tuple-element.99) | copy-start | bytes 786436
  672.8 10.1 %copy-start.22 = (f32[128,512]{1,0:T(8,128)S(1)}, f32[128,512]{1,0:T(8,128)}, u32[]{:S(2)}) copy-start(f32[128,512]{1,0:T(8,128)} %get-tuple-element.100) | copy-start | bytes 786436
  675.6 7.9 %copy-start.20 = (f32[128,1024]{1,0:T(8,128)S(1)}, f32[128,1024]{1,0:T(8,128)}, u32[]{:S(2)}) copy-start(f32[128,1024]{1,0:T(8,128)} %get-tuple-element.101) | copy-start | bytes 1572868
  675.6 8.7 %copy-start.17 = (f32[128,3072]{1,0:T(8,128)S(1)}, f32[128,3072]{1,0:T(8,128)}, u32[]{:S(2)}) copy-start(f32[128,3072]{1,0:T(8,128)} %get-tuple-element.102) | copy-start | bytes 4718596
  678.0 7.4 %copy-start.16 = (f32[128,3072]{1,0:T(8,128)S(1)}, f32[128,3072]{1,0:T(8,128)}, u32[]{:S(2)}) copy-start(f32[128,3072]{1,0:T(8,128)} %get-tuple-element.103) | copy-start | bytes 4718596
  (20 other events, 62.3 us)

commit v3 on v2

--- a/solution.py
+++ b/solution.py
@@ -7,6 +7,7 @@
 from jax.experimental import pallas as pl
 from jax.experimental.pallas import tpu as pltpu
 from jax.sharding import PartitionSpec as P
+
 
 HEAD_DIM = 128
 
@@ -314,7 +315,7 @@
         )
         return (grad_query, grad_key, grad_value, delta[..., 0])
 
-    grad_query_all, grad_key_all, grad_value_all, delta_all = lax.map(
+    grad_query_all, grad_key_all, grad_value_all, _ = lax.map(
         attend_back, (query_blocks, key_blocks, value_blocks, grad_blocks, log_totals)
     )
     grad_key_full = grad_key_all.transpose(1, 2, 0, 3).reshape(seq_count, full_len, kv_cols)
@@ -406,7 +407,9 @@
 
 LINE_CHUNKS = 8
 LINE_LAG = 2
-LINE_START_TURNS = 6
+LINE_START_TURNS = 1
+LINE_FROM_TURN = 1
+LINE_GIVE_TURN = 6
 MESH = pl.DeviceIdType.MESH
 
 
@@ -449,7 +452,16 @@
     pl.semaphore_wait(barrier, ends + 1)
 
 
-def fetch_steps(n, place, groups, weights, outs, sems, turns, start_turns):
+def nearest(n):
+    return [sorted(range(n), key=lambda q: (abs(q - p), q)) for p in range(n)]
+
+
+def ranked(n, place):
+    table = nearest(n)
+    return [sum(jnp.where(place == p, table[p][k], 0) for p in range(n)) for k in range(n)]
+
+
+def fetch_steps(n, place, groups, weights, outs, sems, turns, start_turns, from_turn):
     own_send, line_send, line_recv, near_send, near_recv, far_send, far_recv = sems
     group = lax.axis_index("fsdp")
     rows = weights[0].shape[0]
@@ -465,8 +477,7 @@
     def block(out, of_group, at):
         return out.at[pl.ds(pl.multiple_of((of_group * n + at) * rows, rows), rows)]
 
-    def held(s):
-        return lax.rem(place + n - s, n)
+    order = ranked(n, place)
 
     def columns(a, at, width):
         return weights[a].at[:, pl.ds(pl.multiple_of(at * width, 128), width)]
@@ -479,34 +490,35 @@
         )
 
     def line_move(a, g, start, width, s):
-        to = lax.rem(place + s, n)
         return line_copy(
-            columns(a, to, width),
+            columns(a, order[s], width),
             block(outs[g], group, place).at[:, pl.ds(start, width)],
-            line_send.at[a, s - 1],
-            line_recv.at[a, s - 1],
-            {"context": to},
+            line_send.at[a, s],
+            line_recv.at[a, place],
+            {"context": order[s]},
         )
 
     def line_arrival(a, g, start, width, s):
         return line_copy(
             columns(a, place, width),
-            block(outs[g], group, held(s)).at[:, pl.ds(start, width)],
-            line_send.at[a, s - 1],
-            line_recv.at[a, s - 1],
-            {"context": held(s)},
+            block(outs[g], group, order[s]).at[:, pl.ds(start, width)],
+            line_send.at[a, s],
+            line_recv.at[a, order[s]],
+            {"context": order[s]},
         )
 
     def near_copy(way, g, s, of_group):
-        piece = block(outs[g], of_group, held(s))
+        piece = block(outs[g], of_group, order[s])
         return line_copy(
             piece, piece, near_send.at[way, g, s], near_recv.at[way, g, s], neighbours[way]
         )
 
-    def far_copy(g, s, of_group):
-        way = 1 if s < n // 2 else 0
-        piece = block(outs[g], of_group, held(s))
-        return line_copy(piece, piece, far_send.at[g, s], far_recv.at[g, s], neighbours[way])
+    def far_copy(half, g, s, of_group):
+        start = (of_group * n + order[s]) * rows + half * (rows // 2)
+        piece = outs[g].at[pl.ds(pl.multiple_of(start, rows // 2), rows // 2)]
+        return line_copy(
+            piece, piece, far_send.at[half, g, s], far_recv.at[half, g, s], neighbours[1 - half]
+        )
 
     def own_start():
         for span in spans:
@@ -529,27 +541,21 @@
         return step
 
     def pass_on(g, s):
-        came = 0 if s < n // 2 else 1
-        flip = 1 if came == 0 else 2
-
         def step():
-            source = jnp.bitwise_xor(group, flip)
-            near_copy(came, g, s, source).wait_recv()
-            far_copy(g, s, source).start()
+            for half in (0, 1):
+                source = jnp.bitwise_xor(group, half + 1)
+                near_copy(half, g, s, source).wait_recv()
+                far_copy(half, g, s, source).start()
 
         return step
 
     def settle():
         for g in range(len(groups)):
             for s in range(n):
-                came = 0 if s < n // 2 else 1
-                rest = 1 - came
-                flip = 1 if rest == 0 else 2
-                near_copy(rest, g, s, jnp.bitwise_xor(group, flip)).wait_recv()
-                far_copy(g, s, jnp.bitwise_xor(group, 3)).wait_recv()
-                near_copy(0, g, s, group).wait_send()
-                near_copy(1, g, s, group).wait_send()
-                far_copy(g, s, group).wait_send()
+                for half in (0, 1):
+                    far_copy(half, g, s, jnp.bitwise_xor(group, 3)).wait_recv()
+                    far_copy(half, g, s, group).wait_send()
+                    near_copy(half, g, s, group).wait_send()
         for span in spans:
             for s in range(1, n):
                 line_move(*span, s).wait_send()
@@ -559,17 +565,19 @@
     plan = [[] for _ in range(turns)]
     for span, s in issue:
         plan[at_turn[span[0], s]].append(line_start(span, s))
-    order = [(g, s) for s in range(n) for g in range(len(groups))]
+    table = nearest(n)
     moves = []
-    for i, (g, s) in enumerate(order):
-        ready = [at_turn[a, s] + 1 for a in groups[g]] if s else [0]
-        moves.append((max(ready), spread(g, s)))
-        if i >= 2:
-            moves.append((0, pass_on(*order[i - 2])))
-    moves += [(0, pass_on(*order[-2])), (0, pass_on(*order[-1]))]
+    for s in range(n):
+        latest = max(table[table[p][s]].index(p) for p in range(n))
+        for g in range(len(groups)):
+            ready = max(at_turn[a, latest] for a in groups[g]) + 1 if s else 0
+            moves.append((ready, spread(g, s)))
+        moves += [(0, pass_on(g, s)) for g in range(len(groups))]
     turn = 0
     for i, (ready, step) in enumerate(moves):
-        turn = min(max(turn, ready, i * turns // len(moves)), turns - 1)
+        late = max(0, i - len(groups))
+        even = from_turn + late * (turns - from_turn) // (len(moves) - len(groups)) if late else 0
+        turn = min(max(turn, ready, even), turns - 1)
         plan[turn].append(step)
     return own_start, plan, settle
 
@@ -580,138 +588,151 @@
         body(pl.ds(pl.multiple_of(r * 16, 16), 16))
 
 
-def give_steps(n, place, groups, grads, outs, bufs, sems, turns):
+def give_steps(n, place, groups, grads, outs, bufs, sems, turns, from_turn, deliver):
     first_send, first_recv, second_send, second_recv, line_send, line_recv = sems
     group = lax.axis_index("fsdp")
-    rows = outs[0].shape[0]
-
-    def flips(s):
-        return (1, 2) if s < n // 2 else (2, 1)
-
-    def part(g, of_group, s):
-        block = of_group * n + lax.rem(place + s, n)
-        return grads[g].at[pl.ds(pl.multiple_of(block * rows, rows), rows)]
-
-    def first_copy(g, s, k):
-        one, two = flips(s)
-        target = jnp.bitwise_xor(group, one if k == 0 else 3)
+    rows = outs[0].shape[-2]
+
+    half_rows = rows // 2
+
+    far = ranked(n, place)[::-1]
+
+    def part(g, of_group, s, half):
+        block = of_group * n + far[s]
+        start = pl.multiple_of(block * rows + half * half_rows, half_rows)
+        return grads[g].at[pl.ds(start, half_rows)]
+
+    def first_copy(g, s, half, k):
+        target = jnp.bitwise_xor(group, half + 1 if k == 0 else 3)
         return line_copy(
-            part(g, target, s),
-            bufs[g]["first"].at[s, k],
-            first_send.at[g, s, k],
-            first_recv.at[g, s, k],
-            {"fsdp": jnp.bitwise_xor(group, one)},
-        )
-
-    def second_copy(g, s):
+            part(g, target, s, half),
+            bufs[g]["first"].at[s, half, k],
+            first_send.at[g, s, half, k],
+            first_recv.at[g, s, half, k],
+            {"fsdp": jnp.bitwise_xor(group, half + 1)},
+        )
+
+    def second_copy(g, s, half):
         return line_copy(
-            bufs[g]["second_out"].at[s],
-            bufs[g]["second"].at[s],
-            second_send.at[g, s],
-            second_recv.at[g, s],
-            {"fsdp": jnp.bitwise_xor(group, flips(s)[1])},
-        )
-
-    def line_move(g, s):
-        return line_copy(
-            bufs[g]["line_out"].at[s - 1],
-            bufs[g]["line"].at[s - 1],
-            line_send.at[g, s - 1],
-            line_recv.at[g, s - 1],
-            {"context": lax.rem(place + s, n)},
-        )
-
-    def store(g, quarter, at, values):
+            bufs[g]["second_out"].at[s, half],
+            bufs[g]["second"].at[s, half],
+            second_send.at[g, s, half],
+            second_recv.at[g, s, half],
+            {"fsdp": jnp.bitwise_xor(group, 2 - half)},
+        )
+
+    def line_moves(g, s, arrival=False):
         start = 0
         for a in groups[g]:
             width = outs[a].shape[1] // n
-            cols = pl.ds(pl.multiple_of(quarter * width, 128), width)
-            outs[a][at, cols] = values[:, start : start + width]
+            quarter = far[s] if arrival else place
+            ref = outs[a].at[:, pl.ds(pl.multiple_of(quarter * width, 128), width)]
+            out = bufs[g]["line_out"].at[min(s, n - 2), :, pl.ds(start, width)]
+            yield line_copy(
+                ref if arrival else out,
+                ref,
+                line_send.at[a, s],
+                line_recv.at[a, quarter],
+                {"context": far[s]},
+            )
             start += width
 
+    def store(g, at, values):
+        start = 0
+        for a in groups[g]:
+            width = outs[a].shape[1] // n
+            cols = pl.ds(pl.multiple_of(place * width, 128), width)
+            outs[a][at, cols] = values[:, start : start + width].astype(jnp.bfloat16)
+            start += width
+
+    def send_first(g, s):
+        for k in (1, 0):
+            for half in (0, 1):
+                first_copy(g, s, half, k).start()
+
     def begin():
-        for s in order_s:
-            for g in range(len(groups)):
-                first_copy(g, s, 1).start()
-                first_copy(g, s, 0).start()
-
-    def across(g, s):
+        for i in range(2 * len(groups)):
+            g, s = order[i]
+            send_first(g, s)
+
+    def across(i):
+        g, s = order[i]
+
         def step():
-            first_copy(g, s, 1).wait_recv()
-            own = part(g, jnp.bitwise_xor(group, flips(s)[1]), s)
-            came = bufs[g]["first"].at[s, 1]
-            out = bufs[g]["second_out"].at[s]
-
-            def add(at):
-                out[at, :] = (
-                    own[at, :].astype(jnp.float32) + came[at, :].astype(jnp.float32)
-                ).astype(jnp.bfloat16)
-
-            piece_rows(rows, add)
-            second_copy(g, s).start()
+            for half in (0, 1):
+                first_copy(g, s, half, 1).wait_recv()
+                own = part(g, jnp.bitwise_xor(group, 2 - half), s, half)
+                came = bufs[g]["first"].at[s, half, 1]
+                out = bufs[g]["second_out"].at[s, half]
+
+                def add(at, own=own, came=came, out=out):
+                    out[at, :] = (
+                        own[at, :].astype(jnp.float32) + came[at, :].astype(jnp.float32)
+                    ).astype(jnp.bfloat16)
+
+                piece_rows(half_rows, add)
+                second_copy(g, s, half).start()
+            if i + 2 * len(groups) < len(order):
+                send_first(*order[i + 2 * len(groups)])
 
         return step
 
     def total(g, s):
         def step():
-            first_copy(g, s, 0).wait_recv()
-            second_copy(g, s).wait_recv()
-            own = part(g, group, s)
-            one = bufs[g]["first"].at[s, 0]
-            two = bufs[g]["second"].at[s]
-
-            def add(at):
-                value = own[at, :].astype(jnp.float32)
-                value = value + one[at, :].astype(jnp.float32) + two[at, :].astype(jnp.float32)
-                if s == 0:
-                    store(g, place, at, value)
-                else:
-                    bufs[g]["line_out"][s - 1, at, :] = value.astype(jnp.bfloat16)
-
-            piece_rows(rows, add)
-            if s:
-                line_move(g, s).start()
+            for half in (0, 1):
+                first_copy(g, s, half, 0).wait_recv()
+                second_copy(g, s, half).wait_recv()
+                own = part(g, group, s, half)
+                one = bufs[g]["first"].at[s, half, 0]
+                two = bufs[g]["second"].at[s, half]
+
+                def add(at, own=own, one=one, two=two, half=half):
+                    value = own[at, :].astype(jnp.float32) + one[at, :].astype(jnp.float32)
+                    value = value + two[at, :].astype(jnp.float32)
+                    to = pl.ds(pl.multiple_of(at.start + half * half_rows, 16), 16)
+                    if not deliver:
+                        width = value.shape[1]
+                        start = sum(grads[h].shape[1] for h in range(g))
+                        outs[0][far[s], to, start : start + width] = value.astype(jnp.bfloat16)
+                    elif s == n - 1:
+                        store(g, to, value)
+                    else:
+                        bufs[g]["line_out"][s, to, :] = value.astype(jnp.bfloat16)
+
+                piece_rows(half_rows, add)
+            if deliver and s < n - 1:
+                for move in line_moves(g, s):
+                    move.start()
 
         return step
 
-    def arrive(g, s):
-        def step():
-            line_move(g, s).wait_recv()
-            quarter = lax.rem(place + n - s, n)
-
-            def widen(at):
-                store(g, quarter, at, bufs[g]["line"][s - 1, at, :].astype(jnp.float32))
-
-            piece_rows(rows, widen)
-
-        return step
-
     def settle():
-        for g in range(len(groups)):
-            for s in range(n):
-                first_copy(g, s, 0).wait_send()
-                first_copy(g, s, 1).wait_send()
-                second_copy(g, s).wait_send()
-                if s:
-                    line_move(g, s).wait_send()
-
-    order_s = list(range(1, n)) + [0]
-    order = [(g, s) for s in order_s for g in range(len(groups))]
+        for g, s in order:
+            for half in (0, 1):
+                first_copy(g, s, half, 0).wait_send()
+                first_copy(g, s, half, 1).wait_send()
+                second_copy(g, s, half).wait_send()
+            if deliver and s < n - 1:
+                for move in line_moves(g, s):
+                    move.wait_send()
+                for move in line_moves(g, s, arrival=True):
+                    move.wait_recv()
+
+    count = len(groups)
+    order = [(g, s) for s in range(n) for g in range(count)]
     steps = []
-    for i in range(len(order) + 4):
+    for i in range(len(order) + count):
         if i < len(order):
-            steps.append(across(*order[i]))
-        if 0 <= i - 1 < len(order):
-            steps.append(total(*order[i - 1]))
-        if 0 <= i - 4 < len(order) and order[i - 4][1]:
-            steps.append(arrive(*order[i - 4]))
+            steps.append(across(i))
+        if 0 <= i - count < len(order):
+            steps.append(total(*order[i - count]))
     plan = [[] for _ in range(turns)]
     for i, step in enumerate(steps):
-        plan[1 + i * (turns - 1) // len(steps)].append(step)
+        plan[from_turn + i * (turns - from_turn) // len(steps)].append(step)
     return begin, plan, settle
 
 
-def line_body(n, chunks, n_part, gather, n_in, n_join, n_rest, groups, giving, extra, finish, *refs):
+def line_body(n, chunks, n_part, gather, n_in, n_join, n_rest, groups, giving, deliver, extra, finish, *refs):
     refs = list(refs)
     take = lambda count: [refs.pop(0) for _ in range(count)]
     reduce = n_part > 0
@@ -726,7 +747,7 @@
     joined = take(n_join)
     rest = take(n_rest)
     fetched = take(len(groups)) if fetching else []
-    given = take(arrays) if giving else []
+    given = take(arrays if deliver else 1) if giving else []
     gains_out = take(1)[0] if extra else None
     if reduce:
         across, sums_in, sums_out, summed = take(4)
@@ -737,8 +758,8 @@
         join_send, join_recv = take(2)
     fetch_sems = take(7) if fetching else None
     if giving:
-        names = ("first", "second_out", "second", "line_out", "line")
-        give_bufs = [dict(zip(names, take(5))) for _ in groups]
+        names = ("first", "second_out", "second", "line_out")[: 4 if deliver else 3]
+        give_bufs = [dict(zip(names, take(len(names)))) for _ in groups]
         give_sems = take(6)
     if extra:
         gain_own, gain_came, gain_line, gain_send, gain_recv, gain_line_send, gain_line_recv = take(7)
@@ -757,14 +778,15 @@
     plan = [[] for _ in range(turns)]
     if fetching:
         start_turns = min(LINE_START_TURNS, chunks) if reduce else 1
+        from_turn = LINE_FROM_TURN if reduce else 1
         own_start, plan, settle = fetch_steps(
-            n, place, groups, weights, fetched, fetch_sems, turns, start_turns
+            n, place, groups, weights, fetched, fetch_sems, turns, start_turns, from_turn
         )
     if fetching:
         own_start()
     if giving:
         begin, plan, settle = give_steps(
-            n, place, groups, grads, given, give_bufs, give_sems, turns
+            n, place, groups, grads, given, give_bufs, give_sems, turns, LINE_GIVE_TURN, deliver
         )
         begin()
 
@@ -847,7 +869,7 @@
         made = finish(j, rows(j % chunks), total, ins, rest)
         made = made if isinstance(made, tuple) else (made,)
         made = list(made)
-        if gather:
+        if gather and j < chunks:
             gathered[place, core, rows(j), :] = made.pop(0)
 
             @pl.when(place < n - 1)
@@ -859,8 +881,8 @@
                 row_copy(1, 0, j).start()
 
             pair_copy(place, core, j).start()
-        if n_join:
-            i = j // chunks
+        if made:
+            i = j // chunks - gather
             joined[i][core, rows(j % chunks), :] = made.pop(0)
             join_copy(i, core, j % chunks).start()
 
@@ -892,6 +914,7 @@
     if reduce:
         for j in range(all_chunks):
             cross(j).start()
+
     def gains_plan():
         group = lax.axis_index("fsdp")
         hops = (
@@ -989,7 +1012,7 @@
                 def _(k=k, j=j):
                     sum_copy(1, k, j).wait_send()
 
-        if gather:
+        if gather and j < chunks:
             for block in range(n):
                 pair_copy(block, 1 - core, j).wait_recv()
                 pair_copy(block, core, j).wait_send()
@@ -1003,9 +1026,9 @@
                 def _(k=k, j=j):
                     row_copy(1, k, j).wait_send()
 
-        if n_join:
-            join_copy(j // chunks, 1 - core, j % chunks).wait_recv()
-            join_copy(j // chunks, core, j % chunks).wait_send()
+        if n_join and j // chunks >= gather:
+            join_copy(j // chunks - gather, 1 - core, j % chunks).wait_recv()
+            join_copy(j // chunks - gather, core, j % chunks).wait_send()
 
 
 def line_call(
@@ -1021,6 +1044,7 @@
     groups=(),
     weights=(),
     grads=(),
+    deliver=True,
     extra=None,
 ):
     parts = () if part is None else part if isinstance(part, tuple) else (part,)
@@ -1042,8 +1066,11 @@
     dma = pltpu.SemaphoreType.DMA
     if giving:
         owned = grads[0].shape[0] // (n * lax.axis_size("fsdp"))
-        for width in weights:
-            outs.append(jax.ShapeDtypeStruct((owned, width * n), jnp.float32))
+        shapes = [(owned, width * n) for width in weights]
+        if not deliver:
+            shapes = [(n, owned, sum(grad.shape[1] for grad in grads))]
+        for shape in shapes:
+            outs.append(jax.ShapeDtypeStruct(shape, jnp.bfloat16))
             out_specs.append(vmem)
     if extra is not None:
         outs.append(jax.ShapeDtypeStruct(extra.shape, jnp.float32))
@@ -1064,16 +1091,19 @@
     if groups and not giving:
         arrays = len(weights)
         pieces = (2, len(groups), n)
-        scratch += [dma((arrays,)), dma((arrays, n - 1)), dma((arrays, n - 1))]
-        scratch += [dma(pieces), dma(pieces), dma(pieces[1:]), dma(pieces[1:])]
+        scratch += [dma((arrays,)), dma((arrays, n)), dma((arrays, n))]
+        scratch += [dma(pieces), dma(pieces), dma(pieces), dma(pieces)]
     if giving:
         for grad in grads:
-            piece = (owned, grad.shape[1])
-            for lead in ((n, 2), (n,), (n,), (n - 1,), (n - 1,)):
-                scratch.append(pltpu.VMEM(lead + piece, jnp.bfloat16))
+            halves = (owned // 2, grad.shape[1])
+            for lead in ((n, 2, 2), (n, 2), (n, 2)):
+                scratch.append(pltpu.VMEM(lead + halves, jnp.bfloat16))
+            if deliver:
+                scratch.append(pltpu.VMEM((n - 1, owned, grad.shape[1]), jnp.bfloat16))
         count = len(groups)
-        scratch += [dma((count, n, 2)), dma((count, n, 2)), dma((count, n)), dma((count, n))]
-        scratch += [dma((count, n - 1)), dma((count, n - 1))]
+        scratch += [dma((count, n, 2, 2)), dma((count, n, 2, 2))]
+        scratch += [dma((count, n, 2)), dma((count, n, 2))]
+        scratch += [dma((len(weights), n)), dma((len(weights), n))]
     if extra is not None:
         stack = pltpu.VMEM((3,) + extra.shape, jnp.float32)
         scratch += [stack, stack, pltpu.VMEM((n,) + extra.shape, jnp.float32)]
@@ -1093,6 +1123,7 @@
             len(rests),
             groups,
             giving,
+            deliver,
             extra is not None,
             finish,
         ),
@@ -1106,7 +1137,6 @@
         cost_estimate=pl.CostEstimate(
             flops=moved, bytes_accessed=20 * moved, transcendentals=0
         ),
-        name="line_%d" % collective,
     )(*operands)
 
 
@@ -1128,6 +1158,8 @@
 
 def finish_mlp_back(j, rows, total, ins, rest):
     residual = ins[0][rows, :]
+    if j >= LINE_CHUNKS:
+        return (residual + total).astype(jnp.bfloat16)
     scale = rms_scale(residual)
     hat = residual * scale
     grad = ins[1][rows, :].astype(jnp.float32) + norm_back(total, hat, scale, ins[2][...])
@@ -1136,9 +1168,7 @@
     return grad.astype(jnp.bfloat16)
 
 
-def finish_ends(j, rows, total, ins, rest):
-    if j >= LINE_CHUNKS:
-        return (ins[3][rows, :] + total).astype(jnp.bfloat16)
+def finish_tokens(j, rows, total, ins, rest):
     values = ins[1][rows, :].astype(jnp.float32)
     scale = rms_scale(values)
     hat = values * scale
@@ -1163,6 +1193,37 @@
     return both.reshape(n * 2 * shape[0], shape[1])
 
 
+def widen_body(h_cols, out, tokens, mlp, *refs):
+    attn, results = refs[:4], refs[4:]
+    results[0][...] = out[...]
+    results[1][...] = tokens[...]
+    for a in range(4):
+        results[2 + a][...] = attn[a][...].astype(jnp.float32)
+    for a in range(3):
+        results[6 + a][...] = mlp[0, :, a * h_cols : (a + 1) * h_cols].astype(jnp.float32)
+
+
+def widen(parts, h_cols, out, tokens, mlp, *attn):
+    rows = mlp.shape[1]
+    width = out.shape[-1]
+    out, tokens = out.reshape(-1, width), tokens.reshape(-1, width)
+    token_rows = pl.BlockSpec((out.shape[0] // parts, width), lambda i: (i, 0))
+    quarters = [pl.BlockSpec((rows, a.shape[1] // parts), lambda i: (0, i)) for a in attn]
+    hidden = pl.BlockSpec((rows, h_cols), lambda i: (0, i))
+    results = [jax.ShapeDtypeStruct(a.shape, a.dtype) for a in (out, tokens)]
+    results += [jax.ShapeDtypeStruct(a.shape, jnp.float32) for a in attn]
+    results += [jax.ShapeDtypeStruct((rows, h_cols * parts), jnp.float32)] * 3
+    return pl.pallas_call(
+        functools.partial(widen_body, h_cols),
+        grid=(parts,),
+        in_specs=[token_rows, token_rows, pl.BlockSpec((1,) + mlp.shape[1:], lambda i: (i, 0, 0))]
+        + quarters,
+        out_specs=tuple([token_rows, token_rows] + quarters + [hidden] * 3),
+        out_shape=tuple(results),
+        name="widen",
+    )(out, tokens, mlp, *attn)
+
+
 def token_half(block, index, parts):
     rows = block.shape[0] // parts
     return lax.dynamic_slice_in_dim(block, index * rows, rows, axis=0)
@@ -1182,7 +1243,7 @@
     up_weight,
     down_weight,
 ):
-    seq_count, local_len, model_width = tokens.shape
+    _, local_len, model_width = tokens.shape
     parts = lax.axis_size("context")
     cores = lax.axis_size("tensor")
     core = lax.axis_index("tensor")
@@ -1223,6 +1284,7 @@
         weights=(query_weight, key_matrix, value_matrix, output_weight),
     )
     normed_attn = normed_attn.reshape(full_len, model_width)
+    own_cot, normed_attn = lax.optimization_barrier((own_cot, normed_attn))
     grad_out = permuted_tokens(own_cot)
 
     raw = jnp.dot(normed_attn, in_weights, preferred_element_type=jnp.float32)
@@ -1275,24 +1337,25 @@
     grad_both = jnp.concatenate([grad_gate, grad_up], axis=1)
     grad_in = row_product(normed_mlp, grad_both).astype(jnp.bfloat16)
     grad_down = row_product(grad_out, hidden).astype(jnp.bfloat16)
-    grad_branch, grad_residual, gain_mlp_part, gate_grad, up_grad, down_grad = line_call(
+    grad_branch, out, grad_residual, gain_mlp_part, mlp_grads = line_call(
         parts,
         3,
         finish_mlp_back,
-        line_parts(grad_both, mlp_in),
+        (line_parts(grad_both, mlp_in), line_parts(hidden, mlp_down)),
         (residual, own_cot, gain_mlp),
         gather=True,
+        joins=(jnp.bfloat16,),
         rests=(rows_f32, sums_f32),
         groups=((0, 1), (2,)),
         weights=(h_cols, h_cols, h_cols),
         grads=(grad_in, grad_down),
-    )
+        deliver=False,
+    )
+    mlp_grads = lax.all_to_all(mlp_grads, "context", split_axis=0, concat_axis=0, tiled=True)
     grad_branch = grad_branch.reshape(full_len, model_width)
-    grad_attended = (
-        jnp.dot(grad_branch, out_weights, preferred_element_type=jnp.float32)
-        .astype(jnp.bfloat16)
-        .reshape(full_len, kv_heads, head_group, HEAD_DIM)
-    )
+    grad_attended = jnp.dot(grad_branch, out_weights, preferred_element_type=jnp.float32)
+    grad_attended = grad_attended.astype(jnp.bfloat16)
+    grad_attended = grad_attended.reshape(full_len, kv_heads, head_group, HEAD_DIM)
     grad_probs = jnp.einsum(
         "ikgd,jkd->kgij", grad_attended, values, preferred_element_type=jnp.float32
     )
@@ -1338,32 +1401,28 @@
         ],
         axis=0,
     )
-    grad_tokens, out, _, query_grad, key_grad, value_grad, output_grad, totals = line_call(
+    grad_tokens, _, query_grad, key_grad, value_grad, output_grad, totals = line_call(
         parts,
         4,
-        finish_ends,
-        (line_parts(grad_raw, in_weights), line_parts(hidden, mlp_down)),
-        (grad_residual, inputs, gain_attn, residual),
-        joins=(jnp.float32, jnp.bfloat16),
+        finish_tokens,
+        line_parts(grad_raw, in_weights),
+        (grad_residual, inputs, gain_attn),
+        joins=(jnp.float32,),
         rests=(sums_f32,),
         groups=((0, 1, 2), (3,)),
         weights=(q_cols, kv_cols, kv_cols, q_cols),
         grads=(attn_in_grad, attn_out_grad),
         extra=gains,
     )
+    ready = (out, grad_tokens, mlp_grads, query_grad, key_grad, value_grad, output_grad)
+    out, grad_tokens, *weight_grads = widen(parts, h_cols, *ready)
     return (
         out.reshape(tokens.shape),
         grad_tokens.reshape(tokens.shape),
         totals[0],
         totals[1],
         totals[2, : heads_part.size].reshape(heads_part.shape),
-        query_grad,
-        key_grad,
-        value_grad,
-        output_grad,
-        gate_grad,
-        up_grad,
-        down_grad,
+        *weight_grads,
     )
 
 

time: 695 us -> 559 us (0.80)
  Pallas kernels: 538 us -> 415 us
  local copies, waits for them, and re-layouts: 33 us -> 19.4 us
    pallas_call x4, Pallas kernels: 538 us -> 409 us  [line_call(): pl.pallas_call(functools.partial(line_body, n, chunks, len(parts), gather...]
    unnamed x89 -> x66, local copies, waits for them, and re-layouts: 13 us -> 4.3 us
  transfers between devices with their start and end apart: 4 -> 5, of which waited for: 0 -> 0; matrix products, arithmetic and copies ran while one was open for 6% -> 11% of each run, Pallas kernels for 34% -> 42%
where the time goes in v3:
time: 559 us; the launch traced here: 555 us
  Pallas kernels  415 us (74%)
  matrix products  91.2 us (16%)
  local copies, waits for them, and re-layouts  19.4 us (3%)
  other arithmetic  18.5 us (3%)
  starting transfers between devices  9.16 us (2%)
    pallas_call x4, Pallas kernels, line_call(): pl.pallas_call(functools.partial(line_body, n, chunks, len(parts), gather...  409 us
    dot_general x4, matrix products, row_product(): lax.dot_general(left, right, (((0,), (0,)), ((), ())), preferred_element_...  21.1 us
    dot_general x4, matrix products, column_product(): lax.dot_general(left, right, (((1,), (1,)), ((), ())), preferred_element_...  21.1 us
    dot_general x1, matrix products, line_shards(): both = jnp.dot(normed_mlp, mlp_in, preferred_element_type=jnp.float32)  11.8 us
  transfers between devices with their start and end apart: 5, of which 0 were waited for; matrix products, arithmetic and copies ran while one was open for 11% of the time, Pallas kernels for 42%

profile of v3, /device:TPU:0, one launch (start us, length us, event | category | flops | bytes accessed | tf_op | source)
XLA Modules:
  0.0 555.2 jit_solution(5789487024253750395)
XLA Ops:
  4.2 67.4 %shard_map.211 = (bf16[4,2,128,2048]{3,2,1,0:T(8,128)(2,1)}, bf16[2048,512]{1,0:T(8,128)(2,1)}, bf16[2048,256]{1,0:T(8,128)(2,1)}) custom-call(bf16[128,2048]{1,0:T(8,128)(2,1)} %get-tuple-element.97.refs_0_.refs_1_.refs_2_, f32[1,2048]{1,0:T(1,128)} %bitcast.214, bf16[128,1024]{1,0:T(8,128)(2,1)} %refs_2_.1, bf16[128,512]{1,0:T(8,128)(2,1)} %refs_3_.2, ...), custom_call_target="tpu_custom_call" | custom-call | flops 4194304 | bytes 83886080 | tf_op jit(solution)/shard_map/pallas_call | solution.py:1114
  71.7 3.3 collective-permute-start.1
  75.9 5.2 fusion.65
  85.3 3.1 multiply_cosine_fusion
  96.0 2.8 fusion.13
  99.3 3.3 convolution_convert_fusion.3
  103.2 134.6 %shard_map.212 = (bf16[4,2,128,2048]{3,2,1,0:T(8,128)(2,1)}, f32[128,2048]{1,0:T(8,128)}, bf16[2048,1536]{1,0:T(8,128)(2,1)}, bf16[2048,768]{1,0:T(8,128)(2,1)}) custom-call(bf16[4,2,128,2048]{3,2,1,0:T(8,128)(2,1)} %bitcast.201, bf16[128,2048]{1,0:T(8,128)(2,1)} %get-tuple-element.97.refs_0_.refs_1_.refs_2_, f32[1,2048]{1,0:T(1,128)} %bitcast.216, ...), custom_call_target="tpu_custom_call" | custom-call | flops 8388608 | bytes 167772160 | tf_op jit(solution)/shard_map/pallas_call | solution.py:1114
  241.3 11.8 %fusion.66 = f32[1024,1536]{0,1:T(8,128)} fusion(bf16[1024,2048]{1,0:T(8,128)(2,1)} %bitcast.228, bf16[2048,1536]{1,0:T(8,128)(2,1)} %get-tuple-element.48), kind=kOutput, calls=%fused_computation.124 | convolution fusion | flops 6442450944 | bytes 16777216 | tf_op jit(solution)/shard_map/dot_general | solution.py:1327
  255.5 6.7 %multiply_convert_fusion.2 = (bf16[1024,768]{0,1:T(8,128)(2,1)S(1)}, bf16[1024,768]{0,1:T(8,128)(2,1)S(1)}, bf16[1024,768]{0,1:T(8,128)(2,1)S(1)}) fusion(f32[1024,1536]{0,1:T(8,128)} %fusion.66, bf16[1024,2048]{1,0:T(8,128)(2,1)S(1)} %bitcast.205, bf16[2048,768]{1,0:T(8,128)(2,1)S(1)} %copy-done.25), kind=kOutput, calls=%fused_computation.24 | convolution fusion | flops 3233021952 | bytes 18350080 | tf_op jit(solution)/shard_map/dot_general | solution.py:1333
  262.1 4.9 convolution_convert_fusion.5.refs_6_
  267.0 5.1 convolution_convert_fusion.4
  272.1 10.0 %convolution_convert_fusion.refs_5_ = bf16[2048,1536]{1,0:T(8,128)(2,1)} fusion(bf16[1024,2048]{1,0:T(8,128)(2,1)S(1)} %bitcast.229, bf16[1024,768]{0,1:T(8,128)(2,1)S(1)} %get-tuple-element.75, bf16[1024,768]{0,1:T(8,128)(2,1)S(1)} %get-tuple-element.74), kind=kOutput, calls=%fused_computation.6 | convolution fusion | flops 6451888128 | bytes 13631488 | tf_op jit(solution)/shard_map/dot_general | solution.py:64
  282.2 8.3 %convolution_convert_fusion.1 = bf16[1024,2048]{1,0:T(8,128)(2,1)} fusion(bf16[2048,1536]{1,0:T(8,128)(2,1)S(1)} %bitcast.225, bf16[1024,768]{0,1:T(8,128)(2,1)S(1)} %get-tuple-element.75, bf16[1024,768]{0,1:T(8,128)(2,1)S(1)} %get-tuple-element.74), kind=kOutput, calls=%fused_computation.15 | convolution fusion | flops 6450839552 | bytes 13631488 | tf_op jit(solution)/shard_map/dot_general | solution.py:70
  290.5 111.0 %shard_map.213 = (bf16[4,2,128,2048]{3,2,1,0:T(8,128)(2,1)}, bf16[2,128,2048]{2,1,0:T(8,128)(2,1)}, f32[128,2048]{1,0:T(8,128)}, f32[1,2048]{1,0:T(1,128)}, bf16[4,128,2304]{2,1,0:T(8,128)(2,1)}) custom-call(bf16[4,2,128,2048]{3,2,1,0:T(8,128)(2,1)} %bitcast.209, bf16[4,2,128,2048]{3,2,1,0:T(8,128)(2,1)} %bitcast.208, ...), custom_call_target="tpu_custom_call" | custom-call | flops 8388608 | bytes 167772160 | tf_op jit(solution)/shard_map/pallas_call | solution.py:1114
  401.5 3.6 convolution_convert_fusion.8
  405.1 5.7 %fusion = (f32[2,1024]{1,0:T(2,128)S(1)}, f32[1024,1024,2]{1,0,2:T(8,128)S(1)}) fusion(f32[2,1024]{1,0:T(2,128)S(1)} %get-tuple-element.93, f32[1024,1024,2]{1,0,2:T(8,128)} %copy-done, pred[1024,1024]{0,1:T(8,128)(4,1)S(1)} %copy-done.8, bf16[1024,2,128]{0,2,1:T(8,128)(2,1)S(1)} %bitcast.234, f32[1024,512]{0,1:T(8,128)S(1)} %fusion.65), kind=kOutput, calls=%fused_computation.3 | convolution fusion | flops 547354624 | bytes 18628608 | tf_op jit(solution)/shard_map/ikgd,jkd->kgij/dot_general | solution.py:1359
  411.2 2.7 fusion.5
  415.8 2.7 fusion.20
  428.7 4.8 all-to-all-start
  435.3 6.2 %fusion.24 = bf16[1024,128]{0,1:T(8,128)(2,1)S(1)} fusion(bf16[1024,2,128]{0,2,1:T(8,128)(2,1)} %bitcast.235, f32[2,1024]{1,0:T(2,128)S(1)} %get-tuple-element.93, f32[1024,1024,2]{1,0,2:T(8,128)} %copy-done, pred[1024,1024]{0,1:T(8,128)(4,1)S(1)} %copy-done.9), kind=kOutput, calls=%fused_computation.42 | convolution fusion | flops 545390592 | bytes 10231808 | tf_op jit(solution)/shard_map/kgij,ikgd->jkd/dot_general | solution.py:1372
  441.6 4.4 convolution_convert_fusion.2
  445.9 3.8 convolution_convert_fusion.6.refs_4_
  449.8 95.8 %shard_map.214 = (f32[2,128,2048]{2,1,0:T(8,128)}, f32[1,2048]{1,0:T(1,128)}, bf16[128,1024]{1,0:T(8,128)(2,1)}, bf16[128,512]{1,0:T(8,128)(2,1)}, bf16[128,512]...) custom-call(bf16[4,2,128,2048]{3,2,1,0:T(8,128)(2,1)} %bitcast.204, ...), custom_call_target="tpu_custom_call" | custom-call | flops 4194304 | bytes 83886080 | tf_op jit(solution)/shard_map/pallas_call | solution.py:1114
  548.4 6.6 %widen.1 = (bf16[256,2048]{1,0:T(8,128)(2,1)}, f32[256,2048]{1,0:T(8,128)}, f32[128,1024]{1,0:T(8,128)}, f32[128,512]{1,0:T(8,128)}, f32[128,512]{1,0:T(8,128)},...) custom-call(bf16[256,2048]{1,0:T(8,128)(2,1)} %bitcast.213, ...), custom_call_target="tpu_custom_call" | custom-call | tf_op jit(solution)/shard_map/widen/pallas_call | solution.py:1216
  (123 shorter events, 40.1 us)
Async XLA Ops:
  71.6 166.3 %collective-permute-start = (bf16[128,2048]{1,0:T(8,128)(2,1)}, bf16[128,2048]{1,0:T(8,128)(2,1)}, u32[]{:S(2)}, u32[]{:S(2)}) collective-permute-start(bf16[128,2048]{1,0:T(8,128)(2,1)} %get-tuple-element.42.refs_3_), channel_id=1, source_target_pairs={{0,2},{2,4},{4,6},{6,0},{1,3},{3,5},{5,7},{7,1},{8,10},{10,12},{12... | collective-permute-start | bytes 1572872 | tf_op jit(solution)/shard_map/ppermute | solution.py:1187
  71.7 167.3 %collective-permute-start.1 = (bf16[128,2048]{1,0:T(8,128)(2,1)}, bf16[128,2048]{1,0:T(8,128)(2,1)}, u32[]{:S(2)}, u32[]{:S(2)}) collective-permute-start(bf16[128,2048]{1,0:T(8,128)(2,1)} %get-tuple-element.42.refs_3_), channel_id=1, source_target_pairs={{0,4},{2,6},{4,0},{6,2},{1,5},{3,7},{5,1},{7,3},{8,12},{10,14},{12... | collective-permute-start | bytes 1572872 | tf_op jit(solution)/shard_map/ppermute | solution.py:1187
  75.0 165.1 %collective-permute-start.2 = (bf16[128,2048]{1,0:T(8,128)(2,1)}, bf16[128,2048]{1,0:T(8,128)(2,1)}, u32[]{:S(2)}, u32[]{:S(2)}) collective-permute-start(bf16[128,2048]{1,0:T(8,128)(2,1)} %get-tuple-element.42.refs_3_), channel_id=1, source_target_pairs={{0,6},{2,0},{4,2},{6,4},{1,7},{3,1},{5,3},{7,5},{8,14},{10,8},{12,... | collective-permute-start | bytes 1572872 | tf_op jit(solution)/shard_map/ppermute | solution.py:1187
  81.2 4.1 copy-start.27
  90.0 3.4 copy-start.7
  96.0 3.3 copy-start
  99.3 3.3 copy-start.15
  99.3 3.3 copy-start.21
  103.2 134.6 %copy-start.2 = (bf16[4,128,2048]{2,1,0:T(8,128)(2,1)S(1)}, bf16[4,128,2048]{2,1,0:T(8,128)(2,1)}, u32[]{:S(2)}) copy-start(bf16[4,128,2048]{2,1,0:T(8,128)(2,1)} %copy-done.1) | copy-start | bytes 6291460
  241.2 12.6 %collective-permute-start.3 = (bf16[4,128,2048]{2,1,0:T(8,128)(2,1)S(1)}, bf16[4,128,2048]{2,1,0:T(8,128)(2,1)S(1)}, u32[]{:S(2)}, u32[]{:S(2)}) collective-permute-start(bf16[4,128,2048]{2,1,0:T(8,128)(2,1)S(1)} %bitcast_dynamic-update-slice_fusion.2), channel_id=1, source_target_pairs={{0,1},{1,0},{2,3},{3,2},{4,5},{5,4},{6,7},{7,6},{8,9},{9,8},{10,11... | collective-permute-start | bytes 6291464 | tf_op jit(solution)/shard_map/ppermute | solution.py:1189
  267.0 5.1 copy-start.23
  267.0 15.1 %slice-start.2 = ((s8[6291456]{0:T(1024)(128)(4,1)}), s8[4194304]{0:T(1024)(128)(4,1)S(1)}, s32[]{:S(2)}) async-start(s8[6291456]{0:T(1024)(128)(4,1)} %bitcast.224), calls=%async_computation.3 | async-start | bytes 8388608
  272.1 10.0 %slice-start.3 = ((s8[6291456]{0:T(1024)(128)(4,1)}), s8[2097152]{0:T(1024)(128)(4,1)S(1)}, s32[]{:S(2)}) async-start(s8[6291456]{0:T(1024)(128)(4,1)} %bitcast.224), calls=%async_computation.4 | async-start | bytes 4194304
  290.5 111.0 %copy-start.18 = (bf16[2048,256]{1,0:T(8,128)(2,1)S(1)}, bf16[2048,256]{1,0:T(8,128)(2,1)}, u32[]{:S(2)}) copy-start(bf16[2048,256]{1,0:T(8,128)(2,1)} %get-tuple-element.45) | copy-start | bytes 3145732
  401.5 3.6 copy-start.8
  405.1 5.7 %copy-start.28 = (bf16[1024,256]{0,1:T(8,128)(2,1)}, bf16[1024,256]{0,1:T(8,128)(2,1)S(1)}, u32[]{:S(2)}) copy-start(bf16[1024,256]{0,1:T(8,128)(2,1)S(1)} %convolution_convert_fusion.8) | copy-start | bytes 1572868
  405.1 5.7 %slice-start = ((s8[8388608]{0:T(1024)(128)(4,1)}), s8[4194304]{0:T(1024)(128)(4,1)S(1)}, s32[]{:S(2)}) async-start(s8[8388608]{0:T(1024)(128)(4,1)} %bitcast.202), calls=%async_computation.1 | async-start | bytes 8388608
  405.1 6.1 %slice-start.1 = ((s8[8388608]{0:T(1024)(128)(4,1)}), s8[4194304]{0:T(1024)(128)(4,1)S(1)}, s32[]{:S(2)}) async-start(s8[8388608]{0:T(1024)(128)(4,1)} %bitcast.202), calls=%async_computation.2 | async-start | bytes 8388608
  425.6 9.0 %copy-start.20 = (f32[1,2048]{1,0:T(1,128)S(1)}, f32[1,2048]{1,0:T(1,128)}, u32[]{:S(2)}) copy-start(f32[1,2048]{1,0:T(1,128)} %get-tuple-element.53) | copy-start | bytes 24580
  425.6 9.7 %copy-start.9 = (pred[1024,1024]{0,1:T(8,128)(4,1)S(1)}, pred[1024,1024]{0,1:T(8,128)(4,1)}, u32[]{:S(2)}) copy-start(pred[1024,1024]{0,1:T(8,128)(4,1)} %iota_compare_fusion) | copy-start | bytes 3145732
  428.7 119.7 %all-to-all-start = ((bf16[4,128,2304]{2,1,0:T(8,128)(2,1)}), bf16[4,128,2304]{2,1,0:T(8,128)(2,1)}, u32[]{:S(2)}, u32[]{:S(2)}) async-start(bf16[4,128,2304]{2,1,0:T(8,128)(2,1)} %get-tuple-element.55), calls=%async_computation | async-start | bytes 4718592 | tf_op jit(solution)/shard_map/all_to_all | solution.py:1354
  435.3 6.3 %copy-start.19 = (bf16[1024,256]{0,1:T(8,128)(2,1)S(1)}, bf16[1024,256]{0,1:T(8,128)(2,1)}, u32[]{:S(2)}) copy-start(bf16[1024,256]{0,1:T(8,128)(2,1)} %get-tuple-element.78) | copy-start | bytes 1572868
  435.3 6.3 %copy-start.26 = (bf16[2048,512]{1,0:T(8,128)(2,1)S(1)}, bf16[2048,512]{1,0:T(8,128)(2,1)}, u32[]{:S(2)}) copy-start(bf16[2048,512]{1,0:T(8,128)(2,1)} %get-tuple-element.44) | copy-start | bytes 6291460
  441.6 4.4 copy-start.22
  (14 other events, 32.6 us)

commit v4 on v3

--- a/solution.py
+++ b/solution.py
@@ -409,6 +409,9 @@
 LINE_LAG = 2
 LINE_START_TURNS = 1
 LINE_FROM_TURN = 1
+LINE_PLAIN_FROM = 0
+LINE_PLAIN_LAG = 1
+LINE_PLAIN_STEP = 1
 LINE_GIVE_TURN = 6
 MESH = pl.DeviceIdType.MESH
 
@@ -589,7 +592,7 @@
 
 
 def give_steps(n, place, groups, grads, outs, bufs, sems, turns, from_turn, deliver):
-    first_send, first_recv, second_send, second_recv, line_send, line_recv = sems
+    first_send, first_recv, second_send, second_recv, line_send, line_recv, mine_sem = sems
     group = lax.axis_index("fsdp")
     rows = outs[0].shape[-2]
 
@@ -601,6 +604,12 @@
         block = of_group * n + far[s]
         start = pl.multiple_of(block * rows + half * half_rows, half_rows)
         return grads[g].at[pl.ds(start, half_rows)]
+
+    def mine_copy(g, s, half, k):
+        target = group if k == 0 else jnp.bitwise_xor(group, 2 - half)
+        return pltpu.make_async_copy(
+            part(g, target, s, half), bufs[g]["mine"].at[s, half, k], mine_sem.at[g, s, half, k]
+        )
 
     def first_copy(g, s, half, k):
         target = jnp.bitwise_xor(group, half + 1 if k == 0 else 3)
@@ -649,6 +658,7 @@
         for k in (1, 0):
             for half in (0, 1):
                 first_copy(g, s, half, k).start()
+                mine_copy(g, s, half, k).start()
 
     def begin():
         for i in range(2 * len(groups)):
@@ -661,7 +671,8 @@
         def step():
             for half in (0, 1):
                 first_copy(g, s, half, 1).wait_recv()
-                own = part(g, jnp.bitwise_xor(group, 2 - half), s, half)
+                mine_copy(g, s, half, 1).wait()
+                own = bufs[g]["mine"].at[s, half, 1]
                 came = bufs[g]["first"].at[s, half, 1]
                 out = bufs[g]["second_out"].at[s, half]
 
@@ -682,7 +693,8 @@
             for half in (0, 1):
                 first_copy(g, s, half, 0).wait_recv()
                 second_copy(g, s, half).wait_recv()
-                own = part(g, group, s, half)
+                mine_copy(g, s, half, 0).wait()
+                own = bufs[g]["mine"].at[s, half, 0]
                 one = bufs[g]["first"].at[s, half, 0]
                 two = bufs[g]["second"].at[s, half]
 
@@ -732,7 +744,66 @@
     return begin, plan, settle
 
 
-def line_body(n, chunks, n_part, gather, n_in, n_join, n_rest, groups, giving, deliver, extra, finish, *refs):
+def spread_steps(n, pieces, out, sems, turns, from_turn):
+    own_send, near_send, near_recv, far_send, far_recv = sems
+    group = lax.axis_index("fsdp")
+    rows = pieces.shape[1]
+    neighbours = ({"fsdp": jnp.bitwise_xor(group, 1)}, {"fsdp": jnp.bitwise_xor(group, 2)})
+
+    def block(of_group, k, half=None):
+        start = (of_group * n + k) * rows
+        if half is None:
+            return out.at[pl.ds(pl.multiple_of(start, rows), rows)]
+        return out.at[pl.ds(pl.multiple_of(start + half * (rows // 2), rows // 2), rows // 2)]
+
+    def own_copy(k):
+        return pltpu.make_async_copy(pieces.at[k], block(group, k), own_send.at[k])
+
+    def near_copy(way, k, of_group):
+        return line_copy(
+            pieces.at[k],
+            block(of_group, k),
+            near_send.at[way, k],
+            near_recv.at[way, k],
+            neighbours[way],
+        )
+
+    def far_copy(half, k, of_group):
+        ref = block(of_group, k, half)
+        return line_copy(
+            ref, ref, far_send.at[half, k], far_recv.at[half, k], neighbours[1 - half]
+        )
+
+    def begin():
+        for k in range(n):
+            for way in (0, 1):
+                near_copy(way, k, group).start()
+            own_copy(k).start()
+
+    def pass_on(k):
+        def step():
+            for half in (0, 1):
+                source = jnp.bitwise_xor(group, half + 1)
+                near_copy(half, k, source).wait_recv()
+                far_copy(half, k, source).start()
+
+        return step
+
+    def settle():
+        for k in range(n):
+            own_copy(k).wait()
+            for half in (0, 1):
+                far_copy(half, k, jnp.bitwise_xor(group, 3)).wait_recv()
+                far_copy(half, k, group).wait_send()
+                near_copy(half, k, group).wait_send()
+
+    plan = [[] for _ in range(turns)]
+    for k in range(n):
+        plan[from_turn + k * (turns - from_turn) // n].append(pass_on(k))
+    return begin, plan, settle
+
+
+def line_body(n, chunks, n_part, gather, spreading, n_in, n_join, n_rest, groups, giving, deliver, extra, finish, *refs):
     refs = list(refs)
     take = lambda count: [refs.pop(0) for _ in range(count)]
     reduce = n_part > 0
@@ -743,24 +814,27 @@
     weights = take(arrays) if fetching else []
     grads = take(len(groups)) if giving else []
     others = take(1)[0] if extra else None
-    gathered = take(1)[0] if gather else None
+    pieces = take(1)[0] if spreading else None
+    gathered_all = take(gather)
     joined = take(n_join)
     rest = take(n_rest)
     fetched = take(len(groups)) if fetching else []
+    spread_out = take(1)[0] if spreading else None
     given = take(arrays if deliver else 1) if giving else []
     gains_out = take(1)[0] if extra else None
     if reduce:
-        across, sums_in, sums_out, summed = take(4)
+        own, own_sem, across, sums_in, sums_out, summed = take(6)
         cross_send, cross_recv, sum_send, sum_recv = take(4)
     if gather:
         row_send, row_recv, pair_send, pair_recv = take(4)
     if n_join:
         join_send, join_recv = take(2)
     fetch_sems = take(7) if fetching else None
+    spread_sems = take(5) if spreading else None
     if giving:
-        names = ("first", "second_out", "second", "line_out")[: 4 if deliver else 3]
+        names = ("mine", "first", "second_out", "second", "line_out")[: 5 if deliver else 4]
         give_bufs = [dict(zip(names, take(len(names)))) for _ in groups]
-        give_sems = take(6)
+        give_sems = take(7)
     if extra:
         gain_own, gain_came, gain_line, gain_send, gain_recv, gain_line_send, gain_line_recv = take(7)
 
@@ -772,7 +846,7 @@
     def rows(j):
         return pl.ds(j * step_rows, step_rows)
 
-    line_barrier(n, place, core, bool(groups))
+    line_barrier(n, place, core, bool(groups) or spreading)
     lag = LINE_LAG if reduce else 0
     turns = chunks * max(n_part, 1) + lag + n
     plan = [[] for _ in range(turns)]
@@ -784,6 +858,11 @@
         )
     if fetching:
         own_start()
+    if spreading:
+        begin, plan, settle = spread_steps(
+            n, pieces, spread_out, spread_sems, turns, LINE_FROM_TURN
+        )
+        begin()
     if giving:
         begin, plan, settle = give_steps(
             n, place, groups, grads, given, give_bufs, give_sems, turns, LINE_GIVE_TURN, deliver
@@ -799,6 +878,11 @@
             other,
         )
 
+    def own_copy(j):
+        return pltpu.make_async_copy(
+            parts[j // chunks].at[:, core, rows(j % chunks)], own.at[:, rows(j)], own_sem.at[j]
+        )
+
     def sum_copy(way, k, j):
         return line_copy(
             sums_out.at[way, k, rows(j)],
@@ -809,45 +893,56 @@
         )
 
     def own_term(target, j):
-        return parts[j // chunks][target, core, rows(j % chunks), :].astype(jnp.float32) + across[
+        return own[target, rows(j), :].astype(jnp.float32) + across[
             target, rows(j), :
         ].astype(jnp.float32)
 
     def send_sums(way, j):
         first = place == (n - 1) * way
-        for k in range(n - 1):
+
+        @pl.loop(0, n - 1)
+        def _(k):
             target = jnp.where(way == 0, n - 1 - k, k)
             passes = jnp.where(way == 0, target - place, place - target) > 0
 
-            @pl.when(passes & first)
-            def _(k=k, target=target):
-                sums_out[way, k, rows(j), :] = own_term(target, j).astype(jnp.bfloat16)
+            @pl.when(passes & jnp.logical_not(first))
+            def _():
+                sum_copy(way, k, j).wait_recv()
+
+            @pl.when(passes)
+            def _():
+                came = sums_in[way, k, rows(j), :].astype(jnp.float32)
+                value = own_term(target, j) + jnp.where(first, 0.0, came)
+                sums_out[way, k, rows(j), :] = value.astype(jnp.bfloat16)
                 sum_copy(way, k, j).start()
 
-            @pl.when(passes & jnp.logical_not(first))
-            def _(k=k, target=target):
-                sum_copy(way, k, j).wait_recv()
-                sums_out[way, k, rows(j), :] = (
-                    own_term(target, j) + sums_in[way, k, rows(j), :].astype(jnp.float32)
-                ).astype(jnp.bfloat16)
-                sum_copy(way, k, j).start()
-
-    def row_copy(way, k, j):
+    def row_copy(way, k, j, w=0):
         block = place - k if way == 0 else place + k
         device = {"context": place + 1 if way == 0 else place - 1}
-        ref = gathered.at[block, core, rows(j)]
-        return line_copy(ref, ref, row_send.at[way, k, j], row_recv.at[way, k, j], device)
-
-    def row_arrival(way, k, j):
+        ref = gathered_all[w].at[block, core, rows(j)]
+        return line_copy(ref, ref, row_send.at[w, way, k, j], row_recv.at[w, way, k, j], device)
+
+    def row_arrival(way, k, j, w=0):
         block = place - 1 - k if way == 0 else place + 1 + k
-        ref = gathered.at[block, core, rows(j)]
-        return line_copy(
-            ref, ref, row_send.at[way, k, j], row_recv.at[way, k, j], other
-        )
-
-    def pair_copy(block, half, j):
-        ref = gathered.at[block, half, rows(j)]
-        return line_copy(ref, ref, pair_send.at[block, j], pair_recv.at[block, j], other)
+        ref = gathered_all[w].at[block, core, rows(j)]
+        return line_copy(ref, ref, row_send.at[w, way, k, j], row_recv.at[w, way, k, j], other)
+
+    def pair_copy(block, half, j, w=0):
+        ref = gathered_all[w].at[block, half, rows(j)]
+        return line_copy(ref, ref, pair_send.at[w, block, j], pair_recv.at[w, block, j], other)
+
+    def send_rows(j, values, w=0):
+        gathered_all[w][place, core, rows(j), :] = values
+
+        @pl.when(place < n - 1)
+        def _():
+            row_copy(0, 0, j, w).start()
+
+        @pl.when(place > 0)
+        def _():
+            row_copy(1, 0, j, w).start()
+
+        pair_copy(place, core, j, w).start()
 
     def finish_rows(j):
         total = None
@@ -870,19 +965,9 @@
         made = made if isinstance(made, tuple) else (made,)
         made = list(made)
         if gather and j < chunks:
-            gathered[place, core, rows(j), :] = made.pop(0)
-
-            @pl.when(place < n - 1)
-            def _():
-                row_copy(0, 0, j).start()
-
-            @pl.when(place > 0)
-            def _():
-                row_copy(1, 0, j).start()
-
-            pair_copy(place, core, j).start()
+            send_rows(j, made.pop(0))
         if made:
-            i = j // chunks - gather
+            i = j // chunks - (gather > 0)
             joined[i][core, rows(j % chunks), :] = made.pop(0)
             join_copy(i, core, j % chunks).start()
 
@@ -890,7 +975,7 @@
         ref = joined[i].at[half, rows(j)]
         return line_copy(ref, ref, join_send.at[i, j], join_recv.at[i, j], other)
 
-    def pass_rows(k, j):
+    def pass_rows(k, j, w=0):
         for way in (0, 1):
             block = place - 1 - k if way == 0 else place + 1 + k
             here = block >= 0 if way == 0 else block <= n - 1
@@ -898,22 +983,23 @@
 
             @pl.when(here)
             def _(way=way, block=block):
-                row_arrival(way, k, j).wait_recv()
+                row_arrival(way, k, j, w).wait_recv()
 
             if k + 1 <= n - 2:
 
                 @pl.when(here & onward)
                 def _(way=way):
-                    row_copy(way, k + 1, j).start()
+                    row_copy(way, k + 1, j, w).start()
 
             @pl.when(here)
             def _(way=way, block=block):
-                pair_copy(block, core, j).start()
+                pair_copy(block, core, j, w).start()
 
     all_chunks = chunks * max(n_part, 1)
     if reduce:
         for j in range(all_chunks):
             cross(j).start()
+            own_copy(j).start()
 
     def gains_plan():
         group = lax.axis_index("fsdp")
@@ -945,7 +1031,6 @@
 
         def first():
             gain_own[0] = others[...]
-            gain_own[0, 0:1, :] = rest[0][...]
             hop(0).start()
 
         def next_hop(h):
@@ -978,26 +1063,40 @@
 
     near = jnp.where(place < n // 2, 0, 1)
     gain_steps = gains_plan() if extra else []
+    if not reduce:
+        for j in range(chunks):
+            finish_rows(j)
     for i in range(turns):
         for step in plan[i]:
             step()
+        if gather > 1 and 0 <= i - LINE_PLAIN_FROM < chunks:
+            j = i - LINE_PLAIN_FROM
+            send_rows(j, ins[-1][rows(j), :], 1)
         if reduce and i < all_chunks:
+            own_copy(i).wait()
             cross(i).wait_recv()
             send_sums(near, i)
         if reduce and 0 <= i - 1 < all_chunks:
             send_sums(1 - near, i - 1)
-        if 0 <= i - lag < all_chunks:
+        if reduce and 0 <= i - lag < all_chunks:
             finish_rows(i - lag)
-        if extra and i - lag >= chunks and gain_steps:
+        if i > 0 and gain_steps:
             gain_steps.pop(0)()
         if gather:
             for k in range(n - 1):
                 if 0 <= i - lag - 1 - k < chunks:
                     pass_rows(k, i - lag - 1 - k)
+                if gather > 1 and 0 <= i - LINE_PLAIN_LAG - k * LINE_PLAIN_STEP < chunks:
+                    pass_rows(k, i - LINE_PLAIN_LAG - k * LINE_PLAIN_STEP, 1)
 
     for step in gain_steps:
         step()
-    if groups:
+    if gather > 1:
+        for i in range(turns, turns + LINE_PLAIN_LAG + (n - 2) * LINE_PLAIN_STEP):
+            for k in range(n - 1):
+                if 0 <= i - LINE_PLAIN_LAG - k * LINE_PLAIN_STEP < chunks:
+                    pass_rows(k, i - LINE_PLAIN_LAG - k * LINE_PLAIN_STEP, 1)
+    if groups or spreading:
         settle()
     for j in range(all_chunks):
         if reduce:
@@ -1012,23 +1111,24 @@
                 def _(k=k, j=j):
                     sum_copy(1, k, j).wait_send()
 
-        if gather and j < chunks:
+        for w in range(gather if j < chunks else 0):
             for block in range(n):
-                pair_copy(block, 1 - core, j).wait_recv()
-                pair_copy(block, core, j).wait_send()
+                pair_copy(block, 1 - core, j, w).wait_recv()
+                pair_copy(block, core, j, w).wait_send()
             for k in range(n - 1):
 
                 @pl.when((place < n - 1) & (place >= k))
-                def _(k=k, j=j):
-                    row_copy(0, k, j).wait_send()
+                def _(k=k, j=j, w=w):
+                    row_copy(0, k, j, w).wait_send()
 
                 @pl.when((place > 0) & (place + k <= n - 1))
-                def _(k=k, j=j):
-                    row_copy(1, k, j).wait_send()
-
-        if n_join and j // chunks >= gather:
-            join_copy(j // chunks - gather, 1 - core, j % chunks).wait_recv()
-            join_copy(j // chunks - gather, core, j % chunks).wait_send()
+                def _(k=k, j=j, w=w):
+                    row_copy(1, k, j, w).wait_send()
+
+        i = j // chunks - (gather > 0)
+        if n_join and i >= 0:
+            join_copy(i, 1 - core, j % chunks).wait_recv()
+            join_copy(i, core, j % chunks).wait_send()
 
 
 def line_call(
@@ -1037,7 +1137,7 @@
     finish,
     part,
     ins,
-    gather=False,
+    gather=0,
     joins=(),
     rests=(),
     chunks=LINE_CHUNKS,
@@ -1046,6 +1146,7 @@
     grads=(),
     deliver=True,
     extra=None,
+    pieces=None,
 ):
     parts = () if part is None else part if isinstance(part, tuple) else (part,)
     reduce = len(parts) > 0
@@ -1053,7 +1154,7 @@
     row_count, model_width = ins[0].shape
     vmem = pl.BlockSpec(memory_space=pltpu.VMEM)
     outs = []
-    if gather:
+    for _ in range(gather):
         outs.append(jax.ShapeDtypeStruct((n, 2, row_count, model_width), jnp.bfloat16))
     outs += [jax.ShapeDtypeStruct((2, row_count, model_width), kind) for kind in joins]
     outs += list(rests)
@@ -1064,6 +1165,10 @@
         outs.append(jax.ShapeDtypeStruct((rows, width), jnp.bfloat16))
         out_specs.append(pl.BlockSpec(memory_space=pl.ANY))
     dma = pltpu.SemaphoreType.DMA
+    if pieces is not None:
+        rows = pieces.shape[0] * pieces.shape[1] * lax.axis_size("fsdp")
+        outs.append(jax.ShapeDtypeStruct((rows, pieces.shape[2]), jnp.bfloat16))
+        out_specs.append(pl.BlockSpec(memory_space=pl.ANY))
     if giving:
         owned = grads[0].shape[0] // (n * lax.axis_size("fsdp"))
         shapes = [(owned, width * n) for width in weights]
@@ -1080,36 +1185,46 @@
     scratch = []
     if reduce:
         slot = pltpu.VMEM((2, n - 1, sum_rows, model_width), jnp.bfloat16)
+        scratch += [pltpu.VMEM((n, sum_rows, model_width), jnp.bfloat16), dma((total_chunks,))]
         scratch += [pltpu.VMEM((n, sum_rows, model_width), jnp.bfloat16), slot, slot]
         scratch += [pltpu.VMEM((row_count // chunks, model_width), jnp.float32)]
         tally = (2, n - 1, total_chunks)
         scratch += [dma((total_chunks,)), dma((total_chunks,)), dma(tally), dma(tally)]
     if gather:
-        scratch += [dma((2, n - 1, chunks)), dma((2, n - 1, chunks)), dma((n, chunks)), dma((n, chunks))]
+        tally = (gather, 2, n - 1, chunks)
+        scratch += [dma(tally), dma(tally), dma((gather, n, chunks)), dma((gather, n, chunks))]
     if joins:
         scratch += [dma((len(joins), chunks)), dma((len(joins), chunks))]
     if groups and not giving:
         arrays = len(weights)
-        pieces = (2, len(groups), n)
+        tally = (2, len(groups), n)
         scratch += [dma((arrays,)), dma((arrays, n)), dma((arrays, n))]
-        scratch += [dma(pieces), dma(pieces), dma(pieces), dma(pieces)]
+        scratch += [dma(tally), dma(tally), dma(tally), dma(tally)]
+    if pieces is not None:
+        scratch += [dma((n,))] + [dma((2, n))] * 4
     if giving:
         for grad in grads:
             halves = (owned // 2, grad.shape[1])
-            for lead in ((n, 2, 2), (n, 2), (n, 2)):
+            for lead in ((n, 2, 2), (n, 2, 2), (n, 2), (n, 2)):
                 scratch.append(pltpu.VMEM(lead + halves, jnp.bfloat16))
             if deliver:
                 scratch.append(pltpu.VMEM((n - 1, owned, grad.shape[1]), jnp.bfloat16))
         count = len(groups)
         scratch += [dma((count, n, 2, 2)), dma((count, n, 2, 2))]
         scratch += [dma((count, n, 2)), dma((count, n, 2))]
-        scratch += [dma((len(weights), n)), dma((len(weights), n))]
+        scratch += [dma((len(weights), n)), dma((len(weights), n)), dma((count, n, 2, 2))]
     if extra is not None:
         stack = pltpu.VMEM((3,) + extra.shape, jnp.float32)
         scratch += [stack, stack, pltpu.VMEM((n,) + extra.shape, jnp.float32)]
         scratch += [dma((3,)), dma((3,)), dma((n - 1,)), dma((n - 1,))]
     operands = list(parts) + list(ins) + (list(grads) if giving else list(weights))
     operands += [] if extra is None else [extra]
+    operands += [] if pieces is None else [pieces]
+    anywhere = [*parts, *grads]
+    in_specs = [
+        pl.BlockSpec(memory_space=pl.ANY) if any(a is b for b in anywhere) else vmem
+        for a in operands
+    ]
     moved = row_count * model_width * 2 * n * (2 * reduce + 2 * gather)
     return pl.pallas_call(
         functools.partial(
@@ -1118,6 +1233,7 @@
             chunks,
             len(parts),
             gather,
+            pieces is not None,
             len(ins),
             len(joins),
             len(rests),
@@ -1128,7 +1244,7 @@
             finish,
         ),
         out_shape=tuple(outs),
-        in_specs=[vmem] * len(operands),
+        in_specs=in_specs,
         out_specs=tuple(out_specs),
         scratch_shapes=scratch,
         compiler_params=pltpu.CompilerParams(
@@ -1172,7 +1288,6 @@
     values = ins[1][rows, :].astype(jnp.float32)
     scale = rms_scale(values)
     hat = values * scale
-    gain_rows(j, rest[0], total * hat)
     return ins[0][rows, :] + norm_back(total, hat, scale, ins[2][...])
 
 
@@ -1279,7 +1394,7 @@
         finish_gather,
         None,
         (inputs, gain_attn),
-        gather=True,
+        gather=1,
         groups=((0, 1, 2), (3,)),
         weights=(query_weight, key_matrix, value_matrix, output_weight),
     )
@@ -1317,7 +1432,7 @@
         finish_attention,
         line_parts(attended, out_weights),
         (inputs, gain_mlp),
-        gather=True,
+        gather=1,
         rests=(rows_f32,),
         groups=((0, 1), (2,)),
         weights=(gate_weight, up_weight, down_weight),
@@ -1343,7 +1458,7 @@
         finish_mlp_back,
         (line_parts(grad_both, mlp_in), line_parts(hidden, mlp_down)),
         (residual, own_cot, gain_mlp),
-        gather=True,
+        gather=1,
         joins=(jnp.bfloat16,),
         rests=(rows_f32, sums_f32),
         groups=((0, 1), (2,)),
@@ -1392,23 +1507,26 @@
     ).astype(jnp.bfloat16)
     attn_in_grad = row_product(normed_attn, grad_raw).astype(jnp.bfloat16)
     attn_out_grad = row_product(grad_branch, attended).astype(jnp.bfloat16)
+    gain_attn_part = (
+        jnp.sum(attn_in_grad.astype(jnp.float32) * in_weights.astype(jnp.float32), axis=1)[None]
+        / gain_attn
+    )
     gains = jnp.concatenate(
         [
-            jnp.zeros((1, model_width), jnp.float32),
+            gain_attn_part,
             gain_mlp_part,
             jnp.pad(heads_part.reshape(1, -1), ((0, 0), (0, model_width - heads_part.size))),
             jnp.zeros((5, model_width), jnp.float32),
         ],
         axis=0,
     )
-    grad_tokens, _, query_grad, key_grad, value_grad, output_grad, totals = line_call(
+    grad_tokens, query_grad, key_grad, value_grad, output_grad, totals = line_call(
         parts,
         4,
         finish_tokens,
         line_parts(grad_raw, in_weights),
         (grad_residual, inputs, gain_attn),
         joins=(jnp.float32,),
-        rests=(sums_f32,),
         groups=((0, 1, 2), (3,)),
         weights=(q_cols, kv_cols, kv_cols, q_cols),
         grads=(attn_in_grad, attn_out_grad),

time: 559 us -> 545 us (0.975)
  Pallas kernels: 415 us -> 403 us
    pallas_call x4, Pallas kernels: 409 us -> 396 us  [line_call(): pl.pallas_call(functools.partial(line_body, n, chunks, len(parts), gather...]
  transfers between devices with their start and end apart: 5 -> 5, of which waited for: 0 -> 0; matrix products, arithmetic and copies ran while one was open for 11% -> 11% of each run, Pallas kernels for 42% -> 41%
where the time goes in v4:
time: 545 us; the launch traced here: 542 us
  Pallas kernels  403 us (74%)
  matrix products  91.8 us (17%)
  local copies, waits for them, and re-layouts  20.1 us (4%)
  other arithmetic  17.4 us (3%)
  starting transfers between devices  8.24 us (2%)
    pallas_call x4, Pallas kernels, line_call(): pl.pallas_call(functools.partial(line_body, n, chunks, len(parts), gather...  396 us
    dot_general x4, matrix products, row_product(): lax.dot_general(left, right, (((0,), (0,)), ((), ())), preferred_element_...  21.4 us
    dot_general x4, matrix products, column_product(): lax.dot_general(left, right, (((1,), (1,)), ((), ())), preferred_element_...  21.1 us
    dot_general x1, matrix products, line_shards(): both = jnp.dot(normed_mlp, mlp_in, preferred_element_type=jnp.float32)  11.7 us
  transfers between devices with their start and end apart: 5, of which 0 were waited for; matrix products, arithmetic and copies ran while one was open for 11% of the time, Pallas kernels for 41%

profile of v4, /device:TPU:0, one launch (start us, length us, event | category | flops | bytes accessed | tf_op | source)
XLA Modules:
  0.0 542.1 jit_solution(12487838074464128663)
XLA Ops:
  4.2 67.5 %shard_map.211 = (bf16[4,2,128,2048]{3,2,1,0:T(8,128)(2,1)}, bf16[2048,512]{1,0:T(8,128)(2,1)}, bf16[2048,256]{1,0:T(8,128)(2,1)}) custom-call(bf16[128,2048]{1,0:T(8,128)(2,1)} %get-tuple-element.99.refs_0_.refs_1_.refs_2_, f32[1,2048]{1,0:T(1,128)} %bitcast.214, bf16[128,1024]{1,0:T(8,128)(2,1)} %refs_2_.1, bf16[128,512]{1,0:T(8,128)(2,1)} %refs_3_.2, ...), custom_call_target="tpu_custom_call" | custom-call | flops 4194304 | bytes 83886080 | tf_op jit(solution)/shard_map/pallas_call | solution.py:1229
  71.8 2.8 collective-permute-start.1
  76.0 5.2 fusion.65
  85.4 3.1 multiply_cosine_fusion
  96.1 2.8 fusion.13
  99.4 3.3 convolution_convert_fusion.3
  103.4 136.0 %shard_map.212 = (bf16[4,2,128,2048]{3,2,1,0:T(8,128)(2,1)}, f32[128,2048]{1,0:T(8,128)}, bf16[2048,1536]{1,0:T(8,128)(2,1)}, bf16[2048,768]{1,0:T(8,128)(2,1)}) custom-call(bf16[4,2,128,2048]{3,2,1,0:T(8,128)(2,1)} %bitcast.201, bf16[128,2048]{1,0:T(8,128)(2,1)} %get-tuple-element.99.refs_0_.refs_1_.refs_2_, f32[1,2048]{1,0:T(1,128)} %bitcast.216, ...), custom_call_target="tpu_custom_call" | custom-call | flops 8388608 | bytes 167772160 | tf_op jit(solution)/shard_map/pallas_call | solution.py:1229
  242.8 11.7 %fusion.66 = f32[1024,1536]{0,1:T(8,128)} fusion(bf16[1024,2048]{1,0:T(8,128)(2,1)} %bitcast.231, bf16[2048,1536]{1,0:T(8,128)(2,1)} %get-tuple-element.48), kind=kOutput, calls=%fused_computation.126 | convolution fusion | flops 6442450944 | bytes 16777216 | tf_op jit(solution)/shard_map/dot_general | solution.py:1442
  257.0 6.7 %multiply_convert_fusion.2 = (bf16[1024,768]{0,1:T(8,128)(2,1)S(1)}, bf16[1024,768]{0,1:T(8,128)(2,1)S(1)}, bf16[1024,768]{0,1:T(8,128)(2,1)S(1)}) fusion(f32[1024,1536]{0,1:T(8,128)} %fusion.66, bf16[1024,2048]{1,0:T(8,128)(2,1)S(1)} %bitcast.205, bf16[2048,768]{1,0:T(8,128)(2,1)S(1)} %copy-done.25), kind=kOutput, calls=%fused_computation.25 | convolution fusion | flops 3233021952 | bytes 18350080 | tf_op jit(solution)/shard_map/dot_general | solution.py:1448
  263.6 4.9 convolution_convert_fusion.5.refs_6_
  268.5 5.1 convolution_convert_fusion.4
  273.6 9.9 %convolution_convert_fusion.refs_5_ = bf16[2048,1536]{1,0:T(8,128)(2,1)} fusion(bf16[1024,2048]{1,0:T(8,128)(2,1)S(1)} %bitcast.232, bf16[1024,768]{0,1:T(8,128)(2,1)S(1)} %get-tuple-element.75, bf16[1024,768]{0,1:T(8,128)(2,1)S(1)} %get-tuple-element.74), kind=kOutput, calls=%fused_computation.6 | convolution fusion | flops 6451888128 | bytes 13631488 | tf_op jit(solution)/shard_map/dot_general | solution.py:64
  283.6 8.3 %convolution_convert_fusion.1 = bf16[1024,2048]{1,0:T(8,128)(2,1)} fusion(bf16[2048,1536]{1,0:T(8,128)(2,1)S(1)} %bitcast.226, bf16[1024,768]{0,1:T(8,128)(2,1)S(1)} %get-tuple-element.75, bf16[1024,768]{0,1:T(8,128)(2,1)S(1)} %get-tuple-element.74), kind=kOutput, calls=%fused_computation.16 | convolution fusion | flops 6450839552 | bytes 13631488 | tf_op jit(solution)/shard_map/dot_general | solution.py:70
  291.9 105.6 %shard_map.213 = (bf16[4,2,128,2048]{3,2,1,0:T(8,128)(2,1)}, bf16[2,128,2048]{2,1,0:T(8,128)(2,1)}, f32[128,2048]{1,0:T(8,128)}, f32[1,2048]{1,0:T(1,128)}, bf16[4,128,2304]{2,1,0:T(8,128)(2,1)}) custom-call(bf16[4,2,128,2048]{3,2,1,0:T(8,128)(2,1)} %bitcast.209, bf16[4,2,128,2048]{3,2,1,0:T(8,128)(2,1)} %bitcast.208, ...), custom_call_target="tpu_custom_call" | custom-call | flops 8388608 | bytes 167772160 | tf_op jit(solution)/shard_map/pallas_call | solution.py:1229
  397.5 3.6 convolution_convert_fusion.8
  401.2 5.7 %fusion = (f32[2,1024]{1,0:T(2,128)S(1)}, f32[1024,1024,2]{1,0,2:T(8,128)S(1)}) fusion(f32[2,1024]{1,0:T(2,128)S(1)} %get-tuple-element.93, f32[1024,1024,2]{1,0,2:T(8,128)} %copy-done.1, pred[1024,1024]{0,1:T(8,128)(4,1)S(1)} %copy-done.9, bf16[1024,2,128]{0,2,1:T(8,128)(2,1)S(1)} %bitcast.235, f32[1024,512]{0,1:T(8,128)S(1)} %fusion.65), kind=kOutput, calls=%fused_computation.3 | convolution fusion | flops 547354624 | bytes 18628608 | tf_op jit(solution)/shard_map/ikgd,jkd->kgij/dot_general | solution.py:1474
  407.2 2.7 fusion.5
  411.8 2.7 fusion.20
  421.7 3.9 all-to-all-start
  425.6 6.5 %fusion.24 = bf16[1024,128]{0,1:T(8,128)(2,1)S(1)} fusion(bf16[1024,2,128]{0,2,1:T(8,128)(2,1)} %bitcast.236, f32[2,1024]{1,0:T(2,128)S(1)} %get-tuple-element.93, f32[1024,1024,2]{1,0,2:T(8,128)} %copy-done.1, pred[1024,1024]{0,1:T(8,128)(4,1)} %iota_compare_fusion), kind=kOutput, calls=%fused_computation.43 | convolution fusion | flops 545390592 | bytes 10231808 | tf_op jit(solution)/shard_map/kgij,ikgd->jkd/dot_general | solution.py:1487
  432.1 4.2 multiply_reduce_fusion
  439.5 4.4 convolution_convert_fusion.2
  443.8 87.2 %shard_map.214 = (f32[2,128,2048]{2,1,0:T(8,128)}, bf16[128,1024]{1,0:T(8,128)(2,1)}, bf16[128,512]{1,0:T(8,128)(2,1)}, bf16[128,512]{1,0:T(8,128)(2,1)}, bf16[128,1024]{1,0:T(8,128)(2,1)}, /*index=5*/f32[8,2048]{1,0:T(8,128)}) custom-call(bf16[4,2,128,2048]{3,2,1,0:T(8,128)(2,1)} %bitcast.204, f32[128,2048]{1,0:T(8,128)} %get-tuple-element.52.refs_1_, ...), custom_call_target="tpu_custom_call" | custom-call | flops 4194304 | bytes 83886080 | tf_op jit(solution)/shard_map/pallas_call | solution.py:1229
  535.2 6.6 %widen.1 = (bf16[256,2048]{1,0:T(8,128)(2,1)}, f32[256,2048]{1,0:T(8,128)}, f32[128,1024]{1,0:T(8,128)}, f32[128,512]{1,0:T(8,128)}, f32[128,512]{1,0:T(8,128)},...) custom-call(bf16[256,2048]{1,0:T(8,128)(2,1)} %bitcast.213, ...), custom_call_target="tpu_custom_call" | custom-call | tf_op jit(solution)/shard_map/widen/pallas_call | solution.py:1331
  (123 shorter events, 40.3 us)
Async XLA Ops:
  71.7 167.7 %collective-permute-start = (bf16[128,2048]{1,0:T(8,128)(2,1)}, bf16[128,2048]{1,0:T(8,128)(2,1)}, u32[]{:S(2)}, u32[]{:S(2)}) collective-permute-start(bf16[128,2048]{1,0:T(8,128)(2,1)} %get-tuple-element.42.refs_3_), channel_id=1, source_target_pairs={{0,2},{2,4},{4,6},{6,0},{1,3},{3,5},{5,7},{7,1},{8,10},{10,12},{12... | collective-permute-start | bytes 1572872 | tf_op jit(solution)/shard_map/ppermute | solution.py:1302
  71.8 168.7 %collective-permute-start.1 = (bf16[128,2048]{1,0:T(8,128)(2,1)}, bf16[128,2048]{1,0:T(8,128)(2,1)}, u32[]{:S(2)}, u32[]{:S(2)}) collective-permute-start(bf16[128,2048]{1,0:T(8,128)(2,1)} %get-tuple-element.42.refs_3_), channel_id=1, source_target_pairs={{0,4},{2,6},{4,0},{6,2},{1,5},{3,7},{5,1},{7,3},{8,12},{10,14},{12... | collective-permute-start | bytes 1572872 | tf_op jit(solution)/shard_map/ppermute | solution.py:1302
  74.5 167.1 %collective-permute-start.2 = (bf16[128,2048]{1,0:T(8,128)(2,1)}, bf16[128,2048]{1,0:T(8,128)(2,1)}, u32[]{:S(2)}, u32[]{:S(2)}) collective-permute-start(bf16[128,2048]{1,0:T(8,128)(2,1)} %get-tuple-element.42.refs_3_), channel_id=1, source_target_pairs={{0,6},{2,0},{4,2},{6,4},{1,7},{3,1},{5,3},{7,5},{8,14},{10,8},{12,... | collective-permute-start | bytes 1572872 | tf_op jit(solution)/shard_map/ppermute | solution.py:1302
  81.3 4.1 copy-start.27
  90.0 3.4 copy-start.8
  99.4 3.3 copy-start.14
  99.4 3.3 copy-start.21
  103.3 136.1 %copy-start.3 = (bf16[4,128,2048]{2,1,0:T(8,128)(2,1)S(1)}, bf16[4,128,2048]{2,1,0:T(8,128)(2,1)}, u32[]{:S(2)}) copy-start(bf16[4,128,2048]{2,1,0:T(8,128)(2,1)} %copy-done.2) | copy-start | bytes 6291460
  242.7 12.6 %collective-permute-start.3 = (bf16[4,128,2048]{2,1,0:T(8,128)(2,1)S(1)}, bf16[4,128,2048]{2,1,0:T(8,128)(2,1)S(1)}, u32[]{:S(2)}, u32[]{:S(2)}) collective-permute-start(bf16[4,128,2048]{2,1,0:T(8,128)(2,1)S(1)} %bitcast_dynamic-update-slice_fusion.2), channel_id=1, source_target_pairs={{0,1},{1,0},{2,3},{3,2},{4,5},{5,4},{6,7},{7,6},{8,9},{9,8},{10,11... | collective-permute-start | bytes 6291464 | tf_op jit(solution)/shard_map/ppermute | solution.py:1304
  268.5 5.1 copy-start.24
  268.5 15.0 %slice-start.2 = ((s8[6291456]{0:T(1024)(128)(4,1)}), s8[4194304]{0:T(1024)(128)(4,1)S(1)}, s32[]{:S(2)}) async-start(s8[6291456]{0:T(1024)(128)(4,1)} %bitcast.225), calls=%async_computation.3 | async-start | bytes 8388608
  273.6 9.9 %slice-start.3 = ((s8[6291456]{0:T(1024)(128)(4,1)}), s8[2097152]{0:T(1024)(128)(4,1)S(1)}, s32[]{:S(2)}) async-start(s8[6291456]{0:T(1024)(128)(4,1)} %bitcast.225), calls=%async_computation.4 | async-start | bytes 4194304
  291.9 105.7 %copy-start.17 = (bf16[2048,256]{1,0:T(8,128)(2,1)S(1)}, bf16[2048,256]{1,0:T(8,128)(2,1)}, u32[]{:S(2)}) copy-start(bf16[2048,256]{1,0:T(8,128)(2,1)} %get-tuple-element.45) | copy-start | bytes 3145732
  397.5 3.6 copy-start.9
  401.1 5.7 %copy-start.28 = (bf16[1024,256]{0,1:T(8,128)(2,1)}, bf16[1024,256]{0,1:T(8,128)(2,1)S(1)}, u32[]{:S(2)}) copy-start(bf16[1024,256]{0,1:T(8,128)(2,1)S(1)} %convolution_convert_fusion.8) | copy-start | bytes 1572868
  401.1 5.7 %slice-start = ((s8[8388608]{0:T(1024)(128)(4,1)}), s8[4194304]{0:T(1024)(128)(4,1)S(1)}, s32[]{:S(2)}) async-start(s8[8388608]{0:T(1024)(128)(4,1)} %bitcast.202), calls=%async_computation.1 | async-start | bytes 8388608
  401.2 6.1 %slice-start.1 = ((s8[8388608]{0:T(1024)(128)(4,1)}), s8[4194304]{0:T(1024)(128)(4,1)S(1)}, s32[]{:S(2)}) async-start(s8[8388608]{0:T(1024)(128)(4,1)} %bitcast.202), calls=%async_computation.2 | async-start | bytes 8388608
  421.7 112.1 %all-to-all-start = ((bf16[4,128,2304]{2,1,0:T(8,128)(2,1)}), bf16[4,128,2304]{2,1,0:T(8,128)(2,1)S(1)}, u32[]{:S(2)}, u32[]{:S(2)}) async-start(bf16[4,128,2304]{2,1,0:T(8,128)(2,1)} %get-tuple-element.55), calls=%async_computation | async-start | bytes 4718592 | tf_op jit(solution)/shard_map/all_to_all | solution.py:1469
  425.6 6.5 %copy-start.18 = (bf16[1024,256]{0,1:T(8,128)(2,1)S(1)}, bf16[1024,256]{0,1:T(8,128)(2,1)}, u32[]{:S(2)}) copy-start(bf16[1024,256]{0,1:T(8,128)(2,1)} %get-tuple-element.78) | copy-start | bytes 1572868
  425.6 6.5 %copy-start.22 = (bf16[4,2,128,2048]{3,2,1,0:T(8,128)(2,1)S(1)}, bf16[4,2,128,2048]{3,2,1,0:T(8,128)(2,1)}, u32[]{:S(2)}) copy-start(bf16[4,2,128,2048]{3,2,1,0:T(8,128)(2,1)} %get-tuple-element.41) | copy-start | bytes 12582916
  425.6 6.5 %copy-start.26 = (bf16[2048,512]{1,0:T(8,128)(2,1)S(1)}, bf16[2048,512]{1,0:T(8,128)(2,1)}, u32[]{:S(2)}) copy-start(bf16[2048,512]{1,0:T(8,128)(2,1)} %get-tuple-element.44) | copy-start | bytes 6291460
  432.1 4.3 copy-start.19
  432.1 4.3 copy-start.15
  432.1 4.3 copy-start.23
  (14 other events, 34.3 us)

commit v5 on v4

--- a/solution.py
+++ b/solution.py
@@ -1308,6 +1308,52 @@
     return both.reshape(n * 2 * shape[0], shape[1])
 
 
+BACK_BLOCK = 256
+
+
+def attend_back_body(kv_heads, group, queries, keys, values, grads, d_queries, d_keys, d_values):
+    length = queries.shape[0]
+    scale = 1.0 / math.sqrt(HEAD_DIM)
+    d_keys[...] = jnp.zeros_like(d_keys)
+    d_values[...] = jnp.zeros_like(d_values)
+    for h in range(kv_heads):
+        own = slice(h * HEAD_DIM, (h + 1) * HEAD_DIM)
+        for start in range(0, length, BACK_BLOCK):
+            end = start + BACK_BLOCK
+            shape = (BACK_BLOCK, end)
+            at = lax.broadcasted_iota(jnp.int32, shape, 0) + start
+            visible = lax.broadcasted_iota(jnp.int32, shape, 1) <= at
+            key, value = keys[0:end, own], values[0:end, own]
+            for m in range(h * group, (h + 1) * group):
+                cols = slice(m * HEAD_DIM, (m + 1) * HEAD_DIM)
+                query, grad = queries[start:end, cols], grads[start:end, cols]
+                weights = jnp.where(visible, jnp.exp(column_product(query, key) * scale), 0.0)
+                probs = weights / jnp.sum(weights, axis=1, keepdims=True)
+                grad_probs = column_product(grad, value)
+                delta = jnp.sum(probs * grad_probs, axis=1, keepdims=True)
+                grad_scores = (probs * (grad_probs - delta)).astype(jnp.bfloat16)
+                d_queries[start:end, cols] = (
+                    jnp.dot(grad_scores, key, preferred_element_type=jnp.float32) * scale
+                )
+                d_keys[0:end, own] += row_product(grad_scores, query) * scale
+                d_values[0:end, own] += row_product(probs.astype(jnp.bfloat16), grad)
+
+
+def attend_back(kv_heads, group, queries, keys, values, grads):
+    vmem = pl.BlockSpec(memory_space=pltpu.VMEM)
+    shapes = [jax.ShapeDtypeStruct(a.shape, jnp.float32) for a in (queries, keys, values)]
+    work = 5 * queries.shape[0] ** 2 * queries.shape[1]
+    return pl.pallas_call(
+        functools.partial(attend_back_body, kv_heads, group),
+        out_shape=tuple(shapes),
+        in_specs=[vmem] * 4,
+        out_specs=(vmem,) * 3,
+        compiler_params=pltpu.CompilerParams(vmem_limit_bytes=48 << 20),
+        cost_estimate=pl.CostEstimate(flops=work, bytes_accessed=4 << 20, transcendentals=0),
+        name="attend_back",
+    )(queries, keys, values, grads)
+
+
 def widen_body(h_cols, out, tokens, mlp, *refs):
     attn, results = refs[:4], refs[4:]
     results[0][...] = out[...]
@@ -1470,23 +1516,16 @@
     grad_branch = grad_branch.reshape(full_len, model_width)
     grad_attended = jnp.dot(grad_branch, out_weights, preferred_element_type=jnp.float32)
     grad_attended = grad_attended.astype(jnp.bfloat16)
-    grad_attended = grad_attended.reshape(full_len, kv_heads, head_group, HEAD_DIM)
-    grad_probs = jnp.einsum(
-        "ikgd,jkd->kgij", grad_attended, values, preferred_element_type=jnp.float32
-    )
-    delta = jnp.sum(probs * grad_probs, axis=-1, keepdims=True)
-    grad_scores = (probs * (grad_probs - delta)).astype(jnp.bfloat16)
-    grad_queries = (
-        jnp.einsum("kgij,jkd->ikgd", grad_scores, keys, preferred_element_type=jnp.float32)
-        * score_scale
-    ).reshape(full_len, q_heads, HEAD_DIM)
-    grad_keys = (
-        jnp.einsum("kgij,ikgd->jkd", grad_scores, queries, preferred_element_type=jnp.float32)
-        * score_scale
-    )
-    grad_values = jnp.einsum(
-        "kgij,ikgd->jkd", probs_low, grad_attended, preferred_element_type=jnp.float32
-    )
+    grad_queries, grad_keys, grad_values = attend_back(
+        kv_heads,
+        head_group,
+        queries.reshape(full_len, q_cols),
+        keys.reshape(full_len, kv_cols),
+        values.reshape(full_len, kv_cols),
+        grad_attended,
+    )
+    grad_queries = grad_queries.reshape(full_len, q_heads, HEAD_DIM)
+    grad_keys = grad_keys.reshape(full_len, kv_heads, HEAD_DIM)
     grad_query_hat = unrotate(grad_queries, cosine_table, sine_table)
     grad_key_hat = unrotate(grad_keys, cosine_table, sine_table)
     heads_part = jnp.stack(
@@ -1554,6 +1593,7 @@
         and gate_weight.shape[1] % (parts * HEAD_DIM) == 0
         and tokens.shape[1] % (cores * LINE_CHUNKS * 16) == 0
         and cores == 2
+        and tokens.shape[1] * parts % BACK_BLOCK == 0
         and lax.axis_size("fsdp") == 4
     )
     return line_shards(*operands) if fits else shards(*operands)

time: 545 us -> 523 us (0.960)
  Pallas kernels: 403 us -> 387 us
  matrix products: 91.8 us -> 79.2 us
    pallas_call x4, Pallas kernels: 396 us -> 374 us  [line_call(): pl.pallas_call(functools.partial(line_body, n, chunks, len(parts), gather...]
    dot_general x4 -> x0, matrix products: 16.7 us -> none  [the longest x1 6.46 us: line_shards(): jnp.einsum('kgij,ikgd->jkd', probs_low, grad_attended, preferred_element_...]
    pallas_call x0 -> x1, Pallas kernels: none -> 5.83 us  [attend_back(): pl.pallas_call(functools.partial(attend_back_body, kv_heads, group), out_...]
  transfers between devices with their start and end apart: 5 -> 5, of which waited for: 0 -> 0; matrix products, arithmetic and copies ran while one was open for 11% -> 14% of each run, Pallas kernels for 41% -> 39%
where the time goes in v5:
time: 523 us; the launch traced here: 519 us
  Pallas kernels  387 us (74%)
  matrix products  79.2 us (15%)
  local copies, waits for them, and re-layouts  23.7 us (5%)
  other arithmetic  20.6 us (4%)
  starting transfers between devices  7.72 us (1%)
    pallas_call x4, Pallas kernels, line_call(): pl.pallas_call(functools.partial(line_body, n, chunks, len(parts), gather...  374 us
    dot_general x4, matrix products, row_product(): lax.dot_general(left, right, (((0,), (0,)), ((), ())), preferred_element_...  24 us
    dot_general x4, matrix products, column_product(): lax.dot_general(left, right, (((1,), (1,)), ((), ())), preferred_element_...  21.2 us
    dot_general x1, matrix products, line_shards(): both = jnp.dot(normed_mlp, mlp_in, preferred_element_type=jnp.float32)  11.8 us
  transfers between devices with their start and end apart: 5, of which 0 were waited for; matrix products, arithmetic and copies ran while one was open for 14% of the time, Pallas kernels for 39%

profile of v5, /device:TPU:0, one launch (start us, length us, event | category | flops | bytes accessed | tf_op | source)
XLA Modules:
  0.0 519.3 jit_solution(17688991689620075449)
XLA Ops:
  4.2 67.4 %shard_map.211 = (bf16[4,2,128,2048]{3,2,1,0:T(8,128)(2,1)}, bf16[2048,512]{1,0:T(8,128)(2,1)}, bf16[2048,256]{1,0:T(8,128)(2,1)}) custom-call(bf16[128,2048]{1,0:T(8,128)(2,1)} %get-tuple-element.105.refs_0_.refs_1_.refs_2_, f32[1,2048]{1,0:T(1,128)} %bitcast.150, bf16[128,1024]{1,0:T(8,128)(2,1)} %refs_2_.1, bf16[128,512]{1,0:T(8,128)(2,1)} %refs_3_.2, ...), custom_call_target="tpu_custom_call" | custom-call | flops 4194304 | bytes 83886080 | tf_op jit(solution)/shard_map/pallas_call | solution.py:1229
  76.1 5.2 %fusion.42 = f32[1024,512]{0,1:T(8,128)S(1)} fusion(bf16[1024,2048]{1,0:T(8,128)(2,1)} %bitcast.163, bf16[2048,512]{1,0:T(8,128)(2,1)} %get-tuple-element.47), kind=kOutput, calls=%fused_computation.108 | convolution fusion | flops 2147483648 | bytes 8388608 | tf_op jit(solution)/shard_map/dot_general | solution.py:1451
  84.3 3.1 multiply_cosine_fusion
  87.5 3.1 fusion.30
  95.4 3.0 fusion
  98.4 2.8 fusion.4
  101.3 3.4 convolution_convert_fusion.3
  105.6 129.7 %shard_map.212 = (bf16[4,2,128,2048]{3,2,1,0:T(8,128)(2,1)}, f32[128,2048]{1,0:T(8,128)}, bf16[2048,1536]{1,0:T(8,128)(2,1)}, bf16[2048,768]{1,0:T(8,128)(2,1)}) custom-call(bf16[4,2,128,2048]{3,2,1,0:T(8,128)(2,1)} %bitcast.139, bf16[128,2048]{1,0:T(8,128)(2,1)} %get-tuple-element.105.refs_0_.refs_1_.refs_2_, f32[1,2048]{1,0:T(1,128)} %bitcast.152, ...), custom_call_target="tpu_custom_call" | custom-call | flops 8388608 | bytes 167772160 | tf_op jit(solution)/shard_map/pallas_call | solution.py:1229
  238.8 11.8 %fusion.43 = f32[1024,1536]{0,1:T(8,128)} fusion(bf16[1024,2048]{1,0:T(8,128)(2,1)} %bitcast.167, bf16[2048,1536]{1,0:T(8,128)(2,1)} %get-tuple-element.51), kind=kOutput, calls=%fused_computation.109 | convolution fusion | flops 6442450944 | bytes 16777216 | tf_op jit(solution)/shard_map/dot_general | solution.py:1488
  253.3 6.9 %multiply_convert_fusion.2 = (bf16[1024,768]{0,1:T(8,128)(2,1)S(1)}, bf16[1024,768]{0,1:T(8,128)(2,1)S(1)}, bf16[1024,768]{0,1:T(8,128)(2,1)S(1)}) fusion(f32[1024,1536]{0,1:T(8,128)} %fusion.43, bf16[1024,2048]{1,0:T(8,128)(2,1)S(1)} %bitcast.142, bf16[2048,768]{1,0:T(8,128)(2,1)S(1)} %copy-done.26), kind=kOutput, calls=%fused_computation.16 | convolution fusion | flops 3233021952 | bytes 18350080 | tf_op jit(solution)/shard_map/dot_general | solution.py:1494
  260.3 8.3 %convolution_convert_fusion.1 = bf16[1024,2048]{1,0:T(8,128)(2,1)} fusion(bf16[2048,1536]{1,0:T(8,128)(2,1)S(1)} %bitcast.162, bf16[1024,768]{0,1:T(8,128)(2,1)S(1)} %get-tuple-element.81, bf16[1024,768]{0,1:T(8,128)(2,1)S(1)} %get-tuple-element.80), kind=kOutput, calls=%fused_computation.8 | convolution fusion | flops 6450839552 | bytes 13631488 | tf_op jit(solution)/shard_map/dot_general | solution.py:70
  268.7 9.6 %convolution_convert_fusion.refs_5_ = bf16[2048,1536]{1,0:T(8,128)(2,1)} fusion(bf16[1024,2048]{1,0:T(8,128)(2,1)S(1)} %bitcast.168, bf16[1024,768]{0,1:T(8,128)(2,1)S(1)} %get-tuple-element.81, bf16[1024,768]{0,1:T(8,128)(2,1)S(1)} %get-tuple-element.80), kind=kOutput, calls=%fused_computation.2 | convolution fusion | flops 6451888128 | bytes 13631488 | tf_op jit(solution)/shard_map/dot_general | solution.py:64
  278.3 4.9 convolution_convert_fusion.5.refs_6_
  283.2 5.1 convolution_convert_fusion.4
  288.3 108.7 %shard_map.213 = (bf16[4,2,128,2048]{3,2,1,0:T(8,128)(2,1)}, bf16[2,128,2048]{2,1,0:T(8,128)(2,1)}, f32[128,2048]{1,0:T(8,128)}, f32[1,2048]{1,0:T(1,128)}, bf16[4,128,2304]{2,1,0:T(8,128)(2,1)}) custom-call(bf16[4,2,128,2048]{3,2,1,0:T(8,128)(2,1)} %bitcast.144, bf16[4,2,128,2048]{3,2,1,0:T(8,128)(2,1)} %bitcast.145, ...), custom_call_target="tpu_custom_call" | custom-call | flops 8388608 | bytes 167772160 | tf_op jit(solution)/shard_map/pallas_call | solution.py:1229
  397.0 4.2 convolution_convert_fusion.8.grads
  401.3 4.5 all-to-all-start
  406.8 5.8 %attend_back.1 = (f32[1024,256]{1,0:T(8,128)S(1)}, f32[1024,128]{1,0:T(8,128)S(1)}, f32[1024,128]{1,0:T(8,128)S(1)}) custom-call(bf16[1024,256]{1,0:T(8,128)(2,1)S(1)} %copy_bitcast_fusion.queries, bf16[1024,128]{1,0:T(8,128)(2,1)S(1)} %pad_maximum_fusion.8.keys, bf16[1024,128]{1,0:T(8,128)(2,1)S(1)} %copy.74.values, bf16[1024,256]{1,0:T(8,128)(2,1)S(1)} %copy-done), custom_call_target="tpu_custom_call" | custom-call | flops 1342177280 | bytes 4194304 | tf_op jit(solution)/shard_map/attend_back/pallas_call | solution.py:1346
  414.3 2.7 fusion.23
  421.6 3.3 multiply_reduce_fusion.1
  426.8 7.1 %multiply_reduce_fusion = (f32[2048]{0:T(1024)S(1)}, bf16[2048,512]{1,0:T(8,128)(2,1)}) fusion(bf16[2048,512]{1,0:T(8,128)(2,1)} %get-tuple-element.47, bf16[1024,2048]{1,0:T(8,128)(2,1)} %bitcast.164, bf16[1024,128]{0,1:T(8,128)(2,1)S(1)} %copy.66, bf16[1024,128]{0,1:T(8,128)(2,1)} %copy.65, bf16[1024,256]{0,1:T(8,128)(2,1)S(1)} %get-tuple-element.84), kind=kOutput, calls=%fused_computation.6 | convolution fusion | flops 2155870208 | bytes 9445376 | tf_op jit(solution)/shard_map/dot_general | solution.py:64
  437.1 4.4 convolution_convert_fusion.2
  441.4 68.2 %shard_map.214 = (f32[2,128,2048]{2,1,0:T(8,128)}, bf16[128,1024]{1,0:T(8,128)(2,1)}, bf16[128,512]{1,0:T(8,128)(2,1)}, bf16[128,512]{1,0:T(8,128)(2,1)}, bf16[128,1024]{1,0:T(8,128)(2,1)}, /*index=5*/f32[8,2048]{1,0:T(8,128)}) custom-call(bf16[4,2,128,2048]{3,2,1,0:T(8,128)(2,1)} %bitcast.141, f32[128,2048]{1,0:T(8,128)} %get-tuple-element.58.refs_1_, ...), custom_call_target="tpu_custom_call" | custom-call | flops 4194304 | bytes 83886080 | tf_op jit(solution)/shard_map/pallas_call | solution.py:1229
  512.5 6.6 %widen.1 = (bf16[256,2048]{1,0:T(8,128)(2,1)}, f32[256,2048]{1,0:T(8,128)}, f32[128,1024]{1,0:T(8,128)}, f32[128,512]{1,0:T(8,128)}, f32[128,512]{1,0:T(8,128)},...) custom-call(bf16[256,2048]{1,0:T(8,128)(2,1)} %bitcast.149, ...), custom_call_target="tpu_custom_call" | custom-call | tf_op jit(solution)/shard_map/widen/pallas_call | solution.py:1377
  (126 shorter events, 37.8 us)
Async XLA Ops:
  71.6 166.0 %collective-permute-start.2 = (bf16[128,2048]{1,0:T(8,128)(2,1)}, bf16[128,2048]{1,0:T(8,128)(2,1)}, u32[]{:S(2)}, u32[]{:S(2)}) collective-permute-start(bf16[128,2048]{1,0:T(8,128)(2,1)} %get-tuple-element.45.refs_3_), channel_id=1, source_target_pairs={{0,6},{2,0},{4,2},{6,4},{1,7},{3,1},{5,3},{7,5},{8,14},{10,8},{12,... | collective-permute-start | bytes 1572872 | tf_op jit(solution)/shard_map/ppermute | solution.py:1302
  73.9 162.7 %collective-permute-start.1 = (bf16[128,2048]{1,0:T(8,128)(2,1)}, bf16[128,2048]{1,0:T(8,128)(2,1)}, u32[]{:S(2)}, u32[]{:S(2)}) collective-permute-start(bf16[128,2048]{1,0:T(8,128)(2,1)} %get-tuple-element.45.refs_3_), channel_id=1, source_target_pairs={{0,4},{2,6},{4,0},{6,2},{1,5},{3,7},{5,1},{7,3},{8,12},{10,14},{12... | collective-permute-start | bytes 1572872 | tf_op jit(solution)/shard_map/ppermute | solution.py:1302
  73.9 161.5 %collective-permute-start = (bf16[128,2048]{1,0:T(8,128)(2,1)}, bf16[128,2048]{1,0:T(8,128)(2,1)}, u32[]{:S(2)}, u32[]{:S(2)}) collective-permute-start(bf16[128,2048]{1,0:T(8,128)(2,1)} %get-tuple-element.45.refs_3_), channel_id=1, source_target_pairs={{0,2},{2,4},{4,6},{6,0},{1,3},{3,5},{5,7},{7,1},{8,10},{10,12},{12... | collective-permute-start | bytes 1572872 | tf_op jit(solution)/shard_map/ppermute | solution.py:1302
  84.0 6.9 %copy-start.1 = (f32[1024,128]{1,0:T(8,128)}, f32[1024,128]{1,0:T(8,128)S(1)}, u32[]{:S(2)}) copy-start(f32[1024,128]{1,0:T(8,128)S(1)} %copy.75) | copy-start | bytes 1572868
  84.2 6.3 %slice-start = ((f32[1024,512]{0,1:T(8,128)}), f32[1024,256]{0,1:T(8,128)S(1)}, s32[]{:S(2)}) async-start(f32[1024,512]{0,1:T(8,128)} %copy-done.8), calls=%async_computation.1 | async-start | bytes 2097152 | tf_op jit(solution)/shard_map/slice | solution.py:1452
  90.9 4.1 copy-start.3
  91.0 3.5 copy-start.10
  91.0 3.5 copy-start.12
  101.2 3.4 copy-start.14
  101.3 3.7 copy-start.23
  105.6 129.8 %copy-start.7 = (bf16[4,128,2048]{2,1,0:T(8,128)(2,1)S(1)}, bf16[4,128,2048]{2,1,0:T(8,128)(2,1)}, u32[]{:S(2)}) copy-start(bf16[4,128,2048]{2,1,0:T(8,128)(2,1)} %copy-done.6) | copy-start | bytes 6291460
  238.7 12.7 %collective-permute-start.3 = (bf16[4,128,2048]{2,1,0:T(8,128)(2,1)S(1)}, bf16[4,128,2048]{2,1,0:T(8,128)(2,1)S(1)}, u32[]{:S(2)}, u32[]{:S(2)}) collective-permute-start(bf16[4,128,2048]{2,1,0:T(8,128)(2,1)S(1)} %bitcast_dynamic-update-slice_fusion.2), channel_id=1, source_target_pairs={{0,1},{1,0},{2,3},{3,2},{4,5},{5,4},{6,7},{7,6},{8,9},{9,8},{10,11... | collective-permute-start | bytes 6291464 | tf_op jit(solution)/shard_map/ppermute | solution.py:1304
  251.4 8.8 %slice-start.1 = ((s8[6291456]{0:T(1024)(128)(4,1)}), s8[4194304]{0:T(1024)(128)(4,1)S(1)}, s32[]{:S(2)}) async-start(s8[6291456]{0:T(1024)(128)(4,1)} %bitcast.161), calls=%async_computation.2 | async-start | bytes 8388608
  253.3 7.0 %slice-start.2 = ((s8[6291456]{0:T(1024)(128)(4,1)}), s8[2097152]{0:T(1024)(128)(4,1)S(1)}, s32[]{:S(2)}) async-start(s8[6291456]{0:T(1024)(128)(4,1)} %bitcast.161), calls=%async_computation.3 | async-start | bytes 4194304
  260.3 8.3 %copy-start.25 = (bf16[4,2,128,2048]{3,2,1,0:T(8,128)(2,1)S(1)}, bf16[4,2,128,2048]{3,2,1,0:T(8,128)(2,1)}, u32[]{:S(2)}) copy-start(bf16[4,2,128,2048]{3,2,1,0:T(8,128)(2,1)} %get-tuple-element.50) | copy-start | bytes 12582916
  288.3 108.7 %copy-start.17 = (bf16[2048,256]{1,0:T(8,128)(2,1)S(1)}, bf16[2048,256]{1,0:T(8,128)(2,1)}, u32[]{:S(2)}) copy-start(bf16[2048,256]{1,0:T(8,128)(2,1)} %get-tuple-element.48) | copy-start | bytes 3145732
  401.3 111.2 %all-to-all-start = ((bf16[4,128,2304]{2,1,0:T(8,128)(2,1)}), bf16[4,128,2304]{2,1,0:T(8,128)(2,1)}, u32[]{:S(2)}, u32[]{:S(2)}) async-start(bf16[4,128,2304]{2,1,0:T(8,128)(2,1)} %get-tuple-element.61), calls=%async_computation | async-start | bytes 4718592 | tf_op jit(solution)/shard_map/all_to_all | solution.py:1515
  412.7 4.4 copy-start.2
  414.2 3.4 copy-start.5
  421.6 4.9 copy-start.9
  426.8 7.2 %copy-start.21 = (bf16[2048]{0:T(1024)(128)(2,1)S(1)}, bf16[2048]{0:T(1024)(128)(2,1)}, u32[]{:S(2)}) copy-start(bf16[2048]{0:T(1024)(128)(2,1)} %param.14) | copy-start | bytes 12292
  426.8 7.2 %copy-start.15 = (bf16[128,2,1024]{2,0,1:T(8,128)(2,1)S(1)}, bf16[128,2,1024]{2,0,1:T(8,128)(2,1)}, u32[]{:S(2)}) copy-start(bf16[128,2,1024]{2,0,1:T(8,128)(2,1)} %copy-done.14) | copy-start | bytes 1572868
  426.8 7.2 %copy-start.24 = (bf16[4,2,128,2048]{3,2,1,0:T(8,128)(2,1)S(1)}, bf16[4,2,128,2048]{3,2,1,0:T(8,128)(2,1)}, u32[]{:S(2)}) copy-start(bf16[4,2,128,2048]{3,2,1,0:T(8,128)(2,1)} %get-tuple-element.54) | copy-start | bytes 12582916
  434.0 3.1 copy-start.20
  (13 other events, 25.9 us)

commit v6 on v5

--- a/solution.py
+++ b/solution.py
@@ -1360,25 +1360,28 @@
     results[1][...] = tokens[...]
     for a in range(4):
         results[2 + a][...] = attn[a][...].astype(jnp.float32)
-    for a in range(3):
-        results[6 + a][...] = mlp[0, :, a * h_cols : (a + 1) * h_cols].astype(jnp.float32)
+    for q in range(mlp.shape[0]):
+        for a in range(3):
+            piece = mlp[q, :, a * h_cols : (a + 1) * h_cols].astype(jnp.float32)
+            results[6 + a][:, q * h_cols : (q + 1) * h_cols] = piece
 
 
 def widen(parts, h_cols, out, tokens, mlp, *attn):
     rows = mlp.shape[1]
     width = out.shape[-1]
     out, tokens = out.reshape(-1, width), tokens.reshape(-1, width)
-    token_rows = pl.BlockSpec((out.shape[0] // parts, width), lambda i: (i, 0))
-    quarters = [pl.BlockSpec((rows, a.shape[1] // parts), lambda i: (0, i)) for a in attn]
-    hidden = pl.BlockSpec((rows, h_cols), lambda i: (0, i))
+    steps = parts // 2
+    token_rows = pl.BlockSpec((out.shape[0] // steps, width), lambda i: (i, 0))
+    quarters = [pl.BlockSpec((rows, a.shape[1] // steps), lambda i: (0, i)) for a in attn]
+    hidden = pl.BlockSpec((rows, 2 * h_cols), lambda i: (0, i))
+    pieces = pl.BlockSpec((2,) + mlp.shape[1:], lambda i: (i, 0, 0))
     results = [jax.ShapeDtypeStruct(a.shape, a.dtype) for a in (out, tokens)]
     results += [jax.ShapeDtypeStruct(a.shape, jnp.float32) for a in attn]
     results += [jax.ShapeDtypeStruct((rows, h_cols * parts), jnp.float32)] * 3
     return pl.pallas_call(
         functools.partial(widen_body, h_cols),
-        grid=(parts,),
-        in_specs=[token_rows, token_rows, pl.BlockSpec((1,) + mlp.shape[1:], lambda i: (i, 0, 0))]
-        + quarters,
+        grid=(steps,),
+        in_specs=[token_rows, token_rows, pieces] + quarters,
         out_specs=tuple([token_rows, token_rows] + quarters + [hidden] * 3),
         out_shape=tuple(results),
         name="widen",
@@ -1593,6 +1596,7 @@
         and gate_weight.shape[1] % (parts * HEAD_DIM) == 0
         and tokens.shape[1] % (cores * LINE_CHUNKS * 16) == 0
         and cores == 2
+        and parts % 2 == 0
         and tokens.shape[1] * parts % BACK_BLOCK == 0
         and lax.axis_size("fsdp") == 4
     )

time: 523 us -> 522 us (level)
  no operation moved by 1% of the time
where the time goes in v6:
time: 522 us; the launch traced here: 518 us
  Pallas kernels  386 us (74%)
  matrix products  79.2 us (15%)
  local copies, waits for them, and re-layouts  23.7 us (5%)
  other arithmetic  20.6 us (4%)
  starting transfers between devices  7.72 us (1%)
    pallas_call x4, Pallas kernels, line_call(): pl.pallas_call(functools.partial(line_body, n, chunks, len(parts), gather...  374 us
    dot_general x4, matrix products, row_product(): lax.dot_general(left, right, (((0,), (0,)), ((), ())), preferred_element_...  24 us
    dot_general x4, matrix products, column_product(): lax.dot_general(left, right, (((1,), (1,)), ((), ())), preferred_element_...  21.2 us
    dot_general x1, matrix products, line_shards(): both = jnp.dot(normed_mlp, mlp_in, preferred_element_type=jnp.float32)  11.8 us
  transfers between devices with their start and end apart: 5, of which 0 were waited for; matrix products, arithmetic and copies ran while one was open for 14% of the time, Pallas kernels for 39%

profile of v6, /device:TPU:0, one launch (start us, length us, event | category | flops | bytes accessed | tf_op | source)
XLA Modules:
  0.0 518.4 jit_solution(2863211636835274806)
XLA Ops:
  4.2 67.4 %shard_map.211 = (bf16[4,2,128,2048]{3,2,1,0:T(8,128)(2,1)}, bf16[2048,512]{1,0:T(8,128)(2,1)}, bf16[2048,256]{1,0:T(8,128)(2,1)}) custom-call(bf16[128,2048]{1,0:T(8,128)(2,1)} %get-tuple-element.105.refs_0_.refs_1_.refs_2_, f32[1,2048]{1,0:T(1,128)} %bitcast.150, bf16[128,1024]{1,0:T(8,128)(2,1)} %refs_2_.1, bf16[128,512]{1,0:T(8,128)(2,1)} %refs_3_.2, ...), custom_call_target="tpu_custom_call" | custom-call | flops 4194304 | bytes 83886080 | tf_op jit(solution)/shard_map/pallas_call | solution.py:1229
  76.1 5.2 %fusion.42 = f32[1024,512]{0,1:T(8,128)S(1)} fusion(bf16[1024,2048]{1,0:T(8,128)(2,1)} %bitcast.163, bf16[2048,512]{1,0:T(8,128)(2,1)} %get-tuple-element.47), kind=kOutput, calls=%fused_computation.108 | convolution fusion | flops 2147483648 | bytes 8388608 | tf_op jit(solution)/shard_map/dot_general | solution.py:1454
  84.3 3.1 multiply_cosine_fusion
  87.5 3.1 fusion.30
  95.4 3.0 fusion
  98.4 2.8 fusion.4
  101.3 3.4 convolution_convert_fusion.3
  105.6 129.7 %shard_map.212 = (bf16[4,2,128,2048]{3,2,1,0:T(8,128)(2,1)}, f32[128,2048]{1,0:T(8,128)}, bf16[2048,1536]{1,0:T(8,128)(2,1)}, bf16[2048,768]{1,0:T(8,128)(2,1)}) custom-call(bf16[4,2,128,2048]{3,2,1,0:T(8,128)(2,1)} %bitcast.139, bf16[128,2048]{1,0:T(8,128)(2,1)} %get-tuple-element.105.refs_0_.refs_1_.refs_2_, f32[1,2048]{1,0:T(1,128)} %bitcast.152, ...), custom_call_target="tpu_custom_call" | custom-call | flops 8388608 | bytes 167772160 | tf_op jit(solution)/shard_map/pallas_call | solution.py:1229
  238.8 11.8 %fusion.43 = f32[1024,1536]{0,1:T(8,128)} fusion(bf16[1024,2048]{1,0:T(8,128)(2,1)} %bitcast.167, bf16[2048,1536]{1,0:T(8,128)(2,1)} %get-tuple-element.51), kind=kOutput, calls=%fused_computation.109 | convolution fusion | flops 6442450944 | bytes 16777216 | tf_op jit(solution)/shard_map/dot_general | solution.py:1491
  253.3 6.9 %multiply_convert_fusion.2 = (bf16[1024,768]{0,1:T(8,128)(2,1)S(1)}, bf16[1024,768]{0,1:T(8,128)(2,1)S(1)}, bf16[1024,768]{0,1:T(8,128)(2,1)S(1)}) fusion(f32[1024,1536]{0,1:T(8,128)} %fusion.43, bf16[1024,2048]{1,0:T(8,128)(2,1)S(1)} %bitcast.142, bf16[2048,768]{1,0:T(8,128)(2,1)S(1)} %copy-done.26), kind=kOutput, calls=%fused_computation.16 | convolution fusion | flops 3233021952 | bytes 18350080 | tf_op jit(solution)/shard_map/dot_general | solution.py:1497
  260.3 8.3 %convolution_convert_fusion.1 = bf16[1024,2048]{1,0:T(8,128)(2,1)} fusion(bf16[2048,1536]{1,0:T(8,128)(2,1)S(1)} %bitcast.162, bf16[1024,768]{0,1:T(8,128)(2,1)S(1)} %get-tuple-element.81, bf16[1024,768]{0,1:T(8,128)(2,1)S(1)} %get-tuple-element.80), kind=kOutput, calls=%fused_computation.8 | convolution fusion | flops 6450839552 | bytes 13631488 | tf_op jit(solution)/shard_map/dot_general | solution.py:70
  268.7 9.6 %convolution_convert_fusion.refs_5_ = bf16[2048,1536]{1,0:T(8,128)(2,1)} fusion(bf16[1024,2048]{1,0:T(8,128)(2,1)S(1)} %bitcast.168, bf16[1024,768]{0,1:T(8,128)(2,1)S(1)} %get-tuple-element.81, bf16[1024,768]{0,1:T(8,128)(2,1)S(1)} %get-tuple-element.80), kind=kOutput, calls=%fused_computation.2 | convolution fusion | flops 6451888128 | bytes 13631488 | tf_op jit(solution)/shard_map/dot_general | solution.py:64
  278.3 4.9 convolution_convert_fusion.5.refs_6_
  283.2 5.1 convolution_convert_fusion.4
  288.3 108.7 %shard_map.213 = (bf16[4,2,128,2048]{3,2,1,0:T(8,128)(2,1)}, bf16[2,128,2048]{2,1,0:T(8,128)(2,1)}, f32[128,2048]{1,0:T(8,128)}, f32[1,2048]{1,0:T(1,128)}, bf16[4,128,2304]{2,1,0:T(8,128)(2,1)}) custom-call(bf16[4,2,128,2048]{3,2,1,0:T(8,128)(2,1)} %bitcast.144, bf16[4,2,128,2048]{3,2,1,0:T(8,128)(2,1)} %bitcast.145, ...), custom_call_target="tpu_custom_call" | custom-call | flops 8388608 | bytes 167772160 | tf_op jit(solution)/shard_map/pallas_call | solution.py:1229
  397.0 4.2 convolution_convert_fusion.8.grads
  401.3 4.5 all-to-all-start
  406.8 5.8 %attend_back.1 = (f32[1024,256]{1,0:T(8,128)S(1)}, f32[1024,128]{1,0:T(8,128)S(1)}, f32[1024,128]{1,0:T(8,128)S(1)}) custom-call(bf16[1024,256]{1,0:T(8,128)(2,1)S(1)} %copy_bitcast_fusion.queries, bf16[1024,128]{1,0:T(8,128)(2,1)S(1)} %pad_maximum_fusion.8.keys, bf16[1024,128]{1,0:T(8,128)(2,1)S(1)} %copy.74.values, bf16[1024,256]{1,0:T(8,128)(2,1)S(1)} %copy-done), custom_call_target="tpu_custom_call" | custom-call | flops 1342177280 | bytes 4194304 | tf_op jit(solution)/shard_map/attend_back/pallas_call | solution.py:1346
  414.3 2.7 fusion.23
  421.6 3.3 multiply_reduce_fusion.1
  426.8 7.1 %multiply_reduce_fusion = (f32[2048]{0:T(1024)S(1)}, bf16[2048,512]{1,0:T(8,128)(2,1)}) fusion(bf16[2048,512]{1,0:T(8,128)(2,1)} %get-tuple-element.47, bf16[1024,2048]{1,0:T(8,128)(2,1)} %bitcast.164, bf16[1024,128]{0,1:T(8,128)(2,1)S(1)} %copy.66, bf16[1024,128]{0,1:T(8,128)(2,1)} %copy.65, bf16[1024,256]{0,1:T(8,128)(2,1)S(1)} %get-tuple-element.84), kind=kOutput, calls=%fused_computation.6 | convolution fusion | flops 2155870208 | bytes 9445376 | tf_op jit(solution)/shard_map/dot_general | solution.py:64
  437.1 4.4 convolution_convert_fusion.2
  441.4 68.2 %shard_map.214 = (f32[2,128,2048]{2,1,0:T(8,128)}, bf16[128,1024]{1,0:T(8,128)(2,1)}, bf16[128,512]{1,0:T(8,128)(2,1)}, bf16[128,512]{1,0:T(8,128)(2,1)}, bf16[128,1024]{1,0:T(8,128)(2,1)}, /*index=5*/f32[8,2048]{1,0:T(8,128)}) custom-call(bf16[4,2,128,2048]{3,2,1,0:T(8,128)(2,1)} %bitcast.141, f32[128,2048]{1,0:T(8,128)} %get-tuple-element.58.refs_1_, ...), custom_call_target="tpu_custom_call" | custom-call | flops 4194304 | bytes 83886080 | tf_op jit(solution)/shard_map/pallas_call | solution.py:1229
  512.5 5.7 %widen.1 = (bf16[256,2048]{1,0:T(8,128)(2,1)}, f32[256,2048]{1,0:T(8,128)}, f32[128,1024]{1,0:T(8,128)}, f32[128,512]{1,0:T(8,128)}, f32[128,512]{1,0:T(8,128)},...) custom-call(bf16[256,2048]{1,0:T(8,128)(2,1)} %bitcast.149, ...), custom_call_target="tpu_custom_call" | custom-call | tf_op jit(solution)/shard_map/widen/pallas_call | solution.py:1381
  (126 shorter events, 37.8 us)
Async XLA Ops:
  71.6 166.0 %collective-permute-start.2 = (bf16[128,2048]{1,0:T(8,128)(2,1)}, bf16[128,2048]{1,0:T(8,128)(2,1)}, u32[]{:S(2)}, u32[]{:S(2)}) collective-permute-start(bf16[128,2048]{1,0:T(8,128)(2,1)} %get-tuple-element.45.refs_3_), channel_id=1, source_target_pairs={{0,6},{2,0},{4,2},{6,4},{1,7},{3,1},{5,3},{7,5},{8,14},{10,8},{12,... | collective-permute-start | bytes 1572872 | tf_op jit(solution)/shard_map/ppermute | solution.py:1302
  73.9 162.7 %collective-permute-start.1 = (bf16[128,2048]{1,0:T(8,128)(2,1)}, bf16[128,2048]{1,0:T(8,128)(2,1)}, u32[]{:S(2)}, u32[]{:S(2)}) collective-permute-start(bf16[128,2048]{1,0:T(8,128)(2,1)} %get-tuple-element.45.refs_3_), channel_id=1, source_target_pairs={{0,4},{2,6},{4,0},{6,2},{1,5},{3,7},{5,1},{7,3},{8,12},{10,14},{12... | collective-permute-start | bytes 1572872 | tf_op jit(solution)/shard_map/ppermute | solution.py:1302
  73.9 161.5 %collective-permute-start = (bf16[128,2048]{1,0:T(8,128)(2,1)}, bf16[128,2048]{1,0:T(8,128)(2,1)}, u32[]{:S(2)}, u32[]{:S(2)}) collective-permute-start(bf16[128,2048]{1,0:T(8,128)(2,1)} %get-tuple-element.45.refs_3_), channel_id=1, source_target_pairs={{0,2},{2,4},{4,6},{6,0},{1,3},{3,5},{5,7},{7,1},{8,10},{10,12},{12... | collective-permute-start | bytes 1572872 | tf_op jit(solution)/shard_map/ppermute | solution.py:1302
  84.0 6.9 %copy-start.1 = (f32[1024,128]{1,0:T(8,128)}, f32[1024,128]{1,0:T(8,128)S(1)}, u32[]{:S(2)}) copy-start(f32[1024,128]{1,0:T(8,128)S(1)} %copy.75) | copy-start | bytes 1572868
  84.2 6.3 %slice-start = ((f32[1024,512]{0,1:T(8,128)}), f32[1024,256]{0,1:T(8,128)S(1)}, s32[]{:S(2)}) async-start(f32[1024,512]{0,1:T(8,128)} %copy-done.8), calls=%async_computation.1 | async-start | bytes 2097152 | tf_op jit(solution)/shard_map/slice | solution.py:1455
  90.9 4.1 copy-start.3
  91.0 3.5 copy-start.10
  91.0 3.5 copy-start.12
  101.2 3.4 copy-start.14
  101.3 3.7 copy-start.23
  105.6 129.8 %copy-start.7 = (bf16[4,128,2048]{2,1,0:T(8,128)(2,1)S(1)}, bf16[4,128,2048]{2,1,0:T(8,128)(2,1)}, u32[]{:S(2)}) copy-start(bf16[4,128,2048]{2,1,0:T(8,128)(2,1)} %copy-done.6) | copy-start | bytes 6291460
  238.7 12.7 %collective-permute-start.3 = (bf16[4,128,2048]{2,1,0:T(8,128)(2,1)S(1)}, bf16[4,128,2048]{2,1,0:T(8,128)(2,1)S(1)}, u32[]{:S(2)}, u32[]{:S(2)}) collective-permute-start(bf16[4,128,2048]{2,1,0:T(8,128)(2,1)S(1)} %bitcast_dynamic-update-slice_fusion.2), channel_id=1, source_target_pairs={{0,1},{1,0},{2,3},{3,2},{4,5},{5,4},{6,7},{7,6},{8,9},{9,8},{10,11... | collective-permute-start | bytes 6291464 | tf_op jit(solution)/shard_map/ppermute | solution.py:1304
  251.4 8.8 %slice-start.1 = ((s8[6291456]{0:T(1024)(128)(4,1)}), s8[4194304]{0:T(1024)(128)(4,1)S(1)}, s32[]{:S(2)}) async-start(s8[6291456]{0:T(1024)(128)(4,1)} %bitcast.161), calls=%async_computation.2 | async-start | bytes 8388608
  253.3 7.0 %slice-start.2 = ((s8[6291456]{0:T(1024)(128)(4,1)}), s8[2097152]{0:T(1024)(128)(4,1)S(1)}, s32[]{:S(2)}) async-start(s8[6291456]{0:T(1024)(128)(4,1)} %bitcast.161), calls=%async_computation.3 | async-start | bytes 4194304
  260.3 8.3 %copy-start.25 = (bf16[4,2,128,2048]{3,2,1,0:T(8,128)(2,1)S(1)}, bf16[4,2,128,2048]{3,2,1,0:T(8,128)(2,1)}, u32[]{:S(2)}) copy-start(bf16[4,2,128,2048]{3,2,1,0:T(8,128)(2,1)} %get-tuple-element.50) | copy-start | bytes 12582916
  288.3 108.7 %copy-start.17 = (bf16[2048,256]{1,0:T(8,128)(2,1)S(1)}, bf16[2048,256]{1,0:T(8,128)(2,1)}, u32[]{:S(2)}) copy-start(bf16[2048,256]{1,0:T(8,128)(2,1)} %get-tuple-element.48) | copy-start | bytes 3145732
  401.3 111.2 %all-to-all-start = ((bf16[4,128,2304]{2,1,0:T(8,128)(2,1)}), bf16[4,128,2304]{2,1,0:T(8,128)(2,1)}, u32[]{:S(2)}, u32[]{:S(2)}) async-start(bf16[4,128,2304]{2,1,0:T(8,128)(2,1)} %get-tuple-element.61), calls=%async_computation | async-start | bytes 4718592 | tf_op jit(solution)/shard_map/all_to_all | solution.py:1518
  412.7 4.4 copy-start.2
  414.2 3.4 copy-start.5
  421.6 4.9 copy-start.9
  426.8 7.2 %copy-start.21 = (bf16[2048]{0:T(1024)(128)(2,1)S(1)}, bf16[2048]{0:T(1024)(128)(2,1)}, u32[]{:S(2)}) copy-start(bf16[2048]{0:T(1024)(128)(2,1)} %param.14) | copy-start | bytes 12292
  426.8 7.2 %copy-start.15 = (bf16[128,2,1024]{2,0,1:T(8,128)(2,1)S(1)}, bf16[128,2,1024]{2,0,1:T(8,128)(2,1)}, u32[]{:S(2)}) copy-start(bf16[128,2,1024]{2,0,1:T(8,128)(2,1)} %copy-done.14) | copy-start | bytes 1572868
  426.8 7.2 %copy-start.24 = (bf16[4,2,128,2048]{3,2,1,0:T(8,128)(2,1)S(1)}, bf16[4,2,128,2048]{3,2,1,0:T(8,128)(2,1)}, u32[]{:S(2)}) copy-start(bf16[4,2,128,2048]{3,2,1,0:T(8,128)(2,1)} %get-tuple-element.54) | copy-start | bytes 12582916
  434.0 3.1 copy-start.20
  (13 other events, 25.9 us)
